TPU v7x, 128 devices: a whole 4x4x4 slice. The times are simulated.
128 devices in a mesh: cp: 4 (over x), fsdp: 32 (over z, y, core).
Axes of the slice: x: 4, y: 4, z: 4, core: 2. Of those that a mesh axis runs over, the one named last changes fastest.
Arguments:
- tokens: int32 [64, 1024], P('fsdp', 'cp')
- lengths: int32 [64], P('fsdp')
- embed_table: bfloat16 [33, 1280], replicated
- layer_vecs: float32 [9, 1280], P(None, 'fsdp')
- w_qkv: bfloat16 [1280, 3, 20, 64], P('fsdp')
- w_out: bfloat16 [1280, 1280], P('fsdp')
- w_up: bfloat16 [1280, 5120], P('fsdp')
- b_up: float32 [5120], P('fsdp')
- w_down: bfloat16 [5120, 1280], P('fsdp')
- grad_out: bfloat16 [64, 1024, 1280], P('fsdp', 'cp')
Outputs:
- output 1: bfloat16 [64, 1024, 1280], P('fsdp', 'cp')
- output 2: float32 [33, 1280], replicated
- output 3: float32 [9, 1280], P(None, 'fsdp')
- output 4: float32 [1280, 3, 20, 64], P('fsdp')
- output 5: float32 [1280, 1280], P('fsdp')
- output 6: float32 [1280, 5120], P('fsdp')
- output 7: float32 [5120], P('fsdp')
- output 8: float32 [5120, 1280], P('fsdp')
All inputs are finite; a program needn't handle non-finite values.
Results may differ from a plain program's by a relative error of at most 0.00862362.
Values are sent between devices in bfloat16 or wider.
A program may use at most 1 GiB of HBM per device.

v0:
```python
import jax
import jax.numpy as jnp
from jax import lax
from jax.sharding import PartitionSpec as P

MASK_ID = 32
LN_EPS = 1e-5
ROPE_BASE = 10000.0
TRAIN_RATIO = 0.15 * 0.8
NEG_BIG = -1e30


def layer_norm(z_in, ln_gain, ln_bias):
    row_mean = jnp.mean(z_in, axis=-1, keepdims=True)
    centered = z_in - row_mean
    row_var = jnp.mean(centered * centered, axis=-1, keepdims=True)
    return centered * lax.rsqrt(row_var + LN_EPS) * ln_gain + ln_bias


def gelu_exact(z_in):
    return jax.nn.gelu(z_in, approximate=False)


def rope_tables(positions, head_dim):
    inv_freq = 1.0 / (ROPE_BASE ** (jnp.arange(0, head_dim, 2, dtype=jnp.float32) / head_dim))
    angles = positions.astype(jnp.float32)[:, None] * inv_freq[None, :]
    return jnp.cos(angles)[:, None, :], jnp.sin(angles)[:, None, :]


def rotate(z_in, cos_t, sin_t):
    lower_half, upper_half = jnp.split(z_in, 2, axis=-1)
    return jnp.concatenate([lower_half * cos_t - upper_half * sin_t, upper_half * cos_t + lower_half * sin_t], axis=-1)


def reduce_grad(full_grad, axis_dim):
    return lax.psum(lax.psum_scatter(full_grad, 'fsdp', scatter_dimension=axis_dim, tiled=True), 'cp')


def solution(mesh):
    cp_size = mesh.shape['cp']
    send_pairs = [(dev_index, (dev_index + 1) % cp_size) for dev_index in range(cp_size)]

    def local_step(tokens, lengths, embed_table, layer_vecs, w_qkv, w_out, w_up, b_up, w_down, grad_out):
        vecs_all = lax.all_gather(layer_vecs, 'fsdp', axis=1, tiled=True)
        qkv_w = lax.all_gather(w_qkv, 'fsdp', axis=0, tiled=True)
        out_w = lax.all_gather(w_out, 'fsdp', axis=0, tiled=True)
        up_w = lax.all_gather(w_up, 'fsdp', axis=0, tiled=True)
        up_b = lax.all_gather(b_up, 'fsdp', axis=0, tiled=True)
        down_w = lax.all_gather(w_down, 'fsdp', axis=0, tiled=True)
        n_seq, seq_loc = tokens.shape
        vocab_size, model_dim = embed_table.shape
        n_heads, head_dim = qkv_w.shape[2], qkv_w.shape[3]
        cp_index = lax.axis_index('cp')
        positions = cp_index * seq_loc + jnp.arange(seq_loc)
        len_col = lengths[:, None]
        is_mask = tokens == MASK_ID
        tok_valid = positions[None, :] < len_col
        mask_count = lax.psum(jnp.sum(is_mask.astype(jnp.int32), axis=1), 'cp')
        drop_scale = (1.0 - TRAIN_RATIO) / (1.0 - mask_count.astype(jnp.float32) / lengths.astype(jnp.float32))
        keep_scale = jnp.where(is_mask | jnp.logical_not(tok_valid), 0.0, drop_scale[:, None])[:, :, None]
        one_hot = (tokens[:, :, None] == jnp.arange(vocab_size)).astype(jnp.bfloat16)
        embedded = jnp.einsum('bsv,vd->bsd', one_hot, embed_table, preferred_element_type=jnp.float32) * keep_scale
        norm_in32, ln1_pull = jax.vjp(layer_norm, embedded, vecs_all[0], vecs_all[1])
        norm_in = norm_in32.astype(jnp.bfloat16)
        qkv_lin = jnp.einsum('bsd,dthe->bsthe', norm_in, qkv_w, preferred_element_type=jnp.float32) + vecs_all[2:5].reshape(3, n_heads, head_dim)
        cos_t, sin_t = rope_tables(positions, head_dim)
        q_rot = rotate(qkv_lin[:, :, 0] * head_dim ** -0.5, cos_t, sin_t).astype(jnp.bfloat16)
        k_rot = rotate(qkv_lin[:, :, 1], cos_t, sin_t).astype(jnp.bfloat16)
        v_val = qkv_lin[:, :, 2].astype(jnp.bfloat16)

        def block_scores(k_blk, step):
            src_index = (cp_index - step) % cp_size
            key_pos = src_index * seq_loc + jnp.arange(seq_loc)
            key_ok = key_pos[None, :] < len_col
            raw_scores = jnp.einsum('bqhd,bkhd->bhqk', q_rot, k_blk, preferred_element_type=jnp.float32)
            return jnp.where(key_ok[:, None, None, :], raw_scores, NEG_BIG)

        def fwd_block(step, k_blk, v_blk, run_max, run_sum, acc_out):
            scores = block_scores(k_blk, step)
            new_max = jnp.maximum(run_max, jnp.max(scores, axis=-1))
            weights = jnp.exp(scores - new_max[..., None])
            rescale = jnp.exp(run_max - new_max)
            run_sum = run_sum * rescale + jnp.sum(weights, axis=-1)
            acc_out = acc_out * jnp.swapaxes(rescale, 1, 2)[..., None] + jnp.einsum('bhqk,bkhd->bqhd', weights.astype(jnp.bfloat16), v_blk, preferred_element_type=jnp.float32)
            return new_max, run_sum, acc_out

        def fwd_body(step, carry):
            k_blk, v_blk, run_max, run_sum, acc_out = carry
            run_max, run_sum, acc_out = fwd_block(step, k_blk, v_blk, run_max, run_sum, acc_out)
            return (lax.ppermute(k_blk, 'cp', send_pairs), lax.ppermute(v_blk, 'cp', send_pairs), run_max, run_sum, acc_out)

        stat_shape = (n_seq, n_heads, seq_loc)
        carry = (k_rot, v_val, jnp.full(stat_shape, NEG_BIG, jnp.float32), jnp.zeros(stat_shape, jnp.float32), jnp.zeros(q_rot.shape, jnp.float32))
        carry = lax.fori_loop(0, cp_size - 1, fwd_body, carry)
        run_max, run_sum, acc_out = fwd_block(cp_size - 1, carry[0], carry[1], carry[2], carry[3], carry[4])
        log_sum = run_max + jnp.log(run_sum)
        attn32 = acc_out / jnp.swapaxes(run_sum, 1, 2)[..., None]
        attn_out = attn32.astype(jnp.bfloat16).reshape(n_seq, seq_loc, model_dim)
        resid_mid = embedded + jnp.einsum('bsd,de->bse', attn_out, out_w, preferred_element_type=jnp.float32) + vecs_all[5]
        norm_mid32, ln2_pull = jax.vjp(layer_norm, resid_mid, vecs_all[6], vecs_all[7])
        norm_mid = norm_mid32.astype(jnp.bfloat16)
        up_lin = jnp.einsum('bsd,df->bsf', norm_mid, up_w, preferred_element_type=jnp.float32) + up_b
        gelu32, gelu_pull = jax.vjp(gelu_exact, up_lin)
        gelu_out = gelu32.astype(jnp.bfloat16)
        layer_out = (resid_mid + jnp.einsum('bsf,fd->bsd', gelu_out, down_w, preferred_element_type=jnp.float32) + vecs_all[8]).astype(jnp.bfloat16)

        grad32 = grad_out.astype(jnp.float32)
        d_down = jnp.einsum('bsf,bsd->fd', gelu_out, grad_out, preferred_element_type=jnp.float32)
        d_gelu = jnp.einsum('bsd,fd->bsf', grad_out, down_w, preferred_element_type=jnp.float32)
        d_up_lin = gelu_pull(d_gelu)[0]
        d_up_b = d_up_lin.astype(jnp.bfloat16)
        d_up = jnp.einsum('bsd,bsf->df', norm_mid, d_up_b, preferred_element_type=jnp.float32)
        d_norm_mid = jnp.einsum('bsf,df->bsd', d_up_b, up_w, preferred_element_type=jnp.float32)
        d_resid_ln, d_gain2, d_bias2 = ln2_pull(d_norm_mid)
        d_resid = grad32 + d_resid_ln
        d_resid_b = d_resid.astype(jnp.bfloat16)
        d_outw = jnp.einsum('bsd,bse->de', attn_out, d_resid_b, preferred_element_type=jnp.float32)
        d_attn = jnp.einsum('bse,de->bsd', d_resid_b, out_w, preferred_element_type=jnp.float32).reshape(n_seq, seq_loc, n_heads, head_dim)
        d_attn_b = d_attn.astype(jnp.bfloat16)
        delta = jnp.swapaxes(jnp.sum(d_attn * attn32, axis=-1), 1, 2)

        def bwd_block(step, k_blk, v_blk, d_query):
            scores = block_scores(k_blk, step)
            weights = jnp.exp(scores - log_sum[..., None])
            d_weights = jnp.einsum('bqhd,bkhd->bhqk', d_attn_b, v_blk, preferred_element_type=jnp.float32)
            d_scores = (weights * (d_weights - delta[..., None])).astype(jnp.bfloat16)
            d_query = d_query + jnp.einsum('bhqk,bkhd->bqhd', d_scores, k_blk, preferred_element_type=jnp.float32)
            d_key = jnp.einsum('bhqk,bqhd->bkhd', d_scores, q_rot, preferred_element_type=jnp.float32)
            d_value = jnp.einsum('bhqk,bqhd->bkhd', weights.astype(jnp.bfloat16), d_attn_b, preferred_element_type=jnp.float32)
            return d_query, d_key, d_value

        def bwd_body(step, carry):
            k_blk, v_blk, dk_blk, dv_blk, d_query = carry
            d_query, d_key, d_value = bwd_block(step, k_blk, v_blk, d_query)
            return (lax.ppermute(k_blk, 'cp', send_pairs), lax.ppermute(v_blk, 'cp', send_pairs), lax.ppermute(dk_blk + d_key, 'cp', send_pairs), lax.ppermute(dv_blk + d_value, 'cp', send_pairs), d_query)

        kv_zero = jnp.zeros(q_rot.shape, jnp.float32)
        carry = (k_rot, v_val, kv_zero, kv_zero, kv_zero)
        carry = lax.fori_loop(0, cp_size - 1, bwd_body, carry)
        d_query, d_key, d_value = bwd_block(cp_size - 1, carry[0], carry[1], carry[4])
        d_key = lax.ppermute(carry[2] + d_key, 'cp', send_pairs)
        d_value = lax.ppermute(carry[3] + d_value, 'cp', send_pairs)

        d_q_lin = rotate(d_query, cos_t, -sin_t) * head_dim ** -0.5
        d_k_lin = rotate(d_key, cos_t, -sin_t)
        d_qkv_lin = jnp.stack([d_q_lin, d_k_lin, d_value], axis=2)
        d_qkv_b = d_qkv_lin.astype(jnp.bfloat16)
        d_qkvw = jnp.einsum('bsd,bsthe->dthe', norm_in, d_qkv_b, preferred_element_type=jnp.float32)
        d_norm_in = jnp.einsum('bsthe,dthe->bsd', d_qkv_b, qkv_w, preferred_element_type=jnp.float32)
        d_embedded, d_gain1, d_bias1 = ln1_pull(d_norm_in)
        d_embedded = d_embedded + d_resid
        d_table = jnp.einsum('bsv,bsd->vd', one_hot, (d_embedded * keep_scale).astype(jnp.bfloat16), preferred_element_type=jnp.float32)
        d_bqkv = jnp.sum(d_qkv_lin, axis=(0, 1)).reshape(3, model_dim)
        d_tail = jnp.stack([jnp.sum(d_resid, axis=(0, 1)), d_gain2, d_bias2, jnp.sum(grad32, axis=(0, 1))])
        d_vecs_full = jnp.concatenate([jnp.stack([d_gain1, d_bias1]), d_bqkv, d_tail], axis=0)
        return (layer_out, lax.psum(d_table, ('cp', 'fsdp')), reduce_grad(d_vecs_full, 1), reduce_grad(d_qkvw, 0), reduce_grad(d_outw, 0), reduce_grad(d_up, 0), reduce_grad(jnp.sum(d_up_lin, axis=(0, 1)), 0), reduce_grad(d_down, 0))

    in_specs = (P('fsdp', 'cp'), P('fsdp'), P(), P(None, 'fsdp'), P('fsdp', None, None, None), P('fsdp', None), P('fsdp', None), P('fsdp'), P('fsdp', None), P('fsdp', 'cp', None))
    out_specs = (P('fsdp', 'cp', None), P(), P(None, 'fsdp'), P('fsdp', None, None, None), P('fsdp', None), P('fsdp', None), P('fsdp'), P('fsdp', None))
    return jax.shard_map(local_step, mesh=mesh, in_specs=in_specs, out_specs=out_specs, check_vma=False)
```

profile of v0, /device:TPU:1, one launch (start us, length us, event | category | flops | bytes accessed | tf_op | source)
XLA Modules:
  0.0 2030.3 jit_solution(1520716815646475697)
XLA Ops:
  10.1 27.6 %all-gather = f32[32,40,9]{1,2,0:T(8,128)S(1)} all-gather(f32[1,40,9]{1,2,0:T(8,128)} %bitcast.212), channel_id=1, replica_groups=mesh['cp'=4,'fsdp'=32] {'fsdp'}, dimensions={0}, use_global_device_ids=true | all-gather | bytes 47520 | tf_op jit(solution)/shard_map/all_gather | solution.py:44
  38.8 6.9 psum.56
  49.6 121.9 %all-reduce = f32[5120]{0:T(1024)S(1)} all-reduce(f32[5120]{0:T(1024)S(1)} %dynamic-update-slice), channel_id=1, replica_groups=mesh['cp'=4,'fsdp'=32] {'fsdp'}, use_global_device_ids=true, to_apply=%add | all-reduce | flops 5120 | bytes 40960
  174.5 13.2 broadcast_add_fusion
  201.3 166.9 %while.48 = (s32[]{:T(128)}, bf16[2,256,20,64]{1,3,2,0:T(8,128)(2,1)}, bf16[2,256,20,64]{1,3,2,0:T(8,128)(2,1)}, f32[2,20,256]{2,1,0:T(8,128)S(1)}, f32[2,20,256...) while((s32[]{:T(128)}, ...), condition=%wide.region_7.8_spmd.clone, body=%wide.region_4.7_spmd.clone.sunk | while | flops 694088448 | bytes 98963856 | solution.py:94
  211.9 8.1 bitcast_add_fusion.12
  220.0 8.9 collective-permute-done
  228.9 28.1 %collective-permute-done.1 = bf16[2,256,20,64]{1,3,2,0:T(8,128)(2,1)} collective-permute-done((bf16[2,256,20,64]{1,3,2,0:T(8,128)(2,1)}, bf16[2,256,20,64]{1,3,2,0:T(8,128)(2,1)}, u32[]{:S(2)}, u32[]{:S(2)}) %collective-permute-start.1) | collective-permute-done | bytes 1310752 | tf_op jit(solution)/shard_map/while/body/eval_jaxpr/ppermute | solution.py:90
  267.0 8.9 bitcast_add_fusion.12
  275.8 8.5 collective-permute-done
  284.3 28.1 %collective-permute-done.1 = bf16[2,256,20,64]{1,3,2,0:T(8,128)(2,1)} collective-permute-done((bf16[2,256,20,64]{1,3,2,0:T(8,128)(2,1)}, bf16[2,256,20,64]{1,3,2,0:T(8,128)(2,1)}, u32[]{:S(2)}, u32[]{:S(2)}) %collective-permute-start.1) | collective-permute-done | bytes 1310752 | tf_op jit(solution)/shard_map/while/body/eval_jaxpr/ppermute | solution.py:90
  322.4 8.9 bitcast_add_fusion.12
  331.3 8.5 collective-permute-done
  339.7 28.1 %collective-permute-done.1 = bf16[2,256,20,64]{1,3,2,0:T(8,128)(2,1)} collective-permute-done((bf16[2,256,20,64]{1,3,2,0:T(8,128)(2,1)}, bf16[2,256,20,64]{1,3,2,0:T(8,128)(2,1)}, u32[]{:S(2)}, u32[]{:S(2)}) %collective-permute-start.1) | collective-permute-done | bytes 1310752 | tf_op jit(solution)/shard_map/while/body/eval_jaxpr/ppermute | solution.py:90
  386.7 17.1 fusion.79
  403.9 26.9 %multiply_convert_fusion.2 = (bf16[2,256,5120]{2,1,0:T(8,128)(2,1)}, f32[2,256,5120]{2,1,0:T(8,128)}) fusion(f32[2,256,5120]{2,1,0:T(8,128)} %get-tuple-element.710, f32[5120]{0:T(1024)S(1)} %all-reduce, u8[256,5120]{1,0:T(8,128)(4,1)S(1)} %get-tuple-element.604, u8[256,5120]{1,0:T(8,128)(4,1)S(1)} %get-tuple-element.603), kind=kLoop, calls=%fused_computation.56 | loop fusion | flops 186122240 | bytes 28856320 | tf_op jit(solution)/shard_map/convert_element_type | solution.py:104
  430.7 22.9 %fusion.113 = (f32[5120]{0:T(1024)}, bf16[2,256,5120]{2,1,0:T(8,128)(2,1)}) fusion(f32[2,256,5120]{2,1,0:T(8,128)} %get-tuple-element.675, bf16[2,256,1280]{2,1,0:T(8,128)(2,1)S(1)} %copy-done.18, bf16[5120,1280]{1,0:T(8,128)(2,1)} %all-gather.12.cloned.1.call-done, f32[2,256,5120]{2,1,0:T(8,128)} %get-tuple-element.710, f32[5120]{0:T(1024)S(1)} %all-reduce), kind=kOutput, calls=%fused_computation.193 | convolution fusion | flops 6752824320 | bytes 40673280 | tf_op jit(solution)/shard_map/bsd,fd->bsf/dot_general | solution.py:109
  453.7 15.7 multiply_reduce_fusion
  484.1 541.5 %while.49 = (s32[]{:T(128)}, bf16[2,256,20,64]{1,3,2,0:T(8,128)(2,1)}, bf16[2,256,20,64]{1,3,2,0:T(8,128)(2,1)}, f32[2,256,20,64]{1,3,2,0:T(8,128)}, f32[2,256,2...) while((s32[]{:T(128)}, ...), condition=%wide.region_16.17_spmd.clone, body=%wide.region_15.16_spmd.clone.sunk | while | flops 1701315328 | bytes 135131152 | solution.py:139
  495.2 6.1 bitcast_add_fusion.13
  501.3 6.0 bitcast_add_fusion.14
  516.5 121.0 %collective-permute-done.2 = bf16[2,256,20,64]{1,3,2,0:T(8,128)(2,1)} collective-permute-done((bf16[2,256,20,64]{1,3,2,0:T(8,128)(2,1)S(1)}, bf16[2,256,20,64]{1,3,2,0:T(8,128)(2,1)}, u32[]{:S(2)}, u32[]{:S(2)}) %collective-permute-start.2) | collective-permute-done | bytes 1310752 | tf_op jit(solution)/shard_map/while/body/eval_jaxpr/ppermute | solution.py:135
  637.5 28.1 %collective-permute-done.3 = bf16[2,256,20,64]{1,3,2,0:T(8,128)(2,1)} collective-permute-done((bf16[2,256,20,64]{1,3,2,0:T(8,128)(2,1)}, bf16[2,256,20,64]{1,3,2,0:T(8,128)(2,1)}, u32[]{:S(2)}, u32[]{:S(2)}) %collective-permute-start.3) | collective-permute-done | bytes 1310752 | tf_op jit(solution)/shard_map/while/body/eval_jaxpr/ppermute | solution.py:135
  676.3 6.1 bitcast_add_fusion.13
  682.4 6.0 bitcast_add_fusion.14
  692.0 6.5 bitcast_add_fusion.15
  698.5 119.4 %collective-permute-done.2 = bf16[2,256,20,64]{1,3,2,0:T(8,128)(2,1)} collective-permute-done((bf16[2,256,20,64]{1,3,2,0:T(8,128)(2,1)S(1)}, bf16[2,256,20,64]{1,3,2,0:T(8,128)(2,1)}, u32[]{:S(2)}, u32[]{:S(2)}) %collective-permute-start.2) | collective-permute-done | bytes 1310752 | tf_op jit(solution)/shard_map/while/body/eval_jaxpr/ppermute | solution.py:135
  817.9 28.1 %collective-permute-done.3 = bf16[2,256,20,64]{1,3,2,0:T(8,128)(2,1)} collective-permute-done((bf16[2,256,20,64]{1,3,2,0:T(8,128)(2,1)}, bf16[2,256,20,64]{1,3,2,0:T(8,128)(2,1)}, u32[]{:S(2)}, u32[]{:S(2)}) %collective-permute-start.3) | collective-permute-done | bytes 1310752 | tf_op jit(solution)/shard_map/while/body/eval_jaxpr/ppermute | solution.py:135
  856.7 6.1 bitcast_add_fusion.13
  862.8 6.0 bitcast_add_fusion.14
  872.4 6.5 bitcast_add_fusion.15
  878.8 118.7 %collective-permute-done.2 = bf16[2,256,20,64]{1,3,2,0:T(8,128)(2,1)} collective-permute-done((bf16[2,256,20,64]{1,3,2,0:T(8,128)(2,1)S(1)}, bf16[2,256,20,64]{1,3,2,0:T(8,128)(2,1)}, u32[]{:S(2)}, u32[]{:S(2)}) %collective-permute-start.2) | collective-permute-done | bytes 1310752 | tf_op jit(solution)/shard_map/while/body/eval_jaxpr/ppermute | solution.py:135
  997.5 28.1 %collective-permute-done.3 = bf16[2,256,20,64]{1,3,2,0:T(8,128)(2,1)} collective-permute-done((bf16[2,256,20,64]{1,3,2,0:T(8,128)(2,1)}, bf16[2,256,20,64]{1,3,2,0:T(8,128)(2,1)}, u32[]{:S(2)}, u32[]{:S(2)}) %collective-permute-start.3) | collective-permute-done | bytes 1310752 | tf_op jit(solution)/shard_map/while/body/eval_jaxpr/ppermute | solution.py:135
  1034.4 6.8 bitcast_add_fusion.5
  1055.8 35.2 %collective-permute-done.6 = f32[2,256,20,64]{1,3,2,0:T(8,128)} collective-permute-done((f32[2,256,20,64]{1,3,2,0:T(8,128)}, f32[2,256,20,64]{1,3,2,0:T(8,128)}, u32[]{:S(2)}, u32[]{:S(2)}) %collective-permute-start.6) | collective-permute-done | bytes 2621472 | tf_op jit(solution)/shard_map/ppermute | solution.py:141
  1094.0 53.2 %collective-permute-done.7 = f32[2,256,20,64]{1,3,2,0:T(8,128)} collective-permute-done((f32[2,256,20,64]{1,3,2,0:T(8,128)}, f32[2,256,20,64]{1,3,2,0:T(8,128)}, u32[]{:S(2)}, u32[]{:S(2)}) %collective-permute-start.7) | collective-permute-done | bytes 2621472 | tf_op jit(solution)/shard_map/ppermute | solution.py:142
  1147.2 18.2 convolution_bitcast_fusion
  1166.1 14.9 convolution_bitcast_fusion.2
  1182.3 16.2 convolution_bitcast_fusion.1
  1203.0 18.7 fusion.106
  1231.7 160.2 %reduce-scatter.6.cloned.1.call-done = f32[40,3,20,64]{3,0,2,1:T(8,128)} async-done(((f32[1280,3,20,64]{3,0,2,1:T(8,128)}), f32[40,3,20,64]{3,0,2,1:T(8,128)}) %reduce-scatter.6.cloned.1.call-update) | async-done | bytes 614416 | tf_op jit(solution)/shard_map/reduce_scatter | solution.py:36
  1391.9 146.2 %reduce-scatter.10.cloned.1.call-done = f32[40,5120]{1,0:T(8,128)} async-done(((f32[1280,5120]{1,0:T(8,128)}), f32[40,5120]{1,0:T(8,128)}) %reduce-scatter.10.cloned.1.call-update) | async-done | bytes 819216 | tf_op jit(solution)/shard_map/reduce_scatter | solution.py:36
  1538.2 146.3 %reduce-scatter.12.cloned.1.call-done = f32[160,1280]{1,0:T(8,128)} async-done(((f32[5120,1280]{1,0:T(8,128)}), f32[160,1280]{1,0:T(8,128)}) %reduce-scatter.12.cloned.1.call-update) | async-done | bytes 819216 | tf_op jit(solution)/shard_map/reduce_scatter | solution.py:36
  1685.6 14.2 fusion.69
  1699.8 91.1 %all-reduce.12.cloned.1.call-done = (f32[9,1280]{1,0:T(8,128)}, f32[5120]{0:T(1024)}) async-done(((f32[9,1280]{1,0:T(8,128)}, f32[5120]{0:T(1024)}), (f32[9,1280]{1,0:T(8,128)}, f32[5120]{0:T(1024)})) %all-reduce.12.cloned.1.call-update) | async-done | bytes 66576
  1792.5 9.2 all-reduce.4
  1801.6 140.2 %all-reduce.10.cloned.1.call-done = f32[33,1280]{1,0:T(8,128)} async-done(((f32[33,1280]{1,0:T(8,128)}), f32[33,1280]{1,0:T(8,128)}) %all-reduce.10.cloned.1.call-update) | async-done | bytes 168976 | tf_op jit(solution)/shard_map/psum | solution.py:156
  1941.8 74.9 %all-reduce.14.cloned.1.call-done = (f32[40,3,20,64]{3,0,2,1:T(8,128)}, f32[40,1280]{1,0:T(8,128)}, f32[40,5120]{1,0:T(8,128)}, f32[160,1280]{1,0:T(8,128)}) async-done(((f32[40,3,20,64]{3,0,2,1:T(8,128)}, f32[40,1280]{1,0:T(8,128)}, f32[40,5120]{1,0:T(8,128)}, f32[160,1280]{1,0:T(8,128)}), (f32[40,3,20,64]{3,0,2,1:T(8,128)}, f32[40,1280]{1,0:T(8,128)}, f32[40,5120]{1,0:T(8,128)}, ...) | async-done | bytes 2457616 | tf_op jit(solution)/shard_map/psum | solution.py:36
  (322 shorter events, 185.6 us)
Async XLA Ops:
  7.2 167.3 %all-gather.6.cloned.1.call-start = ((), (), s32[]{:S(2)}) async-start(), calls=%async_computation.4 | async-start | bytes 20275200 | tf_op jit(solution)/shard_map/all_gather | solution.py:45
  8.0 371.4 %all-gather.8.cloned.1.call-start = ((), (), s32[]{:S(2)}) async-start(), calls=%async_computation.5 | async-start | bytes 3379200 | tf_op jit(solution)/shard_map/all_gather | solution.py:46
  8.7 378.0 %all-gather.10.cloned.1.call-start = ((), (), s32[]{:S(2)}) async-start(), calls=%async_computation.6 | async-start | bytes 13516800 | tf_op jit(solution)/shard_map/all_gather | solution.py:47
  9.4 421.3 %all-gather.12.cloned.1.call-start = ((), (), s32[]{:S(2)}) async-start(), calls=%async_computation.7 | async-start | bytes 13516800 | tf_op jit(solution)/shard_map/all_gather | solution.py:49
  10.0 1221.7 %reduce-scatter.8.cloned.1.call-start = ((), (), s32[]{:S(2)}) async-start(), calls=%async_computation.10 | async-start | bytes 6758400 | tf_op jit(solution)/shard_map/reduce_scatter | solution.py:36
  38.5 136.0 %copy-start.34 = (f32[1280]{0:T(1024)}, f32[1280]{0:T(1024)S(1)}, u32[]{:S(2)}) copy-start(f32[1280]{0:T(1024)S(1)} %get-tuple-element.619) | copy-start | bytes 15364
  38.5 136.0 %copy-start.59 = (f32[1280]{0:T(1024)}, f32[1280]{0:T(1024)S(1)}, u32[]{:S(2)}) copy-start(f32[1280]{0:T(1024)S(1)} %get-tuple-element.618) | copy-start | bytes 15364
  38.5 348.2 %copy-start.57 = (f32[1280]{0:T(1024)}, f32[1280]{0:T(1024)S(1)}, u32[]{:S(2)}) copy-start(f32[1280]{0:T(1024)S(1)} %get-tuple-element.615) | copy-start | bytes 15364
  38.5 430.9 %copy-start.42 = (f32[1280]{0:T(1024)}, f32[1280]{0:T(1024)S(1)}, u32[]{:S(2)}) copy-start(f32[1280]{0:T(1024)S(1)} %get-tuple-element.616) | copy-start | bytes 15364
  47.8 139.9 %copy-start.40 = (f32[2,256]{1,0:T(2,128)}, f32[2,256]{1,0:T(2,128)S(1)}, u32[]{:S(2)}) copy-start(f32[2,256]{1,0:T(2,128)S(1)} %broadcast_multiply_fusion.1) | copy-start | bytes 6148
  48.0 326.1 %copy-start.36 = (pred[2,256]{1,0:T(4,128)(4,1)}, pred[2,256]{1,0:T(4,128)(4,1)S(1)}, u32[]{:S(2)}) copy-start(pred[2,256]{1,0:T(4,128)(4,1)S(1)} %broadcast_compare_fusion.2) | copy-start | bytes 1540
  191.6 176.6 %copy-start.12 = (bf16[2,256,20,32]{1,3,2,0:T(8,128)(2,1)}, bf16[2,256,20,32]{1,3,2,0:T(8,128)(2,1)S(1)}, u32[]{:S(2)}) copy-start(bf16[2,256,20,32]{1,3,2,0:T(8,128)(2,1)S(1)} %get-tuple-element.687) | copy-start | bytes 1966084
  202.8 26.1 %collective-permute-start = (bf16[2,256,20,64]{1,3,2,0:T(8,128)(2,1)S(1)}, bf16[2,256,20,64]{1,3,2,0:T(8,128)(2,1)}, u32[]{:S(2)}, u32[]{:S(2)}) collective-permute-start(bf16[2,256,20,64]{1,3,2,0:T(8,128)(2,1)S(1)} %copy.96), channel_id=1, source_target_pairs={{0,32},{32,64},{64,96},{96,0},{1,33},{33,65},{65,97},{97,1},{2,34}... | collective-permute-start | bytes 3932168 | tf_op jit(solution)/shard_map/while/body/eval_jaxpr/ppermute | solution.py:90
  205.7 51.3 %collective-permute-start.1 = (bf16[2,256,20,64]{1,3,2,0:T(8,128)(2,1)}, bf16[2,256,20,64]{1,3,2,0:T(8,128)(2,1)}, u32[]{:S(2)}, u32[]{:S(2)}) collective-permute-start(bf16[2,256,20,64]{1,3,2,0:T(8,128)(2,1)} %copy.97), channel_id=1, source_target_pairs={{0,32},{32,64},{64,96},{96,0},{1,33},{33,65},{65,97},{97,1},{2,34}... | collective-permute-start | bytes 3932168 | tf_op jit(solution)/shard_map/while/body/eval_jaxpr/ppermute | solution.py:90
  258.3 26.0 %collective-permute-start = (bf16[2,256,20,64]{1,3,2,0:T(8,128)(2,1)S(1)}, bf16[2,256,20,64]{1,3,2,0:T(8,128)(2,1)}, u32[]{:S(2)}, u32[]{:S(2)}) collective-permute-start(bf16[2,256,20,64]{1,3,2,0:T(8,128)(2,1)S(1)} %copy.96), channel_id=1, source_target_pairs={{0,32},{32,64},{64,96},{96,0},{1,33},{33,65},{65,97},{97,1},{2,34}... | collective-permute-start | bytes 3932168 | tf_op jit(solution)/shard_map/while/body/eval_jaxpr/ppermute | solution.py:90
  260.8 51.6 %collective-permute-start.1 = (bf16[2,256,20,64]{1,3,2,0:T(8,128)(2,1)}, bf16[2,256,20,64]{1,3,2,0:T(8,128)(2,1)}, u32[]{:S(2)}, u32[]{:S(2)}) collective-permute-start(bf16[2,256,20,64]{1,3,2,0:T(8,128)(2,1)} %copy.97), channel_id=1, source_target_pairs={{0,32},{32,64},{64,96},{96,0},{1,33},{33,65},{65,97},{97,1},{2,34}... | collective-permute-start | bytes 3932168 | tf_op jit(solution)/shard_map/while/body/eval_jaxpr/ppermute | solution.py:90
  313.7 26.0 %collective-permute-start = (bf16[2,256,20,64]{1,3,2,0:T(8,128)(2,1)S(1)}, bf16[2,256,20,64]{1,3,2,0:T(8,128)(2,1)}, u32[]{:S(2)}, u32[]{:S(2)}) collective-permute-start(bf16[2,256,20,64]{1,3,2,0:T(8,128)(2,1)S(1)} %copy.96), channel_id=1, source_target_pairs={{0,32},{32,64},{64,96},{96,0},{1,33},{33,65},{65,97},{97,1},{2,34}... | collective-permute-start | bytes 3932168 | tf_op jit(solution)/shard_map/while/body/eval_jaxpr/ppermute | solution.py:90
  316.2 51.6 %collective-permute-start.1 = (bf16[2,256,20,64]{1,3,2,0:T(8,128)(2,1)}, bf16[2,256,20,64]{1,3,2,0:T(8,128)(2,1)}, u32[]{:S(2)}, u32[]{:S(2)}) collective-permute-start(bf16[2,256,20,64]{1,3,2,0:T(8,128)(2,1)} %copy.97), channel_id=1, source_target_pairs={{0,32},{32,64},{64,96},{96,0},{1,33},{33,65},{65,97},{97,1},{2,34}... | collective-permute-start | bytes 3932168 | tf_op jit(solution)/shard_map/while/body/eval_jaxpr/ppermute | solution.py:90
  384.8 84.7 %copy-start.54 = (f32[2,256]{1,0:T(2,128)}, f32[2,256]{1,0:T(2,128)S(1)}, u32[]{:S(2)}) copy-start(f32[2,256]{1,0:T(2,128)S(1)} %broadcast_multiply_fusion) | copy-start | bytes 6148
  386.7 82.8 %copy-start.63 = (f32[2,256]{1,0:T(2,128)}, f32[2,256]{1,0:T(2,128)S(1)}, u32[]{:S(2)}) copy-start(f32[2,256]{1,0:T(2,128)S(1)} %fusion.97) | copy-start | bytes 6148
  484.1 541.5 %copy-start.13 = (bf16[2,256,20,32]{1,3,2,0:T(8,128)(2,1)S(1)}, bf16[2,256,20,32]{1,3,2,0:T(8,128)(2,1)}, u32[]{:S(2)}) copy-start(bf16[2,256,20,32]{1,3,2,0:T(8,128)(2,1)} %copy-done.12) | copy-start | bytes 1966084
  501.3 164.3 %collective-permute-start.4 = (f32[2,256,20,64]{1,3,2,0:T(8,128)}, f32[2,256,20,64]{1,3,2,0:T(8,128)}, u32[]{:S(2)}, u32[]{:S(2)}) collective-permute-start(f32[2,256,20,64]{1,3,2,0:T(8,128)} %bitcast_add_fusion.13), channel_id=1, source_target_pairs={{0,32},{32,64},{64,96},{96,0},{1,33},{33,65},{65,97},{97,1},{2,34}... | collective-permute-start | bytes 7864328 | tf_op jit(solution)/shard_map/while/body/eval_jaxpr/ppermute | solution.py:135
  507.3 158.3 %collective-permute-start.5 = (f32[2,256,20,64]{1,3,2,0:T(8,128)}, f32[2,256,20,64]{1,3,2,0:T(8,128)}, u32[]{:S(2)}, u32[]{:S(2)}) collective-permute-start(f32[2,256,20,64]{1,3,2,0:T(8,128)} %bitcast_add_fusion.14), channel_id=1, source_target_pairs={{0,32},{32,64},{64,96},{96,0},{1,33},{33,65},{65,97},{97,1},{2,34}... | collective-permute-start | bytes 7864328 | tf_op jit(solution)/shard_map/while/body/eval_jaxpr/ppermute | solution.py:135
  507.3 130.2 %collective-permute-start.2 = (bf16[2,256,20,64]{1,3,2,0:T(8,128)(2,1)S(1)}, bf16[2,256,20,64]{1,3,2,0:T(8,128)(2,1)}, u32[]{:S(2)}, u32[]{:S(2)}) collective-permute-start(bf16[2,256,20,64]{1,3,2,0:T(8,128)(2,1)S(1)} %copy.115), channel_id=1, source_target_pairs={{0,32},{32,64},{64,96},{96,0},{1,33},{33,65},{65,97},{97,1},{2,34}... | collective-permute-start | bytes 3932168 | tf_op jit(solution)/shard_map/while/body/eval_jaxpr/ppermute | solution.py:135
  507.8 157.8 %collective-permute-start.3 = (bf16[2,256,20,64]{1,3,2,0:T(8,128)(2,1)}, bf16[2,256,20,64]{1,3,2,0:T(8,128)(2,1)}, u32[]{:S(2)}, u32[]{:S(2)}) collective-permute-start(bf16[2,256,20,64]{1,3,2,0:T(8,128)(2,1)} %copy.116), channel_id=1, source_target_pairs={{0,32},{32,64},{64,96},{96,0},{1,33},{33,65},{65,97},{97,1},{2,34}... | collective-permute-start | bytes 3932168 | tf_op jit(solution)/shard_map/while/body/eval_jaxpr/ppermute | solution.py:135
  682.4 163.5 %collective-permute-start.4 = (f32[2,256,20,64]{1,3,2,0:T(8,128)}, f32[2,256,20,64]{1,3,2,0:T(8,128)}, u32[]{:S(2)}, u32[]{:S(2)}) collective-permute-start(f32[2,256,20,64]{1,3,2,0:T(8,128)} %bitcast_add_fusion.13), channel_id=1, source_target_pairs={{0,32},{32,64},{64,96},{96,0},{1,33},{33,65},{65,97},{97,1},{2,34}... | collective-permute-start | bytes 7864328 | tf_op jit(solution)/shard_map/while/body/eval_jaxpr/ppermute | solution.py:135
  688.5 157.5 %collective-permute-start.5 = (f32[2,256,20,64]{1,3,2,0:T(8,128)}, f32[2,256,20,64]{1,3,2,0:T(8,128)}, u32[]{:S(2)}, u32[]{:S(2)}) collective-permute-start(f32[2,256,20,64]{1,3,2,0:T(8,128)} %bitcast_add_fusion.14), channel_id=1, source_target_pairs={{0,32},{32,64},{64,96},{96,0},{1,33},{33,65},{65,97},{97,1},{2,34}... | collective-permute-start | bytes 7864328 | tf_op jit(solution)/shard_map/while/body/eval_jaxpr/ppermute | solution.py:135
  688.5 129.4 %collective-permute-start.2 = (bf16[2,256,20,64]{1,3,2,0:T(8,128)(2,1)S(1)}, bf16[2,256,20,64]{1,3,2,0:T(8,128)(2,1)}, u32[]{:S(2)}, u32[]{:S(2)}) collective-permute-start(bf16[2,256,20,64]{1,3,2,0:T(8,128)(2,1)S(1)} %copy.115), channel_id=1, source_target_pairs={{0,32},{32,64},{64,96},{96,0},{1,33},{33,65},{65,97},{97,1},{2,34}... | collective-permute-start | bytes 3932168 | tf_op jit(solution)/shard_map/while/body/eval_jaxpr/ppermute | solution.py:135
  688.5 157.5 %collective-permute-start.3 = (bf16[2,256,20,64]{1,3,2,0:T(8,128)(2,1)}, bf16[2,256,20,64]{1,3,2,0:T(8,128)(2,1)}, u32[]{:S(2)}, u32[]{:S(2)}) collective-permute-start(bf16[2,256,20,64]{1,3,2,0:T(8,128)(2,1)} %copy.116), channel_id=1, source_target_pairs={{0,32},{32,64},{64,96},{96,0},{1,33},{33,65},{65,97},{97,1},{2,34}... | collective-permute-start | bytes 3932168 | tf_op jit(solution)/shard_map/while/body/eval_jaxpr/ppermute | solution.py:135
  862.8 162.8 %collective-permute-start.4 = (f32[2,256,20,64]{1,3,2,0:T(8,128)}, f32[2,256,20,64]{1,3,2,0:T(8,128)}, u32[]{:S(2)}, u32[]{:S(2)}) collective-permute-start(f32[2,256,20,64]{1,3,2,0:T(8,128)} %bitcast_add_fusion.13), channel_id=1, source_target_pairs={{0,32},{32,64},{64,96},{96,0},{1,33},{33,65},{65,97},{97,1},{2,34}... | collective-permute-start | bytes 7864328 | tf_op jit(solution)/shard_map/while/body/eval_jaxpr/ppermute | solution.py:135
  868.8 156.8 %collective-permute-start.5 = (f32[2,256,20,64]{1,3,2,0:T(8,128)}, f32[2,256,20,64]{1,3,2,0:T(8,128)}, u32[]{:S(2)}, u32[]{:S(2)}) collective-permute-start(f32[2,256,20,64]{1,3,2,0:T(8,128)} %bitcast_add_fusion.14), channel_id=1, source_target_pairs={{0,32},{32,64},{64,96},{96,0},{1,33},{33,65},{65,97},{97,1},{2,34}... | collective-permute-start | bytes 7864328 | tf_op jit(solution)/shard_map/while/body/eval_jaxpr/ppermute | solution.py:135
  868.8 128.7 %collective-permute-start.2 = (bf16[2,256,20,64]{1,3,2,0:T(8,128)(2,1)S(1)}, bf16[2,256,20,64]{1,3,2,0:T(8,128)(2,1)}, u32[]{:S(2)}, u32[]{:S(2)}) collective-permute-start(bf16[2,256,20,64]{1,3,2,0:T(8,128)(2,1)S(1)} %copy.115), channel_id=1, source_target_pairs={{0,32},{32,64},{64,96},{96,0},{1,33},{33,65},{65,97},{97,1},{2,34}... | collective-permute-start | bytes 3932168 | tf_op jit(solution)/shard_map/while/body/eval_jaxpr/ppermute | solution.py:135
  868.8 156.8 %collective-permute-start.3 = (bf16[2,256,20,64]{1,3,2,0:T(8,128)(2,1)}, bf16[2,256,20,64]{1,3,2,0:T(8,128)(2,1)}, u32[]{:S(2)}, u32[]{:S(2)}) collective-permute-start(bf16[2,256,20,64]{1,3,2,0:T(8,128)(2,1)} %copy.116), channel_id=1, source_target_pairs={{0,32},{32,64},{64,96},{96,0},{1,33},{33,65},{65,97},{97,1},{2,34}... | collective-permute-start | bytes 3932168 | tf_op jit(solution)/shard_map/while/body/eval_jaxpr/ppermute | solution.py:135
  1041.3 49.7 %collective-permute-start.6 = (f32[2,256,20,64]{1,3,2,0:T(8,128)}, f32[2,256,20,64]{1,3,2,0:T(8,128)}, u32[]{:S(2)}, u32[]{:S(2)}) collective-permute-start(f32[2,256,20,64]{1,3,2,0:T(8,128)} %bitcast_add_fusion.5), channel_id=1, source_target_pairs={{0,32},{32,64},{64,96},{96,0},{1,33},{33,65},{65,97},{97,1},{2,34}... | collective-permute-start | bytes 7864328 | tf_op jit(solution)/shard_map/ppermute | solution.py:141
  1046.4 100.7 %collective-permute-start.7 = (f32[2,256,20,64]{1,3,2,0:T(8,128)}, f32[2,256,20,64]{1,3,2,0:T(8,128)}, u32[]{:S(2)}, u32[]{:S(2)}) collective-permute-start(f32[2,256,20,64]{1,3,2,0:T(8,128)} %bitcast_add_fusion.4), channel_id=1, source_target_pairs={{0,32},{32,64},{64,96},{96,0},{1,33},{33,65},{65,97},{97,1},{2,34}... | collective-permute-start | bytes 7864328 | tf_op jit(solution)/shard_map/ppermute | solution.py:142
  1051.0 340.9 %reduce-scatter.6.cloned.1.call-start = ((), (), s32[]{:S(2)}) async-start(), calls=%async_computation.9 | async-start | bytes 40550400 | tf_op jit(solution)/shard_map/reduce_scatter | solution.py:36
  1093.7 53.5 %copy-start.16 = (f32[2,256,1,20,64]{1,4,3,0,2:T(8,128)}, f32[2,256,1,20,64]{1,4,3,0,2:T(8,128)S(1)}, u32[]{:S(2)}) copy-start(f32[2,256,1,20,64]{1,4,3,0,2:T(8,128)S(1)} %maximum_multiply_fusion) | copy-start | bytes 7864324
  1093.7 53.5 %copy-start.6 = (f32[2,256,1280]{2,1,0:T(8,128)S(1)}, f32[2,256,1280]{2,1,0:T(8,128)}, u32[]{:S(2)}) copy-start(f32[2,256,1280]{2,1,0:T(8,128)} %get-tuple-element.703) | copy-start | bytes 7864324
  1093.7 53.5 %copy-start.35 = (f32[1280]{0:T(1024)S(1)}, f32[1280]{0:T(1024)}, u32[]{:S(2)}) copy-start(f32[1280]{0:T(1024)} %copy-done.34) | copy-start | bytes 15364
  1093.7 53.5 %copy-start.41 = (f32[2,256]{1,0:T(2,128)S(1)}, f32[2,256]{1,0:T(2,128)}, u32[]{:S(2)}) copy-start(f32[2,256]{1,0:T(2,128)} %copy-done.40) | copy-start | bytes 6148
  1093.7 53.5 %copy-start.49 = (f32[2,256]{1,0:T(2,128)S(1)}, f32[2,256]{1,0:T(2,128)}, u32[]{:S(2)}) copy-start(f32[2,256]{1,0:T(2,128)} %copy-done.48) | copy-start | bytes 6148
  1093.7 53.5 %copy-start.60 = (f32[1280]{0:T(1024)S(1)}, f32[1280]{0:T(1024)}, u32[]{:S(2)}) copy-start(f32[1280]{0:T(1024)} %copy-done.59) | copy-start | bytes 15364
  1165.4 372.8 %reduce-scatter.10.cloned.1.call-start = ((), (), s32[]{:S(2)}) async-start(), calls=%async_computation.11 | async-start | bytes 27033600 | tf_op jit(solution)/shard_map/reduce_scatter | solution.py:36
  1181.0 503.5 %reduce-scatter.12.cloned.1.call-start = ((), (), s32[]{:S(2)}) async-start(), calls=%async_computation.12 | async-start | bytes 27033600 | tf_op jit(solution)/shard_map/reduce_scatter | solution.py:36
  1198.6 592.3 %all-reduce.12.cloned.1.call-start = ((), (), s32[]{:S(2)}) async-start(), calls=%async_computation.13 | async-start | bytes 204800
  1226.8 715.1 %all-reduce.10.cloned.1.call-start = ((), (), s32[]{:S(2)}) async-start(), calls=%async_computation.8 | async-start | bytes 409600 | tf_op jit(solution)/shard_map/psum | solution.py:156
  1231.6 454.0 %copy-start.56 = (f32[1280]{0:T(1024)S(1)}, f32[1280]{0:T(1024)}, u32[]{:S(2)}) copy-start(f32[1280]{0:T(1024)} %get-tuple-element.614) | copy-start | bytes 15364
  1231.6 785.1 %all-reduce.14.cloned.1.call-start = ((), (), s32[]{:S(2)}) async-start(), calls=%async_computation.14 | async-start | bytes 6144000 | tf_op jit(solution)/shard_map/psum | solution.py:36
  (56 other events, 565.6 us)
Sparse Core Ops, SparseCore 0:
  10.4 83.1 all-gather.5
  95.9 44.5 all-gather.7
  142.7 63.0 all-gather.9
  207.9 63.2 all-gather.11
  1051.1 125.0 reduce-scatter.7
  1180.1 211.7 reduce-scatter.5
  1395.9 142.1 reduce-scatter.9
  1542.1 142.3 reduce-scatter.11
  1688.5 102.3 all-reduce.11
  1796.1 145.7 all-reduce.9
  1944.5 72.2 all-reduce.13
where the time goes:
time: 2040 us; the launch traced here: 2030 us
  waiting for transfers between devices  1400 us (69%)
  matrix products  311 us (15%)
  blocking collectives  166 us (8%)
  other arithmetic  61.2 us (3%)
  local copies, waits for them, and re-layouts  58.9 us (3%)
    reduce_scatter x4, waiting for transfers between devices, reduce_grad(): lax.psum_scatter(full_grad, 'fsdp', scatter_dimension=axis_dim, tiled=True)  453 us
    ppermute x3, waiting for transfers between devices, bwd_body(): lax.ppermute(k_blk, 'cp', send_pairs)  359 us
    psum x1, waiting for transfers between devices, local_step(): lax.psum(d_table, ('cp', 'fsdp'))  140 us
    unnamed x1, blocking collectives  122 us
    unnamed x12, waiting for transfers between devices  93.8 us
    ppermute x3, waiting for transfers between devices, bwd_body(): lax.ppermute(v_blk, 'cp', send_pairs)  84.3 us
    ppermute x3, waiting for transfers between devices, fwd_body(): lax.ppermute(v_blk, 'cp', send_pairs)  84.3 us
    psum x1, waiting for transfers between devices, reduce_grad(): lax.psum(lax.psum_scatter(full_grad, 'fsdp', scatter_dimension=axis_dim,...  74.9 us
  transfers between devices with their start and end apart: 31, of which 20 were waited for; matrix products, arithmetic and copies ran while one was open for 15% of the time, Pallas kernels for 0%

commit v1 on v0

v1 whole, which is shorter than its diff:
```python
import functools

import jax
import jax.numpy as jnp
from jax import lax
from jax.experimental import pallas as pl
from jax.experimental.pallas import tpu as pltpu
from jax.sharding import Mesh, PartitionSpec as P

MASK_ID = 32
VOCAB = 33
LN_EPS = 1e-5
ROPE_BASE = 10000.0
TRAIN_RATIO = 0.15 * 0.8
NEG_BIG = -1e30
SEQ = 1024
QLEN = 256
HEADS = 20
HDIM = 64
PAIRS = HEADS // 2
DIM = HEADS * HDIM
ROWS = 40
F32 = jnp.float32
BF16 = jnp.bfloat16
SWAP = [(0, 1), (1, 0)]
CHIP = ('z', 'y')
FSDP = ('z', 'y', 'c')
PADW = 64
HIGH = lax.Precision.HIGHEST


def mm(a, b, dims=((1,), (0,))):
    return lax.dot_general(a, b, (dims, ((), ())), preferred_element_type=F32)


def ln_stats(z_in):
    row_mean = jnp.mean(z_in, axis=-1, keepdims=True)
    centered = z_in - row_mean
    row_var = jnp.mean(centered * centered, axis=-1, keepdims=True)
    inv = lax.rsqrt(row_var + LN_EPS)
    return centered * inv, inv


def ln_back(d_out, gain, xhat, inv):
    d_hat = d_out * gain
    m1 = jnp.mean(d_hat, axis=-1, keepdims=True)
    m2 = jnp.mean(d_hat * xhat, axis=-1, keepdims=True)
    return inv * (d_hat - m1 - xhat * m2)


def expand_qkv(ohk_ref, ohq_ref, tab_ref, csk_ref, csq_ref):
    ohk = ohk_ref[0]
    z_q = mm(ohq_ref[0], tab_ref[0, 0, :, 0:256])
    q = z_q[:, :128] * csq_ref[:, :128] + z_q[:, 128:] * csq_ref[:, 128:]
    z_k = mm(ohk, tab_ref[0, 0, :, 256:512])
    k = z_k[:, :128] * csk_ref[:, :128] + z_k[:, 128:] * csk_ref[:, 128:]
    v = mm(ohk, tab_ref[0, 0, :, 512:640])
    return q, k.astype(BF16), v.astype(BF16)


def attn_fwd_kernel(len_ref, ohk_ref, ohq_ref, tab_ref, csk_ref, csq_ref, o_ref, lse_ref):
    seq_len = len_ref[pl.program_id(0)]
    q, k, v = expand_qkv(ohk_ref, ohq_ref, tab_ref, csk_ref, csq_ref)
    low = lax.broadcasted_iota(jnp.int32, (QLEN, 128), 1) < HDIM
    key_ok = lax.broadcasted_iota(jnp.int32, (QLEN, SEQ), 1) < seq_len
    outs, stats = [], []
    for head in range(2):
        q_h = jnp.where(low if head == 0 else jnp.logical_not(low), q, 0.0).astype(BF16)
        s = jnp.where(key_ok, mm(q_h, k, ((1,), (1,))), NEG_BIG)
        top = jnp.max(s, axis=-1, keepdims=True)
        e = jnp.exp(s - top)
        total = jnp.sum(e, axis=-1, keepdims=True)
        outs.append(mm(e.astype(BF16), v) / total)
        stats.append(jnp.broadcast_to(top + jnp.log(total), (QLEN, 128)))
    o_ref[0] = jnp.where(low, outs[0], outs[1]).astype(BF16)
    lse_ref[0] = jnp.where(low, stats[0], stats[1])


def attn_bwd_kernel(len_ref, ohk_ref, ohq_ref, tab_ref, csk_ref, csq_ref, do_ref, lse_ref, s_ref):
    seq_len = len_ref[pl.program_id(0)]
    q, k, v = expand_qkv(ohk_ref, ohq_ref, tab_ref, csk_ref, csq_ref)
    d_o = do_ref[0]
    low = lax.broadcasted_iota(jnp.int32, (QLEN, 128), 1) < HDIM
    key_ok = lax.broadcasted_iota(jnp.int32, (QLEN, SEQ), 1) < seq_len
    dv, dk, dqs = None, None, []
    for head in range(2):
        mine = low if head == 0 else jnp.logical_not(low)
        q_h = jnp.where(mine, q, 0.0).astype(BF16)
        do_h = jnp.where(mine, d_o, jnp.zeros_like(d_o))
        s = mm(q_h, k, ((1,), (1,)))
        p = jnp.where(key_ok, jnp.exp(s - lse_ref[0, :, HDIM * head:HDIM * head + 1]), 0.0)
        t = p * mm(do_h, v, ((1,), (1,)))
        ds = (t - p * jnp.sum(t, axis=-1, keepdims=True)).astype(BF16)
        dv_h = mm(p.astype(BF16), do_h, ((0,), (0,)))
        dk_h = mm(ds, q_h, ((0,), (0,)))
        dv = dv_h if dv is None else dv + dv_h
        dk = dk_h if dk is None else dk + dk_h
        dqs.append(mm(ds, k))
    dq = jnp.where(low, dqs[0], dqs[1])
    ohk = ohk_ref[0]
    ohq = ohq_ref[0]
    top = ((0,), (0,))
    s_ref[0, 0, :, 0:128] = mm(ohq, (dq * csq_ref[:, :128]).astype(BF16), top)[:ROWS]
    s_ref[0, 0, :, 128:256] = mm(ohq, (dq * csq_ref[:, 128:]).astype(BF16), top)[:ROWS]
    s_ref[0, 0, :, 256:384] = mm(ohk, (dk * csk_ref[:, :128]).astype(BF16), top)[:ROWS]
    s_ref[0, 0, :, 384:512] = mm(ohk, (dk * csk_ref[:, 128:]).astype(BF16), top)[:ROWS]
    s_ref[0, 0, :, 512:640] = mm(ohk, dv.astype(BF16), top)[:ROWS]


def attn_specs():
    return [
        pl.BlockSpec(memory_space=pltpu.SMEM),
        pl.BlockSpec((1, SEQ, 128), lambda b, j: (b, 0, 0)),
        pl.BlockSpec((1, QLEN, 128), lambda b, j: (b, 0, 0)),
        pl.BlockSpec((1, 1, 128, 640), lambda b, j: (b, j, 0, 0)),
        pl.BlockSpec((SEQ, 256), lambda b, j: (0, 0)),
        pl.BlockSpec((QLEN, 256), lambda b, j: (0, 0)),
    ]


def row_spec():
    return pl.BlockSpec((1, QLEN, 128), lambda b, j: (b, 0, j))


def attn_fwd(lengths, ohk, ohq, tab, csk, csq):
    return pl.pallas_call(
        attn_fwd_kernel, grid=(2, PAIRS), in_specs=attn_specs(), out_specs=[row_spec(), row_spec()],
        out_shape=[jax.ShapeDtypeStruct((2, QLEN, DIM), BF16), jax.ShapeDtypeStruct((2, QLEN, DIM), F32)],
        cost_estimate=pl.CostEstimate(flops=12_000_000_000, bytes_accessed=12_000_000, transcendentals=10_000_000),
        name='attn_fwd')(lengths, ohk, ohq, tab, csk, csq)


def attn_bwd(lengths, ohk, ohq, tab, csk, csq, d_o, lse):
    return pl.pallas_call(
        attn_bwd_kernel, grid=(2, PAIRS), in_specs=attn_specs() + [row_spec(), row_spec()],
        out_specs=pl.BlockSpec((1, 1, ROWS, 640), lambda b, j: (b, j, 0, 0)),
        out_shape=jax.ShapeDtypeStruct((2, PAIRS, ROWS, 640), F32),
        cost_estimate=pl.CostEstimate(flops=30_000_000_000, bytes_accessed=15_000_000, transcendentals=10_000_000),
        name='attn_bwd')(lengths, ohk, ohq, tab, csk, csq, d_o, lse)


def rot_half(z_in):
    return jnp.concatenate([-z_in[..., HDIM // 2:], z_in[..., :HDIM // 2]], axis=-1)


def rot_half_t(z_in):
    return jnp.concatenate([z_in[..., HDIM // 2:], -z_in[..., :HDIM // 2]], axis=-1)


def split3(z_in):
    hi = lax.reduce_precision(z_in, 8, 7)
    rest = z_in - hi
    mid = lax.reduce_precision(rest, 8, 7)
    return jnp.concatenate([hi.astype(BF16), mid.astype(BF16), (rest - mid).astype(BF16)], axis=1)


def build_tab(t_all):
    q = t_all[:, :, 0] * HDIM ** -0.5
    k = t_all[:, :, 1]
    v = t_all[:, :, 2]

    def pairs(z_in):
        return z_in.reshape(2, VOCAB, PAIRS, 128)
    wide = jnp.concatenate([pairs(q), pairs(rot_half(q)), pairs(k), pairs(rot_half(k))], axis=-1)
    wide = split3(wide)
    v_hi = jnp.pad(pairs(v).astype(BF16), ((0, 0), (0, 2 * VOCAB), (0, 0), (0, 0)))
    full = jnp.concatenate([wide, v_hi], axis=-1)
    full = jnp.pad(full, ((0, 0), (0, 128 - 3 * VOCAB), (0, 0), (0, 0)))
    return jnp.swapaxes(full, 1, 2)


def one_hot3(tok):
    lanes = jnp.arange(128)
    return ((tok[..., None] == lanes % VOCAB) & (lanes < 3 * VOCAB)).astype(BF16)


def all_sum(small, axes):
    for axis, size in axes:
        step = 1
        while step < size:
            small = small + lax.ppermute(small, axis, [(i, i ^ step) for i in range(size)])
            step *= 2
    return small


def solution(mesh):
    mesh4 = Mesh(mesh.devices.reshape(4, 4, 4, 2), ('x', 'z', 'y', 'c'))

    def local_step(tokens, lengths, embed_table, layer_vecs, w_qkv, w_out, w_up, b_up, w_down, grad_out):
        xi = lax.axis_index('x')
        ci = lax.axis_index('c')
        chip = lax.axis_index('z') * 4 + lax.axis_index('y')
        fi = chip * 2 + ci
        wq_loc = lax.dynamic_slice_in_dim(w_qkv, 5 * xi, 5, axis=2).reshape(ROWS, 960)
        qkv_w = lax.all_gather(wq_loc, FSDP, axis=0, tiled=True)
        packed = jnp.concatenate([layer_vecs.reshape(360), b_up, jnp.zeros((504,), F32)]).reshape(8, 128)
        packed = lax.all_gather(packed, FSDP, axis=0, tiled=True).reshape(32, 1024)
        vecs = packed[:, :360].reshape(32, 9, ROWS).transpose(1, 0, 2).reshape(9, DIM)
        up_b = lax.dynamic_index_in_dim(packed[:, 360:520].reshape(16, 2, 160), ci, axis=1, keepdims=False).reshape(2560)
        tok_all = lax.all_gather(tokens, 'x', axis=1, tiled=True)
        up_loc = w_up.reshape(ROWS, 16, 2, 160)
        up_mine = lax.dynamic_index_in_dim(up_loc, ci, axis=2, keepdims=False).reshape(ROWS, 2560)
        up_send = lax.dynamic_index_in_dim(up_loc, 1 - ci, axis=2, keepdims=False).reshape(ROWS, 2560)
        up_recv = lax.ppermute(up_send, 'c', SWAP)
        up_pair = jnp.concatenate([jnp.where(ci == 0, up_mine, up_recv), jnp.where(ci == 0, up_recv, up_mine)], axis=0)
        shard = jnp.concatenate([up_pair[:, :DIM], up_pair[:, DIM:], w_down, w_out], axis=0)
        gathered = lax.all_gather(shard, CHIP, axis=0, tiled=False)
        grad_own = grad_out.reshape(2 * QLEN, DIM)
        grad2 = jnp.concatenate([grad_own, lax.ppermute(grad_own, 'c', SWAP)], axis=0)

        positions = jnp.arange(SEQ)
        tok_eff = jnp.where(positions[None, :] < lengths[:, None], tok_all, MASK_ID)
        tok_own = lax.dynamic_slice_in_dim(tok_eff, xi * QLEN, QLEN, axis=1)
        mask_count = jnp.sum((tok_all == MASK_ID).astype(F32), axis=1)
        drop_scale = (1.0 - TRAIN_RATIO) / (1.0 - mask_count / lengths.astype(F32))
        ohk = one_hot3(tok_eff)
        ohq = one_hot3(tok_own)
        oh_own = ohq[:, :, :VOCAB]
        row_scale = jnp.where(jnp.arange(VOCAB)[None, :] == MASK_ID, 0.0, drop_scale[:, None])
        e_rows = embed_table.astype(F32)[None] * row_scale[:, :, None]
        xhat1, inv1 = ln_stats(e_rows)
        h_rows = (xhat1 * vecs[0] + vecs[1]).astype(BF16).reshape(2 * VOCAB, DIM)
        t_loc = mm(h_rows, qkv_w)
        t_all = lax.all_gather(t_loc, 'x', axis=0, tiled=False)
        t_all = t_all.reshape(4, 2, VOCAB, 3, 5, HDIM).transpose(1, 2, 3, 0, 4, 5).reshape(2, VOCAB, 3, HEADS, HDIM)
        t_all = t_all + vecs[2:5].reshape(3, HEADS, HDIM)
        tab = build_tab(t_all)
        inv_freq = 1.0 / (ROPE_BASE ** (jnp.arange(0, HDIM, 2, dtype=F32) / HDIM))
        angles = positions.astype(F32)[:, None] * inv_freq[None, :]
        csk = jnp.concatenate([jnp.tile(jnp.cos(angles), (1, 4)), jnp.tile(jnp.sin(angles), (1, 4))], axis=1)
        csq = lax.dynamic_slice_in_dim(csk, xi * QLEN, QLEN, axis=0)

        attn_o, lse = attn_fwd(lengths, ohk, ohq, tab, csk, csq)
        attn_o, gathered = lax.optimization_barrier((attn_o, gathered))
        up_w0 = gathered[:, 0:80].reshape(DIM, DIM)
        up_w1 = gathered[:, 80:160].reshape(DIM, DIM)
        down_w = gathered[:, 160:320].reshape(2 * DIM, DIM)
        out_mine = gathered[:, 320:360]
        out_recv = lax.ppermute(out_mine, 'c', SWAP)
        out_w = jnp.stack([jnp.where(ci == 0, out_mine, out_recv), jnp.where(ci == 0, out_recv, out_mine)], axis=1).reshape(DIM, DIM)
        attn_o2 = attn_o.reshape(2 * QLEN, DIM)
        keep_own = jnp.where(tok_own == MASK_ID, 0.0, drop_scale[:, None])
        embedded = jnp.einsum('bsv,vd->bsd', oh_own, embed_table, preferred_element_type=F32) * keep_own[:, :, None]
        x1 = embedded.reshape(2 * QLEN, DIM) + mm(attn_o2, out_w) + vecs[5]
        xhat2, inv2 = ln_stats(x1)
        nm = (xhat2 * vecs[6] + vecs[7]).astype(BF16)
        nm2 = jnp.concatenate([nm, lax.ppermute(nm, 'c', SWAP)], axis=0)
        up_lin = jnp.concatenate([mm(nm2, up_w0), mm(nm2, up_w1)], axis=1) + up_b
        cdf = 0.5 * (1.0 + lax.erf(up_lin * 0.7071067811865476))
        gelu_b = (up_lin * cdf).astype(BF16)
        slope = cdf + up_lin * (0.3989422804014327 * jnp.exp(-0.5 * up_lin * up_lin))
        down2 = mm(gelu_b, down_w)
        down_got = lax.ppermute(down2[2 * QLEN:], 'c', SWAP)
        layer_out = (x1 + down2[:2 * QLEN] + down_got + vecs[8]).astype(BF16).reshape(2, QLEN, DIM)

        d_down = mm(gelu_b, grad2, ((0,), (0,)))
        d_up_lin = mm(grad2, down_w, ((1,), (1,))) * slope
        d_up_b = d_up_lin.astype(BF16)
        d_up = mm(nm2, d_up_b, ((0,), (0,)))
        d_nm2 = mm(d_up_b[:, :DIM], up_w0, ((1,), (1,))) + mm(d_up_b[:, DIM:], up_w1, ((1,), (1,)))
        d_nm = d_nm2[:2 * QLEN] + lax.ppermute(d_nm2[2 * QLEN:], 'c', SWAP)
        grad32 = grad_own.astype(F32)
        d_resid = grad32 + ln_back(d_nm, vecs[6], xhat2, inv2)
        d_resid_b = d_resid.astype(BF16)
        d_outw = mm(attn_o2, d_resid_b, ((0,), (0,)))
        d_attn_b = mm(d_resid_b, out_w, ((1,), (1,))).astype(BF16)
        s_tab = attn_bwd(lengths, ohk, ohq, tab, csk, csq, d_attn_b.reshape(2, QLEN, DIM), lse)

        s_tab = jnp.swapaxes(s_tab[:, :, :VOCAB], 1, 2)

        def heads(z_in):
            return z_in.reshape(2, VOCAB, HEADS, HDIM)
        s_q = (heads(s_tab[..., 0:128]) + rot_half_t(heads(s_tab[..., 128:256]))) * HDIM ** -0.5
        s_k = heads(s_tab[..., 256:384]) + rot_half_t(heads(s_tab[..., 384:512]))
        s_v = heads(s_tab[..., 512:640])
        s_all = jnp.stack([s_q, s_k, s_v], axis=2)
        d_bqkv = jnp.sum(s_all, axis=(0, 1)).reshape(3, DIM)
        s_x = s_all.reshape(2 * VOCAB, 3, 4, 5, HDIM).transpose(2, 0, 1, 3, 4).reshape(4, 2 * VOCAB, 960)
        s_mine = lax.dynamic_index_in_dim(s_x, xi, axis=0, keepdims=False)
        for hop in range(1, 4):
            part = lax.dynamic_index_in_dim(s_x, (xi + hop) % 4, axis=0, keepdims=False)
            s_mine = s_mine + lax.ppermute(part, 'x', [(i, (i + hop) % 4) for i in range(4)])
        d_qkvw = lax.dot_general(h_rows.astype(F32), s_mine, (((0,), (0,)), ((), ())), precision=HIGH, preferred_element_type=F32)
        d_h = lax.dot_general(s_mine, qkv_w.astype(F32), (((1,), (1,)), ((), ())), precision=HIGH, preferred_element_type=F32)
        d_h = d_h.reshape(2, VOCAB, DIM)
        d_e = ln_back(d_h, vecs[0], xhat1, inv1)
        d_e = d_e + jnp.einsum('bsv,bsd->bvd', oh_own, d_resid_b.reshape(2, QLEN, DIM), preferred_element_type=F32)
        d_table = jnp.sum(d_e * row_scale[:, :, None], axis=0)
        d_up_bias = jnp.sum(d_up_lin, axis=0).reshape(1, 2, DIM)
        d_up_bias = jnp.where(jnp.arange(2)[:, None, None] == ci, d_up_bias, 0.0).reshape(4, DIM)
        small = jnp.concatenate([
            d_table,
            jnp.sum(d_h * xhat1, axis=(0, 1))[None], jnp.sum(d_h, axis=(0, 1))[None], d_bqkv,
            jnp.sum(d_resid, axis=0)[None], jnp.sum(d_nm * xhat2, axis=0)[None], jnp.sum(d_nm, axis=0)[None],
            jnp.sum(grad32, axis=0)[None], d_up_bias, jnp.zeros((2, DIM), F32)], axis=0)
        small = all_sum(small, (('c', 2), ('x', 4), ('y', 4), ('z', 4)))
        d_vecs = lax.dynamic_slice(small, (VOCAB, fi * ROWS), (9, ROWS))
        d_bup_half = lax.dynamic_slice_in_dim(small, VOCAB + 9 + 2 * ci, 2, axis=0).reshape(2560)
        d_bup = lax.dynamic_slice_in_dim(d_bup_half, chip * 160, 160, axis=0)

        r_down = all_sum(lax.psum_scatter(d_down, CHIP, scatter_dimension=0, tiled=True), (('x', 4),))
        r_up = all_sum(lax.psum_scatter(d_up, CHIP, scatter_dimension=0, tiled=True), (('x', 4),))
        d_oq = jnp.concatenate([d_outw, d_qkvw, jnp.zeros((DIM, PADW), F32)], axis=1).reshape(16, 2, ROWS, DIM + 960 + PADW)
        oq_keep = lax.dynamic_index_in_dim(d_oq, ci, axis=1, keepdims=False)
        oq_give = lax.dynamic_index_in_dim(d_oq, 1 - ci, axis=1, keepdims=False)
        d_oq = oq_keep + lax.ppermute(oq_give, 'c', SWAP)
        r_oq = lax.psum_scatter(d_oq, CHIP, scatter_dimension=0, tiled=False)
        r_out = all_sum(r_oq[:, :DIM], (('x', 4),))
        r_qkv = lax.all_gather(r_oq[:, DIM:DIM + 960], 'x', axis=0, tiled=False)
        up_keep = lax.dynamic_slice_in_dim(r_up, ci * ROWS, ROWS, axis=0)
        up_give = lax.dynamic_slice_in_dim(r_up, (1 - ci) * ROWS, ROWS, axis=0)
        up_got = lax.ppermute(up_give, 'c', SWAP)
        r_up = jnp.stack([jnp.where(ci == 0, up_keep, up_got).reshape(ROWS, 16, 160),
                          jnp.where(ci == 0, up_got, up_keep).reshape(ROWS, 16, 160)], axis=2).reshape(ROWS, 5120)
        r_qkv = r_qkv.reshape(4, ROWS, 3, 5, HDIM).transpose(1, 2, 0, 3, 4).reshape(ROWS, 3, HEADS, HDIM)
        return layer_out, small[:VOCAB], d_vecs, r_qkv, r_out, r_up, d_bup, r_down

    in_specs = (P(FSDP, 'x'), P(FSDP), P(), P(None, FSDP), P(FSDP, None, None, None), P(FSDP, None), P(FSDP, None), P(FSDP), P(FSDP, None), P(FSDP, 'x', None))
    out_specs = (P(FSDP, 'x', None), P(), P(None, FSDP), P(FSDP, None, None, None), P(FSDP, None), P(FSDP, None), P(FSDP), P(FSDP, None))
    return jax.shard_map(local_step, mesh=mesh4, in_specs=in_specs, out_specs=out_specs, check_vma=False)
```

time: 2040 us -> 616 us (0.30)
  waiting for transfers between devices: 1400 us -> 115 us
  matrix products: 311 us -> 97.7 us
  Pallas kernels: 0 us -> 91.6 us
  blocking collectives: 166 us -> 77.4 us
  local copies, waits for them, and re-layouts: 58.9 us -> 107 us
  starting transfers between devices: 11.5 us -> 32.9 us
    ppermute x20 -> x24, waiting for transfers between devices: 642 us -> 92.3 us  [the longest x13 63.5 us: all_sum(): lax.ppermute(small, axis, [(i, i ^ step) for i in range(size)])]
    reduce_scatter x4 -> x2, waiting for transfers between devices: 453 us -> 0.02 us  [the longest x1 0.02 us: local_step(): lax.psum_scatter(d_down, CHIP, scatter_dimension=0, tiled=True)]
    psum x2 -> x0, waiting for transfers between devices: 215 us -> none  [the longest x1 140 us: local_step(): lax.psum(d_table, ('cp', 'fsdp'))]
    dot_general x42 -> x16, matrix products: 311 us -> 97.7 us  [the longest x12 86.6 us: mm(): return lax.dot_general(a, b, (dims, ((), ())), preferred_element_type=F32)]
    unnamed x1 -> x0, blocking collectives: 122 us -> none
    unnamed x12 -> x6, waiting for transfers between devices: 93.8 us -> 0.08 us
    pallas_call x0 -> x2, Pallas kernels: none -> 91.6 us  [the longest x1 58.6 us: attn_bwd(): pl.pallas_call(attn_bwd_kernel, grid=(2, PAIRS), in_specs=attn_specs() +...]
    all_gather x1 -> x4, blocking collectives: 27.6 us -> 77.4 us  [the longest x1 28.7 us: local_step(): packed = lax.all_gather(packed, FSDP, axis=0, tiled=True).reshape(32, 1024)]
  transfers between devices with their start and end apart: 31 -> 29, of which waited for: 20 -> 15; matrix products, arithmetic and copies ran while one was open for 15% -> 36% of each run, Pallas kernels for 0% -> 15%
where the time goes in v1:
time: 616 us; the launch traced here: 605 us
  waiting for transfers between devices  115 us (19%)
  local copies, waits for them, and re-layouts  107 us (17%)
  matrix products  97.7 us (16%)
  Pallas kernels  91.6 us (15%)
  blocking collectives  77.4 us (13%)
  other arithmetic  67.1 us (11%)
  starting transfers between devices  32.9 us (5%)
  between operations  15.7 us (3%)
    dot_general x12, matrix products, mm(): return lax.dot_general(a, b, (dims, ((), ())), preferred_element_type=F32)  86.6 us
    ppermute x13, waiting for transfers between devices, all_sum(): lax.ppermute(small, axis, [(i, i ^ step) for i in range(size)])  63.5 us
    pallas_call x1, Pallas kernels, attn_bwd(): pl.pallas_call(attn_bwd_kernel, grid=(2, PAIRS), in_specs=attn_specs() +...  58.6 us
    pallas_call x1, Pallas kernels, attn_fwd(): pl.pallas_call(attn_fwd_kernel, grid=(2, PAIRS), in_specs=attn_specs(), o...  33 us
    all_gather x1, blocking collectives, local_step(): packed = lax.all_gather(packed, FSDP, axis=0, tiled=True).reshape(32, 1024)  28.7 us
    all_gather x1, blocking collectives, local_step(): r_qkv = lax.all_gather(r_oq[:, DIM:DIM + 960], 'x', axis=0, tiled=False)  24.3 us
    all_gather x1, waiting for transfers between devices, local_step(): gathered = lax.all_gather(shard, CHIP, axis=0, tiled=False)  22.3 us
    ppermute x3, waiting for transfers between devices, local_step(): lax.ppermute(part, 'x', [(i, (i + hop) % 4) for i in range(4)])  16.2 us
  transfers between devices with their start and end apart: 29, of which 15 were waited for; matrix products, arithmetic and copies ran while one was open for 36% of the time, Pallas kernels for 15%

profile of v1, /device:TPU:1, one launch (start us, length us, event | category | flops | bytes accessed | tf_op | source)
XLA Modules:
  0.0 604.5 jit_solution(11954553344112585255)
XLA Ops:
  11.0 4.1 dynamic-slice_reduce_fusion.1
  19.4 9.8 %all_gather.27 = s32[2,1024]{1,0:T(2,128)S(1)} all-gather(s32[2,256]{1,0:T(2,128)S(1)} %copy-done.69), channel_id=1, replica_groups=mesh['x'=4,'z'=4,'y'=4,'c'=2] {'x'}, dimensions={1}, use_global_device_ids=true | all-gather | bytes 10240 | tf_op jit(solution)/shard_map/all_gather | solution.py:200
  29.6 28.7 %all_gather.28 = f32[256,128]{1,0:T(8,128)S(1)} all-gather(f32[8,128]{1,0:T(8,128)S(1)} %maximum_bitcast_fusion.1), channel_id=1, replica_groups=mesh['x'=4,'z'=4,'y'=4,'c'=2] {'z','y','c'}, dimensions={0}, use_global_device_ids=true | all-gather | bytes 135168 | tf_op jit(solution)/shard_map/all_gather | solution.py:197
  65.8 2.4 convolution_bitcast_fusion
  68.2 14.5 %all-gather.3 = f32[4,66,960]{2,1,0:T(8,128)S(1)} all-gather(f32[1,66,960]{2,1,0:T(8,128)S(1)} %convolution_bitcast_fusion), channel_id=2, replica_groups=mesh['x'=4,'z'=4,'y'=4,'c'=2] {'x'}, dimensions={0}, use_global_device_ids=true | all-gather | bytes 1267200 | tf_op jit(solution)/shard_map/all_gather | solution.py:224
  83.4 2.4 reshape.533
  85.8 3.5 copy.126
  105.6 33.0 %attn_fwd.1 = (bf16[2,256,1280]{2,1,0:T(8,128)(2,1)}, f32[2,256,1280]{2,1,0:T(8,128)}) custom-call(s32[2]{0:T(128)} %len_ref.3, bf16[2,1024,128]{2,1,0:T(8,128)(2,1)} %and_convert_fusion.ohk_ref, bf16[2,256,128]{2,1,0:T(8,128)(2,1)} %get-tuple-element.74.ohq_ref, bf16[2,10,128,640]{3,2,1,0:T(8,128)(2,1)} %pad_bitcast_fusion.tab_ref, ...), custom_call_target="tpu_custom_call" | custom-call | flops 12000000000 | bytes 12000000 | tf_op jit(solution)/shard_map/attn_fwd/pallas_call | solution.py:126
  138.7 22.3 %all-gather.9.cloned.1.call-done = bf16[5760,1280]{1,0:T(8,128)(2,1)} async-done(((bf16[360,1280]{1,0:T(8,128)(2,1)}), bf16[5760,1280]{1,0:T(8,128)(2,1)}) %all-gather.9.cloned.1.call-update) | async-done | bytes 14745616 | tf_op jit(solution)/shard_map/all_gather | solution.py:207
  175.5 3.3 slice.157
  178.8 5.7 fusion.49
  184.5 9.5 %fusion.23 = f32[1024,1280]{1,0:T(8,128)} fusion(bf16[1280,1280]{1,0:T(8,128)(2,1)S(1)} %bitcast.127, bf16[512,1280]{1,0:T(8,128)(2,1)} %collective-permute-done.2, bf16[512,1280]{1,0:T(8,128)(2,1)} %add_convert_fusion), kind=kOutput, calls=%fused_computation.71 | convolution fusion | flops 3360686080 | bytes 11141120 | tf_op jit(solution)/shard_map/dot_general | solution.py:33
  194.1 7.6 %fusion.24 = f32[1024,1280]{1,0:T(8,128)} fusion(bf16[1280,1280]{1,0:T(8,128)(2,1)S(1)} %bitcast.129, bf16[512,1280]{1,0:T(8,128)(2,1)} %collective-permute-done.2, bf16[512,1280]{1,0:T(8,128)(2,1)} %add_convert_fusion), kind=kOutput, calls=%fused_computation.72 | convolution fusion | flops 3360686080 | bytes 11141120 | tf_op jit(solution)/shard_map/dot_general | solution.py:33
  201.6 14.0 %fusion.50 = (f32[2560]{0:T(1024)S(1)}, bf16[1024,2560]{1,0:T(8,128)(2,1)}) fusion(f32[2560]{0:T(1024)S(1)} %add.325, f32[1024,1280]{1,0:T(8,128)} %fusion.23, f32[1024,1280]{1,0:T(8,128)} %fusion.24, bf16[2560,1280]{1,0:T(8,128)(2,1)S(1)} %bitcast.116, bf16[512,1280]{1,0:T(8,128)(2,1)} %collective-permute-done.4, bf16[512,1280]{1,0:T(8,128)(2,1)} %bitcast.22), kind=kOutput, calls=%fused_computation.171 | convolution fusion | flops 6750205440 | bytes 24924160 | tf_op jit(solution)/shard_map/dot_general | solution.py:33
  215.7 12.9 %fusion.22 = f32[1280,2560]{1,0:T(8,128)} fusion(bf16[1024,2560]{1,0:T(8,128)(2,1)} %get-tuple-element.42, bf16[512,1280]{1,0:T(8,128)(2,1)} %collective-permute-done.2, bf16[512,1280]{1,0:T(8,128)(2,1)} %add_convert_fusion), kind=kOutput, calls=%fused_computation.70 | convolution fusion | flops 6716129280 | bytes 20971520 | tf_op jit(solution)/shard_map/dot_general | solution.py:33
  228.7 5.5 multiply_convert_fusion
  236.6 11.7 %fusion.15 = f32[2560,1280]{1,0:T(8,128)} fusion(bf16[1024,2560]{1,0:T(8,128)(2,1)S(1)} %multiply_convert_fusion, bf16[512,1280]{1,0:T(8,128)(2,1)} %collective-permute-done.4, bf16[512,1280]{1,0:T(8,128)(2,1)} %bitcast.22), kind=kOutput, calls=%fused_computation.49 | convolution fusion | flops 6716129280 | bytes 20971520 | tf_op jit(solution)/shard_map/dot_general | solution.py:33
  248.6 6.5 %fusion.9 = f32[1024,1280]{1,0:T(8,128)S(1)} fusion(bf16[1280,1280]{1,0:T(8,128)(2,1)} %bitcast.130, bf16[1024,2560]{1,0:T(8,128)(2,1)} %get-tuple-element.42), kind=kOutput, calls=%fused_computation.25 | convolution fusion | flops 3355443200 | bytes 11141120 | tf_op jit(solution)/shard_map/dot_general | solution.py:33
  255.1 5.5 convolution_add_fusion
  264.2 6.9 %fusion.55 = f32[1024,1280]{1,0:T(8,128)S(1)} fusion(bf16[1024,2560]{1,0:T(8,128)(2,1)S(1)} %bitcast.123, bf16[2560,1280]{1,0:T(8,128)(2,1)S(1)} %bitcast.119), kind=kOutput, calls=%fused_computation.178 | convolution fusion | flops 6710886400 | bytes 17039360 | tf_op jit(solution)/shard_map/dot_general | solution.py:33
  275.2 4.0 multiply_reduce_fusion
  279.7 4.3 fusion.48
  284.0 2.9 convolution_convert_fusion
  286.9 58.6 %attn_bwd.1 = f32[2,10,40,640]{3,2,1,0:T(8,128)} custom-call(s32[2]{0:T(128)} %len_ref.3, bf16[2,1024,128]{2,1,0:T(8,128)(2,1)} %and_convert_fusion.ohk_ref, bf16[2,256,128]{2,1,0:T(8,128)(2,1)} %get-tuple-element.74.ohq_ref, bf16[2,10,128,640]{3,2,1,0:T(8,128)(2,1)} %pad_bitcast_fusion.tab_ref, f32[1024,256]{1,0:T(8,128)} %pad_maximum_fusion.6.csk_ref, ...), custom_call_target="tpu_custom_call" | custom-call | flops 30000001024 | bytes 15000000 | tf_op jit(solution)/shard_map/attn_bwd/pallas_call | solution.py:134
  361.6 2.5 reshape.573
  365.2 2.4 maximum_add_fusion.2
  371.5 2.4 copy.160
  378.5 4.6 fusion.56
  383.1 4.9 collective-permute-done.6
  388.0 11.3 %collective-permute-done.7 = f32[66,960]{0,1:T(8,128)S(1)} collective-permute-done((f32[66,960]{0,1:T(8,128)S(1)}, f32[66,960]{0,1:T(8,128)S(1)}, u32[]{:S(2)}, u32[]{:S(2)}) %collective-permute-start.7) | collective-permute-done | bytes 253472 | tf_op jit(solution)/shard_map/ppermute | solution.py:282
  400.3 4.3 fusion.46
  404.6 9.5 %maximum_maximum_fusion = f32[1280,2304]{0,1:T(8,128)} fusion(f32[1280,960]{0,1:T(8,128)} %fusion.46, f32[1280,1280]{0,1:T(8,128)} %fusion.56, f32[2304]{0:T(1024)S(1)} %pad.14.clone), kind=kLoop, calls=%fused_computation.1 | loop fusion | flops 5898240 | bytes 23274496 | tf_op jit(solution)/shard_map/concatenate | solution.py:303
  414.2 13.6 %copy.168 = f32[1280,2304]{1,0:T(8,128)} copy(f32[1280,2304]{0,1:T(8,128)} %maximum_maximum_fusion) | data formatting | bytes 23592960 | tf_op jit(solution)/shard_map/concatenate | solution.py:303
  427.8 3.2 dynamic-slice_bitcast_fusion
  432.3 9.2 %collective-permute-done.16 = f32[16,40,2304]{2,1,0:T(8,128)S(1)} collective-permute-done((f32[16,40,2304]{2,1,0:T(8,128)S(1)}, f32[16,40,2304]{2,1,0:T(8,128)S(1)}, u32[]{:S(2)}, u32[]{:S(2)}) %collective-permute-start.16) | collective-permute-done | bytes 5898272 | tf_op jit(solution)/shard_map/ppermute | solution.py:306
  441.5 3.6 bitcast_add_fusion
  458.1 4.5 multiply_reduce_fusion.5
  468.9 5.9 collective-permute-done.10
  476.6 22.3 %collective-permute-done.11 = f32[48,1280]{1,0:T(8,128)S(1)} collective-permute-done((f32[48,1280]{1,0:T(8,128)S(1)}, f32[48,1280]{1,0:T(8,128)S(1)}, u32[]{:S(2)}, u32[]{:S(2)}) %collective-permute-start.11) | collective-permute-done | bytes 245792 | tf_op jit(solution)/shard_map/ppermute | solution.py:181
  500.2 5.1 collective-permute-done.12
  505.4 2.8 collective-permute-start.13
  508.2 6.2 %collective-permute-done.13 = f32[48,1280]{1,0:T(8,128)S(1)} collective-permute-done((f32[48,1280]{1,0:T(8,128)S(1)}, f32[48,1280]{1,0:T(8,128)S(1)}, u32[]{:S(2)}, u32[]{:S(2)}) %collective-permute-start.13) | collective-permute-done | bytes 245792 | tf_op jit(solution)/shard_map/ppermute | solution.py:181
  517.3 6.5 %collective-permute-done.14 = f32[48,1280]{1,0:T(8,128)S(1)} collective-permute-done((f32[48,1280]{1,0:T(8,128)S(1)}, f32[48,1280]{1,0:T(8,128)S(1)}, u32[]{:S(2)}, u32[]{:S(2)}) %collective-permute-start.14) | collective-permute-done | bytes 245792 | tf_op jit(solution)/shard_map/ppermute | solution.py:181
  524.1 6.5 %collective-permute-done.15 = f32[48,1280]{1,0:T(8,128)S(1)} collective-permute-done((f32[48,1280]{1,0:T(8,128)S(1)}, f32[48,1280]{1,0:T(8,128)S(1)}, u32[]{:S(2)}, u32[]{:S(2)}) %collective-permute-start.15) | collective-permute-done | bytes 245792 | tf_op jit(solution)/shard_map/ppermute | solution.py:181
  537.6 9.4 %collective-permute-done.20 = f32[80,2560]{1,0:T(8,128)} collective-permute-done((f32[80,2560]{1,0:T(8,128)S(1)}, f32[80,2560]{1,0:T(8,128)}, u32[]{:S(2)}, u32[]{:S(2)}) %collective-permute-start.20) | collective-permute-done | bytes 819232 | tf_op jit(solution)/shard_map/ppermute | solution.py:181
  549.1 10.9 %collective-permute-start.21 = (f32[40,2560]{1,0:T(8,128)}, f32[40,2560]{1,0:T(8,128)}, u32[]{:S(2)}, u32[]{:S(2)}) collective-permute-start(f32[40,2560]{1,0:T(8,128)} %constant_dynamic-slice_fusion.1), channel_id=1, source_target_pairs={{0,1},{1,0},{2,3},{3,2},{4,5},{5,4},{6,7},{7,6},{8,9},{9,8},{10,11... | collective-permute-start | bytes 1228808 | tf_op jit(solution)/shard_map/ppermute | solution.py:312
  561.6 24.3 %all-gather.2 = f32[160,960]{1,0:T(8,128)} all-gather(f32[40,960]{1,0:T(8,128)S(1)} %slice.214), channel_id=4, replica_groups=mesh['x'=4,'z'=4,'y'=4,'c'=2] {'x'}, dimensions={0}, use_global_device_ids=true | all-gather | bytes 768000 | tf_op jit(solution)/shard_map/all_gather | solution.py:309
  594.9 2.7 reshape.562
  (398 shorter events, 130.1 us)
Async XLA Ops:
  7.2 58.6 %all-gather.7.cloned.1.call-start = ((), (), s32[]{:S(2)}) async-start(), calls=%async_computation.3 | async-start | bytes 2703360 | tf_op jit(solution)/shard_map/all_gather | solution.py:195
  9.2 151.8 %all-gather.9.cloned.1.call-start = ((), (), s32[]{:S(2)}) async-start(), calls=%async_computation.6 | async-start | bytes 15667200 | tf_op jit(solution)/shard_map/all_gather | solution.py:207
  15.6 14.0 %copy-start.70 = (f32[160]{0:T(256)S(1)}, f32[160]{0:T(256)}, u32[]{:S(2)}) copy-start(f32[160]{0:T(256)} %param.17) | copy-start | bytes 1924
  15.6 2.5 collective-permute-start
  17.0 41.4 %copy-start.39 = (bf16[33,1280]{1,0:T(8,128)(2,1)S(1)}, bf16[33,1280]{1,0:T(8,128)(2,1)}, u32[]{:S(2)}) copy-start(bf16[33,1280]{1,0:T(8,128)(2,1)} %param.12) | copy-start | bytes 253444
  19.2 449.1 %reduce-scatter.6.cloned.1.call-start = ((), (), s32[]{:S(2)}) async-start(), calls=%async_computation.4 | async-start | bytes 13926400 | tf_op jit(solution)/shard_map/reduce_scatter | solution.py:302
  63.7 19.0 %copy-start.65 = (f32[66]{0:T(128)}, f32[66]{0:T(128)S(1)}, u32[]{:S(2)}) copy-start(f32[66]{0:T(128)S(1)} %broadcast_select_fusion.4) | copy-start | bytes 796
  64.6 99.6 %copy-start.44 = (pred[2,256,128]{2,1,0:T(32,128)(4,1)}, pred[2,256,128]{2,1,0:T(32,128)(4,1)S(1)}, u32[]{:S(2)}) copy-start(pred[2,256,128]{2,1,0:T(32,128)(4,1)S(1)} %get-tuple-element.73) | copy-start | bytes 196612
  138.7 25.3 %copy-start.55 = (f32[32,40]{1,0:T(8,128)S(1)}, f32[32,40]{1,0:T(8,128)}, u32[]{:S(2)}) copy-start(f32[32,40]{1,0:T(8,128)} %get-tuple-element.28) | copy-start | bytes 15364
  138.7 25.4 %copy-start.54 = (f32[32,40]{1,0:T(8,128)S(1)}, f32[32,40]{1,0:T(8,128)}, u32[]{:S(2)}) copy-start(f32[32,40]{1,0:T(8,128)} %get-tuple-element.27) | copy-start | bytes 15364
  138.7 25.5 %copy-start.53 = (f32[32,40]{1,0:T(8,128)S(1)}, f32[32,40]{1,0:T(8,128)}, u32[]{:S(2)}) copy-start(f32[32,40]{1,0:T(8,128)} %get-tuple-element.29) | copy-start | bytes 15364
  162.5 4.5 collective-permute-start.1
  174.7 9.8 %collective-permute-start.2 = (bf16[512,1280]{1,0:T(8,128)(2,1)}, bf16[512,1280]{1,0:T(8,128)(2,1)}, u32[]{:S(2)}, u32[]{:S(2)}) collective-permute-start(bf16[512,1280]{1,0:T(8,128)(2,1)} %add_convert_fusion), channel_id=1, source_target_pairs={{0,1},{1,0},{2,3},{3,2},{4,5},{5,4},{6,7},{7,6},{8,9},{9,8},{10,11... | collective-permute-start | bytes 3932168 | tf_op jit(solution)/shard_map/ppermute | solution.py:247
  175.1 26.6 %collective-permute-start.4 = (bf16[512,1280]{1,0:T(8,128)(2,1)}, bf16[512,1280]{1,0:T(8,128)(2,1)}, u32[]{:S(2)}, u32[]{:S(2)}) collective-permute-start(bf16[512,1280]{1,0:T(8,128)(2,1)} %bitcast.22), channel_id=1, source_target_pairs={{0,1},{1,0},{2,3},{3,2},{4,5},{5,4},{6,7},{7,6},{8,9},{9,8},{10,11... | collective-permute-start | bytes 3932168 | tf_op jit(solution)/shard_map/ppermute | solution.py:209
  178.8 22.9 %copy-start.7 = (bf16[16,160,1280]{2,1,0:T(8,128)(2,1)}, bf16[16,160,1280]{2,1,0:T(8,128)(2,1)S(1)}, u32[]{:S(2)}) copy-start(bf16[16,160,1280]{2,1,0:T(8,128)(2,1)S(1)} %slice.157) | copy-start | bytes 19660804
  228.6 285.9 %reduce-scatter.8.cloned.1.call-start = ((), (), s32[]{:S(2)}) async-start(), calls=%async_computation.5 | async-start | bytes 13926400 | tf_op jit(solution)/shard_map/reduce_scatter | solution.py:301
  248.3 284.4 %reduce-scatter.10.cloned.1.call-start = ((), (), s32[]{:S(2)}) async-start(), calls=%async_computation.7 | async-start | bytes 6266880
  248.6 15.6 %slice-start = ((s8[6553600]{0:T(1024)(128)(4,1)}), s8[4194304]{0:T(1024)(128)(4,1)S(1)}, s32[]{:S(2)}) async-start(s8[6553600]{0:T(1024)(128)(4,1)} %bitcast.117), calls=%async_computation.8 | async-start | bytes 8388608
  248.6 15.6 %slice-start.4 = ((s8[5242880]{0:T(1024)(128)(4,1)}), s8[4194304]{0:T(1024)(128)(4,1)S(1)}, s32[]{:S(2)}) async-start(s8[5242880]{0:T(1024)(128)(4,1)} %bitcast.122), calls=%async_computation.12 | async-start | bytes 8388608
  263.9 11.3 %collective-permute-start.5 = (f32[512,1280]{1,0:T(8,128)}, f32[512,1280]{1,0:T(8,128)}, u32[]{:S(2)}, u32[]{:S(2)}) collective-permute-start(f32[512,1280]{1,0:T(8,128)} %slice.202), channel_id=1, source_target_pairs={{0,1},{1,0},{2,3},{3,2},{4,5},{5,4},{6,7},{7,6},{8,9},{9,8},{10,11... | collective-permute-start | bytes 7864328 | tf_op jit(solution)/shard_map/ppermute | solution.py:261
  274.4 5.3 collective-permute-start.3
  374.0 14.0 %collective-permute-start.6 = (f32[66,960]{0,1:T(8,128)S(1)}, f32[66,960]{0,1:T(8,128)S(1)}, u32[]{:S(2)}, u32[]{:S(2)}) collective-permute-start(f32[66,960]{0,1:T(8,128)S(1)} %get-tuple-element.53), channel_id=1, source_target_pairs={{0,32},{32,64},{64,96},{96,0},{1,33},{33,65},{65,97},{97,1},{2,34}... | collective-permute-start | bytes 760328 | tf_op jit(solution)/shard_map/ppermute | solution.py:282
  375.3 12.7 %collective-permute-start.8 = (f32[66,960]{0,1:T(8,128)S(1)}, f32[66,960]{0,1:T(8,128)S(1)}, u32[]{:S(2)}, u32[]{:S(2)}) collective-permute-start(f32[66,960]{0,1:T(8,128)S(1)} %get-tuple-element.54), channel_id=1, source_target_pairs={{0,96},{32,0},{64,32},{96,64},{1,97},{33,1},{65,33},{97,65},{2,98}... | collective-permute-start | bytes 760328 | tf_op jit(solution)/shard_map/ppermute | solution.py:282
  376.8 23.5 %copy-start.48 = (f32[1280]{0:T(1024)S(1)}, f32[1280]{0:T(1024)}, u32[]{:S(2)}) copy-start(f32[1280]{0:T(1024)} %copy-done.47) | copy-start | bytes 15364
  376.8 23.5 %copy-start.51 = (f32[1280]{0:T(1024)S(1)}, f32[1280]{0:T(1024)}, u32[]{:S(2)}) copy-start(f32[1280]{0:T(1024)} %copy-done.50) | copy-start | bytes 15364
  376.8 23.5 %copy-start.62 = (f32[66]{0:T(128)S(1)}, f32[66]{0:T(128)}, u32[]{:S(2)}) copy-start(f32[66]{0:T(128)} %copy-done.61) | copy-start | bytes 796
  376.8 23.5 %copy-start.64 = (f32[66]{0:T(128)S(1)}, f32[66]{0:T(128)}, u32[]{:S(2)}) copy-start(f32[66]{0:T(128)} %copy-done.63) | copy-start | bytes 796
  376.8 23.5 %copy-start.66 = (f32[66]{0:T(128)S(1)}, f32[66]{0:T(128)}, u32[]{:S(2)}) copy-start(f32[66]{0:T(128)} %copy-done.65) | copy-start | bytes 796
  376.8 22.6 %collective-permute-start.7 = (f32[66,960]{0,1:T(8,128)S(1)}, f32[66,960]{0,1:T(8,128)S(1)}, u32[]{:S(2)}, u32[]{:S(2)}) collective-permute-start(f32[66,960]{0,1:T(8,128)S(1)} %get-tuple-element.55), channel_id=1, source_target_pairs={{0,64},{32,96},{64,0},{96,32},{1,65},{33,97},{65,1},{97,33},{2,66}... | collective-permute-start | bytes 760328 | tf_op jit(solution)/shard_map/ppermute | solution.py:282
  383.1 17.2 %copy-start.10 = (f32[66,1280]{1,0:T(8,128)S(1)}, f32[66,1280]{1,0:T(8,128)}, u32[]{:S(2)}) copy-start(f32[66,1280]{1,0:T(8,128)} %copy-done.9) | copy-start | bytes 1013764
  431.0 10.6 %collective-permute-start.16 = (f32[16,40,2304]{2,1,0:T(8,128)S(1)}, f32[16,40,2304]{2,1,0:T(8,128)S(1)}, u32[]{:S(2)}, u32[]{:S(2)}) collective-permute-start(f32[16,40,2304]{2,1,0:T(8,128)S(1)} %dynamic-slice_bitcast_fusion), channel_id=1, source_target_pairs={{0,1},{1,0},{2,3},{3,2},{4,5},{5,4},{6,7},{7,6},{8,9},{9,8},{10,11... | collective-permute-start | bytes 17694728 | tf_op jit(solution)/shard_map/ppermute | solution.py:306
  465.7 1.6 collective-permute-start.9
  467.4 7.5 %collective-permute-start.10 = (f32[48,1280]{1,0:T(8,128)S(1)}, f32[48,1280]{1,0:T(8,128)S(1)}, u32[]{:S(2)}, u32[]{:S(2)}) collective-permute-start(f32[48,1280]{1,0:T(8,128)S(1)} %add.357), channel_id=1, source_target_pairs={{0,32},{32,0},{64,96},{96,64},{1,33},{33,1},{65,97},{97,65},{2,34}... | collective-permute-start | bytes 737288 | tf_op jit(solution)/shard_map/ppermute | solution.py:181
  468.3 46.3 %copy-start.42 = (f32[80,2560]{1,0:T(8,128)S(1)}, f32[80,2560]{1,0:T(8,128)}, u32[]{:S(2)}) copy-start(f32[80,2560]{1,0:T(8,128)} %reduce-scatter.6.cloned.1.call-done) | copy-start | bytes 2457604
  468.3 46.3 %collective-permute-start.19 = (f32[80,2560]{1,0:T(8,128)}, f32[80,2560]{1,0:T(8,128)}, u32[]{:S(2)}, u32[]{:S(2)}) collective-permute-start(f32[80,2560]{1,0:T(8,128)} %reduce-scatter.6.cloned.1.call-done), channel_id=1, source_target_pairs={{0,32},{32,0},{64,96},{96,64},{1,33},{33,1},{65,97},{97,65},{2,34}... | collective-permute-start | bytes 2457608 | tf_op jit(solution)/shard_map/ppermute | solution.py:181
  474.9 24.0 %collective-permute-start.11 = (f32[48,1280]{1,0:T(8,128)S(1)}, f32[48,1280]{1,0:T(8,128)S(1)}, u32[]{:S(2)}, u32[]{:S(2)}) collective-permute-start(f32[48,1280]{1,0:T(8,128)S(1)} %add.358), channel_id=1, source_target_pairs={{0,64},{32,96},{64,0},{96,32},{1,65},{33,97},{65,1},{97,33},{2,66}... | collective-permute-start | bytes 737288 | tf_op jit(solution)/shard_map/ppermute | solution.py:181
  499.0 6.4 %collective-permute-start.12 = (f32[48,1280]{1,0:T(8,128)S(1)}, f32[48,1280]{1,0:T(8,128)S(1)}, u32[]{:S(2)}, u32[]{:S(2)}) collective-permute-start(f32[48,1280]{1,0:T(8,128)S(1)} %add.359), channel_id=1, source_target_pairs={{0,2},{2,0},{4,6},{6,4},{1,3},{3,1},{5,7},{7,5},{8,10},{10,8},{12,... | collective-permute-start | bytes 737288 | tf_op jit(solution)/shard_map/ppermute | solution.py:181
  505.4 9.0 %collective-permute-start.13 = (f32[48,1280]{1,0:T(8,128)S(1)}, f32[48,1280]{1,0:T(8,128)S(1)}, u32[]{:S(2)}, u32[]{:S(2)}) collective-permute-start(f32[48,1280]{1,0:T(8,128)S(1)} %add.360), channel_id=1, source_target_pairs={{0,4},{2,6},{4,0},{6,2},{1,5},{3,7},{5,1},{7,3},{8,12},{10,14},{12... | collective-permute-start | bytes 737288 | tf_op jit(solution)/shard_map/ppermute | solution.py:181
  514.4 9.4 %collective-permute-start.14 = (f32[48,1280]{1,0:T(8,128)S(1)}, f32[48,1280]{1,0:T(8,128)S(1)}, u32[]{:S(2)}, u32[]{:S(2)}) collective-permute-start(f32[48,1280]{1,0:T(8,128)S(1)} %add.361), channel_id=1, source_target_pairs={{0,8},{8,0},{16,24},{24,16},{1,9},{9,1},{17,25},{25,17},{2,10},{10... | collective-permute-start | bytes 737288 | tf_op jit(solution)/shard_map/ppermute | solution.py:181
  514.5 20.2 %copy-start.41 = (f32[160,1280]{1,0:T(8,128)S(1)}, f32[160,1280]{1,0:T(8,128)}, u32[]{:S(2)}) copy-start(f32[160,1280]{1,0:T(8,128)} %reduce-scatter.8.cloned.1.call-done) | copy-start | bytes 2457604
  514.5 20.2 %collective-permute-start.22 = (f32[160,1280]{1,0:T(8,128)}, f32[160,1280]{1,0:T(8,128)}, u32[]{:S(2)}, u32[]{:S(2)}) collective-permute-start(f32[160,1280]{1,0:T(8,128)} %reduce-scatter.8.cloned.1.call-done), channel_id=1, source_target_pairs={{0,32},{32,0},{64,96},{96,64},{1,33},{33,1},{65,97},{97,65},{2,34}... | collective-permute-start | bytes 2457608 | tf_op jit(solution)/shard_map/ppermute | solution.py:181
  516.0 31.0 %collective-permute-start.20 = (f32[80,2560]{1,0:T(8,128)S(1)}, f32[80,2560]{1,0:T(8,128)}, u32[]{:S(2)}, u32[]{:S(2)}) collective-permute-start(f32[80,2560]{1,0:T(8,128)S(1)} %add.370), channel_id=1, source_target_pairs={{0,64},{32,96},{64,0},{96,32},{1,65},{33,97},{65,1},{97,33},{2,66}... | collective-permute-start | bytes 2457608 | tf_op jit(solution)/shard_map/ppermute | solution.py:181
  523.8 6.8 %collective-permute-start.15 = (f32[48,1280]{1,0:T(8,128)S(1)}, f32[48,1280]{1,0:T(8,128)S(1)}, u32[]{:S(2)}, u32[]{:S(2)}) collective-permute-start(f32[48,1280]{1,0:T(8,128)S(1)} %add.362), channel_id=1, source_target_pairs={{0,16},{8,24},{16,0},{24,8},{1,17},{9,25},{17,1},{25,9},{2,18},{10... | collective-permute-start | bytes 737288 | tf_op jit(solution)/shard_map/ppermute | solution.py:181
  534.6 25.4 %copy-start.40 = (f32[1,40,2304]{2,1,0:T(8,128)S(1)}, f32[1,40,2304]{2,1,0:T(8,128)}, u32[]{:S(2)}) copy-start(f32[1,40,2304]{2,1,0:T(8,128)} %reduce-scatter.10.cloned.1.call-done) | copy-start | bytes 1105924
  534.6 25.4 %collective-permute-start.17 = (f32[40,1280]{1,0:T(8,128)S(1)}, f32[40,1280]{1,0:T(8,128)S(1)}, u32[]{:S(2)}, u32[]{:S(2)}) collective-permute-start(f32[40,1280]{1,0:T(8,128)S(1)} %slice.215), channel_id=1, source_target_pairs={{0,32},{32,0},{64,96},{96,64},{1,33},{33,1},{65,97},{97,65},{2,34}... | collective-permute-start | bytes 614408 | tf_op jit(solution)/shard_map/ppermute | solution.py:181
  536.9 52.4 %collective-permute-start.23 = (f32[160,1280]{1,0:T(8,128)}, f32[160,1280]{1,0:T(8,128)}, u32[]{:S(2)}, u32[]{:S(2)}) collective-permute-start(f32[160,1280]{1,0:T(8,128)} %add.376), channel_id=1, source_target_pairs={{0,64},{32,96},{64,0},{96,32},{1,65},{33,97},{65,1},{97,33},{2,66}... | collective-permute-start | bytes 2457608 | tf_op jit(solution)/shard_map/ppermute | solution.py:181
  549.1 42.6 %collective-permute-start.21 = (f32[40,2560]{1,0:T(8,128)}, f32[40,2560]{1,0:T(8,128)}, u32[]{:S(2)}, u32[]{:S(2)}) collective-permute-start(f32[40,2560]{1,0:T(8,128)} %constant_dynamic-slice_fusion.1), channel_id=1, source_target_pairs={{0,1},{1,0},{2,3},{3,2},{4,5},{5,4},{6,7},{7,6},{8,9},{9,8},{10,11... | collective-permute-start | bytes 1228808 | tf_op jit(solution)/shard_map/ppermute | solution.py:312
  560.1 28.6 %collective-permute-start.18 = (f32[40,1280]{1,0:T(8,128)S(1)}, f32[40,1280]{1,0:T(8,128)S(1)}, u32[]{:S(2)}, u32[]{:S(2)}) collective-permute-start(f32[40,1280]{1,0:T(8,128)S(1)} %slice_add_fusion.2), channel_id=1, source_target_pairs={{0,64},{32,96},{64,0},{96,32},{1,65},{33,97},{65,1},{97,33},{2,66}... | collective-permute-start | bytes 614408 | tf_op jit(solution)/shard_map/ppermute | solution.py:181
  (61 other events, 273.2 us)
Sparse Core Ops, SparseCore 0:
  10.8 47.9 all-gather.6
  61.5 99.4 all-gather.8
  228.8 93.8 reduce-scatter.5
  325.9 94.5 reduce-scatter.7
  445.3 79.2 reduce-scatter.9

commit v2 on v1

v2 whole, which is shorter than its diff:
```python
import functools

import jax
import jax.numpy as jnp
from jax import lax
from jax.experimental import pallas as pl
from jax.experimental.pallas import tpu as pltpu
from jax.sharding import Mesh, PartitionSpec as P

MASK_ID = 32
VOCAB = 33
LN_EPS = 1e-5
ROPE_BASE = 10000.0
TRAIN_RATIO = 0.15 * 0.8
NEG_BIG = -1e30
SEQ = 1024
QLEN = 256
HEADS = 20
HDIM = 64
PAIRS = HEADS // 2
DIM = HEADS * HDIM
ROWS = 40
F32 = jnp.float32
BF16 = jnp.bfloat16
SWAP = [(0, 1), (1, 0)]
CHIP = ('z', 'y')
FSDP = ('z', 'y', 'c')
QCOLS = 1024
MESH = pl.DeviceIdType.MESH
LO, HI, ALL = range(3)
NT = ((1,), (1,))
TN = ((0,), (0,))
LANES = 128
HALF = HDIM // 2
FFH = 2 * DIM
TOK = 2 * QLEN
HALF_D = DIM // 2
COST = pl.CostEstimate(flops=20_000_000_000, bytes_accessed=15_000_000, transcendentals=10_000_000)
HIGH = lax.Precision.HIGHEST


def mm(a, b, dims=((1,), (0,))):
    return lax.dot_general(a, b, (dims, ((), ())), preferred_element_type=F32)


def ln_stats(z_in):
    row_mean = jnp.mean(z_in, axis=-1, keepdims=True)
    centered = z_in - row_mean
    row_var = jnp.mean(centered * centered, axis=-1, keepdims=True)
    inv = lax.rsqrt(row_var + LN_EPS)
    return centered * inv, inv


def ln_back(d_out, gain, xhat, inv):
    d_hat = d_out * gain
    m1 = jnp.mean(d_hat, axis=-1, keepdims=True)
    m2 = jnp.mean(d_hat * xhat, axis=-1, keepdims=True)
    return inv * (d_hat - m1 - xhat * m2)


def rot_half(z_in, sign):
    lane = lax.broadcasted_iota(jnp.int32, z_in.shape, 1)
    down, up = pltpu.roll(z_in, LANES - HALF, 1), pltpu.roll(z_in, HALF, 1)
    return jnp.where(lane % HDIM < HALF, -sign * down, sign * up)


def split3(z_in):
    hi = z_in.astype(BF16).astype(F32)
    rest = z_in - hi
    mid = rest.astype(BF16).astype(F32)
    return jnp.concatenate([hi, mid, rest - mid, jnp.zeros((LANES - 3 * ROWS, z_in.shape[1]), F32)], axis=0).astype(BF16)


def expand_qkv(ohk_ref, ohq_ref, tq_ref, tk_ref, tv_ref, csk_ref, csq_ref):
    ohk = ohk_ref[0]
    t_q = tq_ref[0] * HDIM ** -0.5
    z_q = mm(ohq_ref[0], split3(jnp.concatenate([t_q, rot_half(t_q, 1.0)], axis=1)))
    q = z_q[:, :LANES] * csq_ref[:, :LANES] + z_q[:, LANES:] * csq_ref[:, LANES:]
    t_k = tk_ref[0]
    z_k = mm(ohk, split3(jnp.concatenate([t_k, rot_half(t_k, 1.0)], axis=1)))
    k = z_k[:, :LANES] * csk_ref[:, :LANES] + z_k[:, LANES:] * csk_ref[:, LANES:]
    t_v = jnp.concatenate([tv_ref[0], jnp.zeros((LANES - ROWS, LANES), F32)], axis=0)
    v = mm(ohk, t_v.astype(BF16))
    return q, k.astype(BF16), v.astype(BF16)


def attn_fwd_kernel(len_ref, ohk_ref, ohq_ref, tq_ref, tk_ref, tv_ref, csk_ref, csq_ref, o_ref, lse_ref):
    seq_len = len_ref[pl.program_id(0)]
    q, k, v = expand_qkv(ohk_ref, ohq_ref, tq_ref, tk_ref, tv_ref, csk_ref, csq_ref)
    low = lax.broadcasted_iota(jnp.int32, (QLEN, LANES), 1) < HDIM
    key_ok = lax.broadcasted_iota(jnp.int32, (QLEN, SEQ), 1) < seq_len
    outs, stats = [], []
    for head in range(2):
        q_h = jnp.where(low if head == 0 else jnp.logical_not(low), q, 0.0).astype(BF16)
        s = jnp.where(key_ok, mm(q_h, k, NT), NEG_BIG)
        top = jnp.max(s, axis=-1, keepdims=True)
        e = jnp.exp(s - top)
        total = jnp.sum(e, axis=-1, keepdims=True)
        outs.append(mm(e.astype(BF16), v) / total)
        stats.append(jnp.broadcast_to(top + jnp.log(total), (QLEN, LANES)))
    o_ref[0] = jnp.where(low, outs[0], outs[1]).astype(BF16)
    lse_ref[0] = jnp.where(low, stats[0], stats[1])


def attn_bwd_kernel(len_ref, ohk_ref, ohq_ref, tq_ref, tk_ref, tv_ref, csk_ref, csq_ref, do_ref, lse_ref, sq_ref, sk_ref, sv_ref):
    seq_len = len_ref[pl.program_id(0)]
    q, k, v = expand_qkv(ohk_ref, ohq_ref, tq_ref, tk_ref, tv_ref, csk_ref, csq_ref)
    d_o = do_ref[0]
    low = lax.broadcasted_iota(jnp.int32, (QLEN, LANES), 1) < HDIM
    key_ok = lax.broadcasted_iota(jnp.int32, (QLEN, SEQ), 1) < seq_len
    dv, dk, dqs = None, None, []
    for head in range(2):
        mine = low if head == 0 else jnp.logical_not(low)
        q_h = jnp.where(mine, q, 0.0).astype(BF16)
        do_h = jnp.where(mine, d_o, jnp.zeros_like(d_o))
        s = mm(q_h, k, NT)
        p = jnp.where(key_ok, jnp.exp(s - lse_ref[0, :, HDIM * head:HDIM * head + 1]), 0.0)
        t = p * mm(do_h, v, NT)
        ds = (t - p * jnp.sum(t, axis=-1, keepdims=True)).astype(BF16)
        dv_h = mm(p.astype(BF16), do_h, TN)
        dk_h = mm(ds, q_h, TN)
        dv = dv_h if dv is None else dv + dv_h
        dk = dk_h if dk is None else dk + dk_h
        dqs.append(mm(ds, k))
    dq = jnp.where(low, dqs[0], dqs[1])
    ohk = ohk_ref[0]
    ohq = ohq_ref[0]
    top = TN
    real = lax.broadcasted_iota(jnp.int32, (ROWS, LANES), 0) < VOCAB

    def by_token(onehot, d_in):
        return jnp.where(real, mm(onehot, d_in.astype(BF16), top)[:ROWS], 0.0)
    s_q = by_token(ohq, dq * csq_ref[:, :LANES]) + rot_half(by_token(ohq, dq * csq_ref[:, LANES:]), -1.0)
    sq_ref[0] = s_q * HDIM ** -0.5
    sk_ref[0] = by_token(ohk, dk * csk_ref[:, :LANES]) + rot_half(by_token(ohk, dk * csk_ref[:, LANES:]), -1.0)
    sv_ref[0] = by_token(ohk, dv)


def tab_spec():
    return pl.BlockSpec((1, ROWS, LANES), lambda b, j: (b, 0, j))


def attn_specs():
    return [
        pl.BlockSpec(memory_space=pltpu.SMEM),
        pl.BlockSpec((1, SEQ, LANES), lambda b, j: (b, 0, 0)),
        pl.BlockSpec((1, QLEN, LANES), lambda b, j: (b, 0, 0)),
        tab_spec(),
        tab_spec(),
        tab_spec(),
        pl.BlockSpec((SEQ, 256), lambda b, j: (0, 0)),
        pl.BlockSpec((QLEN, 256), lambda b, j: (0, 0)),
    ]


def row_spec():
    return pl.BlockSpec((1, QLEN, LANES), lambda b, j: (b, 0, j))


def attn_fwd(lengths, ohk, ohq, tq, tk, tv, csk, csq):
    return pl.pallas_call(
        attn_fwd_kernel, grid=(2, PAIRS), in_specs=attn_specs(), out_specs=[row_spec(), row_spec()],
        out_shape=[jax.ShapeDtypeStruct((2, QLEN, DIM), BF16), jax.ShapeDtypeStruct((2, QLEN, DIM), F32)],
        cost_estimate=COST,
        name='attn_fwd')(lengths, ohk, ohq, tq, tk, tv, csk, csq)


def attn_bwd(lengths, ohk, ohq, tq, tk, tv, csk, csq, d_o, lse):
    return pl.pallas_call(
        attn_bwd_kernel, grid=(2, PAIRS), in_specs=attn_specs() + [row_spec(), row_spec()],
        out_specs=[tab_spec()] * 3, out_shape=[jax.ShapeDtypeStruct((2, ROWS, DIM), F32)] * 3,
        cost_estimate=COST,
        name='attn_bwd')(lengths, ohk, ohq, tq, tk, tv, csk, csq, d_o, lse)


class Ring:
    def __init__(self, axis, ports):
        self.me = lax.axis_index(axis)
        self.axis, self.ports = axis, ports
        self.right = lax.rem(self.me + 1, 4)
        self.left = lax.rem(self.me + 3, 4)
        self.far = lax.rem(self.me + 2, 4)
        self.open = []

    def send(self, src, dst, to):
        copy = remote(src, dst, next(self.ports), {self.axis: to})
        copy.start()
        self.open.append(copy)
        return copy

    def drain(self):
        for copy in self.open:
            copy.wait_send()
        self.open = []

    def rs_start(self, chunk, bufs):
        self.chunk = chunk
        self.b1, self.b2, self.b3, self.b4, self.b5, self.b6 = bufs
        self.m1 = self.send(chunk(self.far, LO), self.b1, self.right)
        self.m3 = self.send(chunk(self.far, HI), self.b3, self.left)
        self.m2 = self.send(chunk(self.right, HI), self.b2, self.right)
        self.m4 = self.send(chunk(self.left, LO), self.b4, self.left)

    def rs_mid(self):
        self.m1.wait_recv()
        self.b1[...] += self.chunk(self.right, LO)[...]
        self.m5 = self.send(self.b1, self.b5, self.right)
        self.m3.wait_recv()
        self.b3[...] += self.chunk(self.left, HI)[...]
        self.m6 = self.send(self.b3, self.b6, self.left)

    def rs_end(self):
        self.m4.wait_recv()
        self.m5.wait_recv()
        low = self.chunk(self.me, LO)[...] + self.b4[...] + self.b5[...]
        self.m2.wait_recv()
        self.m6.wait_recv()
        high = self.chunk(self.me, HI)[...] + self.b2[...] + self.b6[...]
        self.drain()
        return low, high

    def ag_start(self, slot):
        self.slot = slot
        self.a1 = self.send(slot(self.me, ALL), slot(self.me, ALL), self.right)
        self.a2 = self.send(slot(self.me, ALL), slot(self.me, ALL), self.left)

    def ag_mid(self):
        self.a1.wait_recv()
        self.a3 = self.send(self.slot(self.left, LO), self.slot(self.left, LO), self.right)
        self.a2.wait_recv()
        self.a4 = self.send(self.slot(self.right, HI), self.slot(self.right, HI), self.left)

    def ag_end(self):
        self.a3.wait_recv()
        self.a4.wait_recv()
        self.drain()


def meet():
    barrier = pltpu.get_barrier_semaphore()
    for axis in ('x', 'z', 'y'):
        me = lax.axis_index(axis)
        for step in (1, 3):
            pl.semaphore_signal(barrier, inc=1, device_id={axis: lax.rem(me + step, 4)}, device_id_type=MESH)
    pl.semaphore_signal(barrier, inc=1, device_id={'c': 1 - lax.axis_index('c')}, device_id_type=MESH)
    pl.semaphore_wait(barrier, 7)


def ports_of(sends, recvs):
    return ((sends.at[i], recvs.at[i]) for i in range(sends.shape[0]))


def remote(src, dst, port, target):
    return pltpu.make_async_remote_copy(src_ref=src, dst_ref=dst, send_sem=port[0], recv_sem=port[-1], device_id=target, device_id_type=MESH)


def core_copy(src, dst, ports):
    return remote(src, dst, next(ports), {'c': 1 - lax.axis_index('c')})


CUT = 24
HALF_W = 1152
WIDE = DIM + QCOLS


def half_rows(half):
    return pl.ds(0, CUT) if half == LO else pl.ds(CUT, ROWS - CUT)


def ring_bufs(lead, width):
    return [pltpu.VMEM(lead + (CUT if i in (0, 3, 4) else ROWS - CUT, width), F32) for i in range(6)]


def oq_kernel(d_out_ref, d_qkv_ref, out_ref, qkv_ref, acc, one_a, one_b, gath, *rest):
    bufs, ports = [rest[6 * i:6 * i + 6] for i in range(4)], ports_of(*rest[-2:])
    ci = lax.axis_index('c')
    meet()
    first = core_copy(d_out_ref.at[:, 1 - ci], acc.at[:, :, pl.ds(0, DIM)], ports)
    second = core_copy(d_qkv_ref.at[:, 1 - ci], acc.at[:, :, pl.ds(DIM, QCOLS)], ports)
    first.start()
    second.start()
    first.wait_recv()

    def add_out(i, carry):
        acc[i, :, :DIM] += d_out_ref[i, ci]
        return carry
    lax.fori_loop(0, 16, add_out, 0)
    second.wait_recv()

    def add_qkv(i, carry):
        acc[i, :, DIM:] += d_qkv_ref[i, ci]
        return carry
    lax.fori_loop(0, 16, add_qkv, 0)
    grid = acc.reshape(4, 4, ROWS, WIDE)
    ya = Ring('y', ports)
    zb = Ring('z', ports)
    ya.rs_start(lambda k, h: grid.at[:, k, half_rows(h), pl.ds(0, HALF_W)], bufs[0])
    zb.rs_start(lambda k, h: grid.at[k, :, half_rows(h), pl.ds(HALF_W, HALF_W)], bufs[1])
    ya.rs_mid()
    zb.rs_mid()
    one_a[:, :CUT], one_a[:, CUT:] = ya.rs_end()
    za = Ring('z', ports)
    za.rs_start(lambda k, h: one_a.at[k, half_rows(h)], bufs[2])
    one_b[:, :CUT], one_b[:, CUT:] = zb.rs_end()
    yb = Ring('y', ports)
    yb.rs_start(lambda k, h: one_b.at[k, half_rows(h)], bufs[3])
    za.rs_mid()
    yb.rs_mid()
    xr = Ring('x', ports)
    low, high = za.rs_end()
    gath[xr.me, :CUT, :HALF_W] = low
    gath[xr.me, CUT:, :HALF_W] = high
    low, high = yb.rs_end()
    gath[xr.me, :CUT, HALF_W:] = low
    gath[xr.me, CUT:, HALF_W:] = high
    xr.ag_start(lambda k, h: gath.at[k] if h == ALL else gath.at[k, half_rows(h)])
    xr.ag_mid()
    xr.ag_end()
    out_ref[...] = (gath[0, :, :DIM] + gath[1, :, :DIM]) + (gath[2, :, :DIM] + gath[3, :, :DIM])
    for k in range(4):
        qkv_ref[:, QCOLS * k:QCOLS * (k + 1)] = gath[k, :, DIM:]
    first.wait_send()
    second.wait_send()


def vmem(n):
    return [pl.BlockSpec(memory_space=pltpu.VMEM)] * n


def reduce_oq(d_out, d_qkv):
    return pl.pallas_call(
        oq_kernel, in_specs=vmem(2), out_specs=vmem(2),
        out_shape=[jax.ShapeDtypeStruct((ROWS, DIM), F32), jax.ShapeDtypeStruct((ROWS, 4 * QCOLS), F32)],
        scratch_shapes=[pltpu.VMEM((16, ROWS, WIDE), F32), pltpu.VMEM((4, ROWS, HALF_W), F32), pltpu.VMEM((4, ROWS, HALF_W), F32),
                        pltpu.VMEM((4, ROWS, WIDE), F32)]
        + ring_bufs((4,), HALF_W) + ring_bufs((4,), HALF_W) + ring_bufs((), HALF_W) + ring_bufs((), HALF_W)
        + [pltpu.SemaphoreType.DMA((30,)), pltpu.SemaphoreType.DMA((30,))],
        compiler_params=pltpu.CompilerParams(collective_id=1, has_side_effects=True, vmem_limit_bytes=56 * 1024 * 1024),
        cost_estimate=COST,
        name='reduce_oq')(d_out, d_qkv)


SMALL = 48
UP_R = 80


def last_kernel(up_ref, down_ref, small_ref, up_out, down_out, small_out, pair, sum_y, sum_z, sum_x, *rest):
    bufs, ports = [rest[6 * i:6 * i + 6] for i in range(2)], ports_of(*rest[-2:])
    ci = lax.axis_index('c')
    meet()

    def up_rows(half):
        return pl.ds(40 * half, 40)
    swap = core_copy(small_ref, pair, ports)
    swap.start()
    xu = Ring('x', ports)
    xd = Ring('x', ports)
    xu.rs_start(lambda k, h: up_ref.at[k, up_rows(h)], bufs[0])
    xd.rs_start(lambda k, h: down_ref.at[k, half_rows(h)], bufs[1])
    swap.wait_recv()
    both = small_ref[...] + pair[...]
    mine = jnp.where(ci == 0, both[:, 0:HALF_D], both[:, HALF_D:1280])

    def gather(ref):
        return lambda k, h: ref.at[k] if h == ALL else ref.at[k, pl.ds(24 * h, 24)]

    def total(ref):
        return (ref[0] + ref[1]) + (ref[2] + ref[3])
    ys = Ring('y', ports)
    sum_y[ys.me] = mine
    ys.ag_start(gather(sum_y))
    xu.rs_mid()
    xd.rs_mid()
    ys.ag_mid()
    ys.ag_end()
    zs = Ring('z', ports)
    sum_z[zs.me] = total(sum_y)
    zs.ag_start(gather(sum_z))
    low, high = xu.rs_end()
    up_out[xu.me, 0:40] = low
    up_out[xu.me, 40:80] = high
    gu = Ring('x', ports)
    gu.ag_start(lambda k, h: up_out.at[k] if h == ALL else up_out.at[k, up_rows(h)])
    low, high = xd.rs_end()
    down_out[xd.me, :CUT] = low
    down_out[xd.me, CUT:] = high
    gd = Ring('x', ports)
    gd.ag_start(lambda k, h: down_out.at[k] if h == ALL else down_out.at[k, half_rows(h)])
    zs.ag_mid()
    zs.ag_end()
    xs = Ring('x', ports)
    sum_x[xs.me] = total(sum_z)
    xs.ag_start(gather(sum_x))
    gu.ag_mid()
    gd.ag_mid()
    xs.ag_mid()
    xs.ag_end()
    small_out[ci] = total(sum_x)
    back = core_copy(small_out.at[ci], small_out.at[ci], ports)
    back.start()
    gu.ag_end()
    gd.ag_end()
    back.wait_recv()
    back.wait_send()
    swap.wait_send()


def reduce_last(up, down, small):
    up_bufs = [pltpu.VMEM((40, HALF_D), F32) for _ in range(6)]
    return pl.pallas_call(
        last_kernel, in_specs=vmem(3), out_specs=vmem(3),
        out_shape=[jax.ShapeDtypeStruct((4, UP_R, HALF_D), F32), jax.ShapeDtypeStruct((4, ROWS, DIM), F32), jax.ShapeDtypeStruct((2, SMALL, HALF_D), F32)],
        scratch_shapes=[pltpu.VMEM((SMALL, DIM), F32)] + [pltpu.VMEM((4, SMALL, HALF_D), F32)] * 3 + up_bufs + ring_bufs((), DIM)
        + [pltpu.SemaphoreType.DMA((34,)), pltpu.SemaphoreType.DMA((34,))],
        compiler_params=pltpu.CompilerParams(collective_id=2, has_side_effects=True, vmem_limit_bytes=40 * 1024 * 1024),
        name='reduce_last')(up, down, small)


def one_hot3(tok):
    lanes = jnp.arange(LANES)
    return ((tok[..., None] == lanes % ROWS) & (lanes < 3 * ROWS)).astype(BF16)


def solution(mesh):
    mesh4 = Mesh(mesh.devices.reshape(4, 4, 4, 2), ('x', 'z', 'y', 'c'))

    def local_step(tokens, lengths, embed_table, layer_vecs, w_qkv, w_out, w_up, b_up, w_down, grad_out):
        xi = lax.axis_index('x')
        ci = lax.axis_index('c')
        chip = lax.axis_index('z') * 4 + lax.axis_index('y')
        fi = chip * 2 + ci
        wq_loc = lax.dynamic_slice_in_dim(jnp.pad(w_qkv.reshape(ROWS, 3 * DIM), ((0, 0), (0, 256))), QCOLS * xi, QCOLS, axis=1)
        qkv_w = lax.all_gather(wq_loc, FSDP, axis=0, tiled=True)
        packed = jnp.concatenate([layer_vecs.reshape(360), b_up, jnp.zeros((504,), F32)]).reshape(8, LANES)
        packed = lax.all_gather(packed, FSDP, axis=0, tiled=True).reshape(32, 1024)
        vecs = packed[:, :360].reshape(32, 9, ROWS).transpose(1, 0, 2).reshape(9, DIM)
        up_b = lax.dynamic_index_in_dim(packed[:, 360:520].reshape(16, 2, 160), ci, axis=1, keepdims=False).reshape(FFH)
        tok_all = lax.all_gather(tokens, 'x', axis=1, tiled=True)
        up_loc = w_up.reshape(ROWS, 16, 2, 160)
        up_mine = lax.dynamic_index_in_dim(up_loc, ci, axis=2, keepdims=False).reshape(ROWS, FFH)
        up_send = lax.dynamic_index_in_dim(up_loc, 1 - ci, axis=2, keepdims=False).reshape(ROWS, FFH)
        up_recv = lax.ppermute(up_send, 'c', SWAP)
        up_pair = jnp.concatenate([jnp.where(ci == 0, up_mine, up_recv), jnp.where(ci == 0, up_recv, up_mine)], axis=0)
        shard = jnp.concatenate([up_pair[:, :DIM], up_pair[:, DIM:], w_down, w_out], axis=0)
        gathered = lax.all_gather(shard, CHIP, axis=0, tiled=False)
        grad_own = grad_out.reshape(TOK, DIM)
        grad2 = jnp.concatenate([grad_own, lax.ppermute(grad_own, 'c', SWAP)], axis=0)

        positions = jnp.arange(SEQ)
        tok_eff = jnp.where(positions[None, :] < lengths[:, None], tok_all, MASK_ID)
        tok_own = lax.dynamic_slice_in_dim(tok_eff, xi * QLEN, QLEN, axis=1)
        mask_count = jnp.sum((tok_all == MASK_ID).astype(F32), axis=1)
        drop_scale = (1.0 - TRAIN_RATIO) / (1.0 - mask_count / lengths.astype(F32))
        ohk = one_hot3(tok_eff)
        ohq = one_hot3(tok_own)
        oh_own = ohq[:, :, :VOCAB]
        row_scale = jnp.where(jnp.arange(VOCAB)[None, :] == MASK_ID, 0.0, drop_scale[:, None])
        e_rows = embed_table.astype(F32)[None] * row_scale[:, :, None]
        xhat1, inv1 = ln_stats(e_rows)
        h_rows = (xhat1 * vecs[0] + vecs[1]).astype(BF16)
        h_rows = jnp.pad(h_rows, ((0, 0), (0, ROWS - VOCAB), (0, 0))).reshape(2 * ROWS, DIM)
        t_loc = mm(h_rows, qkv_w)
        t_all = jnp.zeros((2 * ROWS, 4 * QCOLS), F32)
        for hop in range(4):
            part = lax.ppermute(t_loc, 'x', [(i, (i + hop) % 4) for i in range(4)]) if hop else t_loc
            t_all = lax.dynamic_update_slice_in_dim(t_all, part, QCOLS * ((xi + 4 - hop) % 4), axis=1)
        t_all = (t_all[:, :3 * DIM] + vecs[2:5].reshape(1, 3 * DIM)).reshape(2, ROWS, 3 * DIM)
        tabs = (t_all[:, :, :DIM], t_all[:, :, DIM:2 * DIM], t_all[:, :, 2 * DIM:])
        inv_freq = 1.0 / (ROPE_BASE ** (jnp.arange(0, HDIM, 2, dtype=F32) / HDIM))
        angles = positions.astype(F32)[:, None] * inv_freq[None, :]
        csk = jnp.concatenate([jnp.tile(jnp.cos(angles), (1, 4)), jnp.tile(jnp.sin(angles), (1, 4))], axis=1)
        csq = lax.dynamic_slice_in_dim(csk, xi * QLEN, QLEN, axis=0)

        attn_o, lse = attn_fwd(lengths, ohk, ohq, *tabs, csk, csq)
        attn_o, gathered = lax.optimization_barrier((attn_o, gathered))
        up_w0 = gathered[:, 0:80].reshape(DIM, DIM)
        up_w1 = gathered[:, 80:160].reshape(DIM, DIM)
        down_w = gathered[:, 160:320].reshape(2 * DIM, DIM)
        out_mine = gathered[:, 320:360]
        out_recv = lax.ppermute(out_mine, 'c', SWAP)
        out_w = jnp.stack([jnp.where(ci == 0, out_mine, out_recv), jnp.where(ci == 0, out_recv, out_mine)], axis=1).reshape(DIM, DIM)
        attn_o2 = attn_o.reshape(TOK, DIM)
        keep_own = jnp.where(tok_own == MASK_ID, 0.0, drop_scale[:, None])
        embedded = jnp.einsum('bsv,vd->bsd', oh_own, embed_table, preferred_element_type=F32) * keep_own[:, :, None]
        x1 = embedded.reshape(TOK, DIM) + mm(attn_o2, out_w) + vecs[5]
        xhat2, inv2 = ln_stats(x1)
        nm = (xhat2 * vecs[6] + vecs[7]).astype(BF16)
        nm2 = jnp.concatenate([nm, lax.ppermute(nm, 'c', SWAP)], axis=0)
        up_lin = jnp.concatenate([mm(nm2, up_w0), mm(nm2, up_w1)], axis=1) + up_b
        cdf = 0.5 * (1.0 + lax.erf(up_lin * 0.7071067811865476))
        gelu_b = (up_lin * cdf).astype(BF16)
        slope = cdf + up_lin * (0.3989422804014327 * jnp.exp(-0.5 * up_lin * up_lin))
        down2 = mm(gelu_b, down_w)
        down_got = lax.ppermute(down2[TOK:], 'c', SWAP)
        layer_out = (x1 + down2[:TOK] + down_got + vecs[8]).astype(BF16).reshape(2, QLEN, DIM)

        d_down = mm(gelu_b, grad2, TN)
        d_up_lin = mm(grad2, down_w, NT) * slope
        d_up_b = d_up_lin.astype(BF16)
        d_up = mm(nm2, d_up_b, TN)
        d_nm2 = mm(d_up_b[:, :DIM], up_w0, NT) + mm(d_up_b[:, DIM:], up_w1, NT)
        d_nm = d_nm2[:TOK] + lax.ppermute(d_nm2[TOK:], 'c', SWAP)
        grad32 = grad_own.astype(F32)
        d_resid = grad32 + ln_back(d_nm, vecs[6], xhat2, inv2)
        d_resid_b = d_resid.astype(BF16)
        d_outw = mm(attn_o2, d_resid_b, TN)
        d_attn_b = mm(d_resid_b, out_w, NT).astype(BF16)
        s_q, s_k, s_v = attn_bwd(lengths, ohk, ohq, *tabs, csk, csq, d_attn_b.reshape(2, QLEN, DIM), lse)

        d_bqkv = jnp.stack([jnp.sum(part, axis=(0, 1)) for part in (s_q, s_k, s_v)])
        s_all = jnp.concatenate([s_q, s_k, s_v, jnp.zeros((2, ROWS, 256), F32)], axis=2).reshape(2 * ROWS, 4 * QCOLS)
        s_mine = lax.dynamic_slice_in_dim(s_all, QCOLS * xi, QCOLS, axis=1)
        for hop in range(1, 4):
            part = lax.dynamic_slice_in_dim(s_all, QCOLS * ((xi + hop) % 4), QCOLS, axis=1)
            s_mine = s_mine + lax.ppermute(part, 'x', [(i, (i + hop) % 4) for i in range(4)])
        d_qkvw = lax.dot_general(h_rows.astype(F32), s_mine, (TN, ((), ())), precision=HIGH)
        d_h = lax.dot_general(s_mine, qkv_w.astype(F32), (NT, ((), ())), precision=HIGH)
        d_h = d_h.reshape(2, ROWS, DIM)[:, :VOCAB]
        d_e = ln_back(d_h, vecs[0], xhat1, inv1)
        d_e = d_e + jnp.einsum('bsv,bsd->bvd', oh_own, d_resid_b.reshape(2, QLEN, DIM), preferred_element_type=F32)
        d_table = jnp.sum(d_e * row_scale[:, :, None], axis=0)
        d_up_bias = jnp.sum(d_up_lin, axis=0).reshape(1, 2, DIM)
        d_up_bias = jnp.where(jnp.arange(2)[:, None, None] == ci, d_up_bias, 0.0).reshape(4, DIM)
        small = jnp.concatenate([
            d_table,
            jnp.sum(d_h * xhat1, axis=(0, 1))[None], jnp.sum(d_h, axis=(0, 1))[None], d_bqkv,
            jnp.sum(d_resid, axis=0)[None], jnp.sum(d_nm * xhat2, axis=0)[None], jnp.sum(d_nm, axis=0)[None],
            jnp.sum(grad32, axis=0)[None], d_up_bias, jnp.zeros((2, DIM), F32)], axis=0)
        r_out, r_qkv = reduce_oq(d_outw.reshape(16, 2, ROWS, DIM), d_qkvw.reshape(16, 2, ROWS, QCOLS))
        r_down = lax.psum_scatter(d_down, CHIP, scatter_dimension=0, tiled=True)
        r_up = lax.psum_scatter(d_up, CHIP, scatter_dimension=0, tiled=True)
        small, r_out = lax.optimization_barrier((small, r_out))
        r_up, r_down, small = reduce_last(r_up.reshape(2 * ROWS, 4, HALF_D).transpose(1, 0, 2), r_down.reshape(4, ROWS, DIM), small)
        r_up = r_up.transpose(1, 0, 2).reshape(2 * ROWS, FFH)
        r_down = r_down.reshape(160, DIM)
        small = small.transpose(1, 0, 2).reshape(SMALL, DIM)
        d_vecs = lax.dynamic_slice(small, (VOCAB, fi * ROWS), (9, ROWS))
        d_bup_half = lax.dynamic_slice_in_dim(small, VOCAB + 9 + 2 * ci, 2, axis=0).reshape(FFH)
        d_bup = lax.dynamic_slice_in_dim(d_bup_half, chip * 160, 160, axis=0)

        up_keep = lax.dynamic_slice_in_dim(r_up, ci * ROWS, ROWS, axis=0)
        up_give = lax.dynamic_slice_in_dim(r_up, (1 - ci) * ROWS, ROWS, axis=0)
        up_got = lax.ppermute(up_give, 'c', SWAP)
        r_up = jnp.stack([jnp.where(ci == 0, up_keep, up_got).reshape(ROWS, 16, 160),
                          jnp.where(ci == 0, up_got, up_keep).reshape(ROWS, 16, 160)], axis=2).reshape(ROWS, 5120)
        r_qkv = r_qkv[:, :3 * DIM].reshape(ROWS, 3, HEADS, HDIM)
        return layer_out, small[:VOCAB], d_vecs, r_qkv, r_out, r_up, d_bup, r_down

    in_specs = (P(FSDP, 'x'), P(FSDP), P(), P(None, FSDP), P(FSDP), P(FSDP), P(FSDP), P(FSDP), P(FSDP), P(FSDP, 'x'))
    out_specs = (P(FSDP, 'x'), P(), P(None, FSDP), P(FSDP), P(FSDP), P(FSDP), P(FSDP), P(FSDP))
    return jax.shard_map(local_step, mesh=mesh4, in_specs=in_specs, out_specs=out_specs, check_vma=False)
```

time: 616 us -> 537 us (0.87)
  Pallas kernels: 91.6 us -> 215 us
  local copies, waits for them, and re-layouts: 107 us -> 52.6 us
  waiting for transfers between devices: 115 us -> 65.6 us
  blocking collectives: 77.4 us -> 35.7 us
  other arithmetic: 67.1 us -> 33.1 us
  starting transfers between devices: 32.9 us -> 14 us
    pallas_call x0 -> x2, Pallas kernels: none -> 121 us  [the longest x1 82.8 us: reduce_oq(): pl.pallas_call(oq_kernel, in_specs=vmem(2), out_specs=vmem(2), out_shape=...]
    ppermute x16 -> x5, waiting for transfers between devices: 73.1 us -> 8.8 us  [the longest x3 8.79 us: local_step(): lax.ppermute(t_loc, 'x', [(i, (i + hop) % 4) for i in range(4)])]
    all_gather x2 -> x0, blocking collectives: 38.8 us -> none  [the longest x1 24.3 us: local_step(): r_qkv = lax.all_gather(r_oq[:, DIM:DIM + 960], 'x', axis=0, tiled=False)]
    all_gather x1, waiting for transfers between devices: 22.3 us -> 44.3 us  [local_step(): gathered = lax.all_gather(shard, CHIP, axis=0, tiled=False)]
    concatenate x9 -> x1, local copies, waits for them, and re-layouts: 20.8 us -> 0.01 us  [local_step(): jnp.concatenate([s_q, s_k, s_v, jnp.zeros((2, ROWS, 256), F32)], axis=2)]
    add x17 -> x1, other arithmetic: 15.8 us -> 0.09 us  [local_step(): t_all[:, :3 * DIM] + vecs[2:5].reshape(1, 3 * DIM)]
    transpose x5 -> x0, local copies, waits for them, and re-layouts: 11.1 us -> none  [the longest x1 3.54 us: local_step(): t_all.reshape(4, 2, VOCAB, 3, 5, HDIM).transpose(1, 2, 3, 0, 4, 5)]
    concatenate x4 -> x1, other arithmetic: 11.9 us -> 1.35 us  [local_step(): jnp.concatenate([s_q, s_k, s_v, jnp.zeros((2, ROWS, 256), F32)], axis=2)]
  transfers between devices with their start and end apart: 29 -> 17, of which waited for: 15 -> 8; matrix products, arithmetic and copies ran while one was open for 36% -> 24% of each run, Pallas kernels for 15% -> 34%
where the time goes in v2:
time: 537 us; the launch traced here: 527 us
  Pallas kernels  215 us (40%)
  matrix products  95.3 us (18%)
  waiting for transfers between devices  65.6 us (12%)
  local copies, waits for them, and re-layouts  52.6 us (10%)
  blocking collectives  35.7 us (7%)
  other arithmetic  33.1 us (6%)
  between operations  15.4 us (3%)
  starting transfers between devices  14 us (3%)
    dot_general x12, matrix products, mm(): return lax.dot_general(a, b, (dims, ((), ())), preferred_element_type=F32)  87.3 us
    pallas_call x1, Pallas kernels, reduce_oq(): pl.pallas_call(oq_kernel, in_specs=vmem(2), out_specs=vmem(2), out_shape=...  82.8 us
    pallas_call x1, Pallas kernels, attn_bwd(): pl.pallas_call(attn_bwd_kernel, grid=(2, PAIRS), in_specs=attn_specs() +...  60.3 us
    all_gather x1, waiting for transfers between devices, local_step(): gathered = lax.all_gather(shard, CHIP, axis=0, tiled=False)  44.3 us
    pallas_call x1, Pallas kernels, reduce_last(): pl.pallas_call(last_kernel, in_specs=vmem(3), out_specs=vmem(3), out_shap...  37.8 us
    pallas_call x1, Pallas kernels, attn_fwd(): pl.pallas_call(attn_fwd_kernel, grid=(2, PAIRS), in_specs=attn_specs(), o...  34.7 us
    all_gather x1, blocking collectives, local_step(): packed = lax.all_gather(packed, FSDP, axis=0, tiled=True).reshape(32, 1024)  26.3 us
    unnamed x96, local copies, waits for them, and re-layouts  12.4 us
  transfers between devices with their start and end apart: 17, of which 8 were waited for; matrix products, arithmetic and copies ran while one was open for 24% of the time, Pallas kernels for 34%

profile of v2, /device:TPU:1, one launch (start us, length us, event | category | flops | bytes accessed | tf_op | source)
XLA Modules:
  0.0 527.2 jit_solution(16930769336841997763)
XLA Ops:
  10.4 4.1 dynamic-slice_reduce_fusion.1
  14.9 1.4 collective-permute-start.3
  18.8 26.3 %all_gather.16 = f32[256,128]{1,0:T(8,128)S(1)} all-gather(f32[8,128]{1,0:T(8,128)S(1)} %maximum_bitcast_fusion), channel_id=1, replica_groups=mesh['x'=4,'z'=4,'y'=4,'c'=2] {'z','y','c'}, dimensions={0}, use_global_device_ids=true | all-gather | bytes 135168 | tf_op jit(solution)/shard_map/all_gather | solution.py:435
  45.9 9.3 %all_gather.15 = s32[2,1024]{1,0:T(2,128)S(1)} all-gather(s32[2,256]{1,0:T(2,128)S(1)} %copy-done.36), channel_id=1, replica_groups=mesh['x'=4,'z'=4,'y'=4,'c'=2] {'x'}, dimensions={1}, use_global_device_ids=true | all-gather | bytes 10240 | tf_op jit(solution)/shard_map/all_gather | solution.py:438
  58.8 3.1 constant_dynamic-update-slice_fusion.3
  61.9 1.5 collective-permute-start
  64.8 2.2 collective-permute-start.1
  71.2 6.6 %collective-permute-done.1 = f32[80,1024]{1,0:T(8,128)S(1)} collective-permute-done((f32[80,1024]{1,0:T(8,128)}, f32[80,1024]{1,0:T(8,128)S(1)}, u32[]{:S(2)}, u32[]{:S(2)}) %collective-permute-start.1) | collective-permute-done | bytes 327712 | tf_op jit(solution)/shard_map/ppermute | solution.py:465
  77.8 2.2 collective-permute-done.2
  81.2 34.7 %attn_fwd.1 = (bf16[2,256,1280]{2,1,0:T(8,128)(2,1)}, f32[2,256,1280]{2,1,0:T(8,128)}) custom-call(s32[2]{0:T(128)} %len_ref.3, bf16[2,1024,128]{2,1,0:T(8,128)(2,1)} %and_convert_fusion.ohk_ref, bf16[2,256,128]{2,1,0:T(8,128)(2,1)} %get-tuple-element.93.ohq_ref, f32[2,40,1280]{2,1,0:T(8,128)} %get-tuple-element.87.tq_ref, ...), custom_call_target="tpu_custom_call" | custom-call | flops 20000000000 | bytes 15000000 | tf_op jit(solution)/shard_map/attn_fwd/pallas_call | solution.py:161
  115.9 44.3 %all-gather.6.cloned.1.call-done = bf16[5760,1280]{1,0:T(8,128)(2,1)} async-done(((bf16[360,1280]{1,0:T(8,128)(2,1)}), bf16[5760,1280]{1,0:T(8,128)(2,1)}) %all-gather.6.cloned.1.call-update) | async-done | bytes 14745616 | tf_op jit(solution)/shard_map/all_gather | solution.py:445
  160.1 1.5 slice.110
  163.5 2.3 collective-permute-done.4
  165.8 2.1 select_bitcast_fusion.1
  169.4 2.0 fusion.55
  171.9 1.6 add_convert_fusion
  175.2 3.3 slice.117
  178.5 5.7 %fusion.52 = (bf16[16,80,1280]{2,1,0:T(8,128)(2,1)S(1)}, bf16[16,80,1280]{2,1,0:T(8,128)(2,1)S(1)}) fusion(bf16[16,360,1280]{2,1,0:T(8,128)(2,1)} %bitcast.94), kind=kLoop, calls=%fused_computation.142 | loop fusion | bytes 13107200 | tf_op jit(solution)/shard_map/slice | solution.py:476
  184.3 9.5 %fusion.21 = f32[1024,1280]{1,0:T(8,128)} fusion(bf16[1280,1280]{1,0:T(8,128)(2,1)S(1)} %bitcast.111, bf16[512,1280]{1,0:T(8,128)(2,1)} %collective-permute-done.5, bf16[512,1280]{1,0:T(8,128)(2,1)} %add_convert_fusion), kind=kOutput, calls=%fused_computation.54 | convolution fusion | flops 3360686080 | bytes 11141120 | tf_op jit(solution)/shard_map/dot_general | solution.py:43
  193.8 7.6 %fusion.22 = f32[1024,1280]{1,0:T(8,128)} fusion(bf16[1280,1280]{1,0:T(8,128)(2,1)S(1)} %bitcast.113, bf16[512,1280]{1,0:T(8,128)(2,1)} %collective-permute-done.5, bf16[512,1280]{1,0:T(8,128)(2,1)} %add_convert_fusion), kind=kOutput, calls=%fused_computation.55 | convolution fusion | flops 3360686080 | bytes 11141120 | tf_op jit(solution)/shard_map/dot_general | solution.py:43
  201.4 14.0 %fusion.53 = (f32[2560]{0:T(1024)S(1)}, bf16[1024,2560]{1,0:T(8,128)(2,1)}) fusion(f32[2560]{0:T(1024)S(1)} %add.264, f32[1024,1280]{1,0:T(8,128)} %fusion.21, f32[1024,1280]{1,0:T(8,128)} %fusion.22, bf16[2560,1280]{1,0:T(8,128)(2,1)S(1)} %bitcast.95, bf16[512,1280]{1,0:T(8,128)(2,1)} %collective-permute-done.7, bf16[512,1280]{1,0:T(8,128)(2,1)} %bitcast.18), kind=kOutput, calls=%fused_computation.143 | convolution fusion | flops 6750205440 | bytes 24924160 | tf_op jit(solution)/shard_map/dot_general | solution.py:43
  215.4 12.8 %fusion.20 = f32[1280,2560]{1,0:T(8,128)} fusion(bf16[1024,2560]{1,0:T(8,128)(2,1)} %get-tuple-element.78, bf16[512,1280]{1,0:T(8,128)(2,1)} %collective-permute-done.5, bf16[512,1280]{1,0:T(8,128)(2,1)} %add_convert_fusion), kind=kOutput, calls=%fused_computation.53 | convolution fusion | flops 6716129280 | bytes 20971520 | tf_op jit(solution)/shard_map/dot_general | solution.py:43
  228.3 5.7 %multiply_convert_fusion = bf16[1024,2560]{1,0:T(8,128)(2,1)S(1)} fusion(f32[1024,1280]{1,0:T(8,128)} %fusion.21, f32[1024,1280]{1,0:T(8,128)} %fusion.22, f32[2560]{0:T(1024)S(1)} %add.264), kind=kLoop, calls=%fused_computation.7 | loop fusion | flops 18350080 | bytes 15738880 | tf_op jit(solution)/shard_map/convert_element_type | solution.py:491
  234.0 2.3 copy-done.7
  236.3 11.8 %fusion.13 = f32[2560,1280]{1,0:T(8,128)} fusion(bf16[1024,2560]{1,0:T(8,128)(2,1)S(1)} %multiply_convert_fusion, bf16[512,1280]{1,0:T(8,128)(2,1)} %collective-permute-done.7, bf16[512,1280]{1,0:T(8,128)(2,1)} %bitcast.18), kind=kOutput, calls=%fused_computation.35 | convolution fusion | flops 6716129280 | bytes 20971520 | tf_op jit(solution)/shard_map/dot_general | solution.py:43
  248.1 6.4 %fusion.7 = f32[1024,1280]{1,0:T(8,128)S(1)} fusion(bf16[1280,1280]{1,0:T(8,128)(2,1)} %bitcast.114, bf16[1024,2560]{1,0:T(8,128)(2,1)} %get-tuple-element.78), kind=kOutput, calls=%fused_computation.17 | convolution fusion | flops 3355443200 | bytes 11141120 | tf_op jit(solution)/shard_map/dot_general | solution.py:43
  254.6 5.5 %convolution_add_fusion = f32[1024,1280]{1,0:T(8,128)S(1)} fusion(f32[1024,1280]{1,0:T(8,128)S(1)} %fusion.7, bf16[1280,1280]{1,0:T(8,128)(2,1)S(1)} %bitcast.112, bf16[1024,2560]{1,0:T(8,128)(2,1)} %get-tuple-element.78), kind=kOutput, calls=%fused_computation.9 | convolution fusion | flops 3356753920 | bytes 16384000 | tf_op jit(solution)/shard_map/dot_general | solution.py:43
  260.1 1.8 slice.150
  263.9 6.9 %fusion.56 = f32[1024,1280]{1,0:T(8,128)S(1)} fusion(bf16[1024,2560]{1,0:T(8,128)(2,1)S(1)} %bitcast.102, bf16[2560,1280]{1,0:T(8,128)(2,1)S(1)} %bitcast.98), kind=kOutput, calls=%fused_computation.146 | convolution fusion | flops 6710886400 | bytes 17039360 | tf_op jit(solution)/shard_map/dot_general | solution.py:43
  270.8 1.8 slice.145
  274.3 1.5 convert_reduce_fusion
  276.2 2.4 copy.37
  278.8 3.9 multiply_reduce_fusion
  282.8 4.2 fusion.51
  287.0 3.0 convolution_convert_fusion
  290.0 60.3 %attn_bwd.1 = (f32[2,40,1280]{2,1,0:T(8,128)}, f32[2,40,1280]{2,1,0:T(8,128)}, f32[2,40,1280]{2,1,0:T(8,128)}) custom-call(s32[2]{0:T(128)} %len_ref.3, bf16[2,1024,128]{2,1,0:T(8,128)(2,1)} %and_convert_fusion.ohk_ref, bf16[2,256,128]{2,1,0:T(8,128)(2,1)} %get-tuple-element.93.ohq_ref, f32[2,40,1280]{2,1,0:T(8,128)} %get-tuple-element.87.tq_ref, ...), custom_call_target="tpu_custom_call" | custom-call | flops 20000000000 | bytes 15000000 | tf_op jit(solution)/shard_map/attn_bwd/pallas_call | solution.py:169
  355.0 1.5 collective-permute-start.9
  356.6 1.5 collective-permute-start.11
  358.0 1.5 collective-permute-start.10
  359.5 4.6 fusion.14.d_out_ref
  365.6 7.9 %collective-permute-done.10 = f32[80,1024]{1,0:T(8,128)S(1)} collective-permute-done((f32[80,1024]{1,0:T(8,128)S(1)}, f32[80,1024]{1,0:T(8,128)S(1)}, u32[]{:S(2)}, u32[]{:S(2)}) %collective-permute-start.10) | collective-permute-done | bytes 327712 | tf_op jit(solution)/shard_map/ppermute | solution.py:515
  373.6 2.5 fusion.57
  377.1 4.6 fusion.36.d_qkv_ref
  381.7 82.8 %reduce_oq.1 = (f32[40,1280]{1,0:T(8,128)}, f32[40,4096]{1,0:T(8,128)}) custom-call(f32[16,2,40,1280]{3,2,1,0:T(8,128)} %fusion.14.d_out_ref, f32[16,2,40,1024]{3,2,1,0:T(8,128)} %fusion.36.d_qkv_ref), custom_call_target="tpu_custom_call" | custom-call | flops 20000000000 | bytes 15000000 | tf_op jit(solution)/shard_map/reduce_oq/pallas_call | solution.py:331
  466.9 37.8 %reduce_last.1 = (f32[4,80,640]{2,1,0:T(8,128)S(1)}, f32[4,40,1280]{2,1,0:T(8,128)S(1)}, f32[2,48,640]{2,1,0:T(8,128)S(1)}) custom-call(f32[4,80,640]{2,1,0:T(8,128)S(1)} %bitcast.85, f32[4,40,1280]{2,1,0:T(8,128)S(1)} %bitcast.88, f32[48,1280]{1,0:T(8,128)S(1)} %concatenate.35.small_ref), custom_call_target="tpu_custom_call" | custom-call | tf_op jit(solution)/shard_map/reduce_last/pallas_call | solution.py:410
  505.9 1.9 slice.128
  507.9 1.5 reshape.332
  515.9 2.7 reshape.334
  (237 shorter events, 45.3 us)
Async XLA Ops:
  7.2 51.5 %all-gather.4.cloned.1.call-start = ((), (), s32[]{:S(2)}) async-start(), calls=%async_computation.2 | async-start | bytes 2703360 | tf_op jit(solution)/shard_map/all_gather | solution.py:433
  9.6 150.6 %all-gather.6.cloned.1.call-start = ((), (), s32[]{:S(2)}) async-start(), calls=%async_computation.5 | async-start | bytes 15667200 | tf_op jit(solution)/shard_map/all_gather | solution.py:445
  9.6 7.9 %copy-start.20 = (bf16[160,1280]{1,0:T(8,128)(2,1)S(1)}, bf16[160,1280]{1,0:T(8,128)(2,1)}, u32[]{:S(2)}) copy-start(bf16[160,1280]{1,0:T(8,128)(2,1)} %param.18) | copy-start | bytes 1228804
  9.6 7.9 %copy-start.27 = (bf16[40,1280]{1,0:T(8,128)(2,1)S(1)}, bf16[40,1280]{1,0:T(8,128)(2,1)}, u32[]{:S(2)}) copy-start(bf16[40,1280]{1,0:T(8,128)(2,1)} %param.15) | copy-start | bytes 307204
  14.9 2.5 collective-permute-start.3
  16.4 28.9 %copy-start.21 = (bf16[33,1280]{1,0:T(8,128)(2,1)S(1)}, bf16[33,1280]{1,0:T(8,128)(2,1)}, u32[]{:S(2)}) copy-start(bf16[33,1280]{1,0:T(8,128)(2,1)} %param.12) | copy-start | bytes 253444
  17.5 28.4 %copy-start.36 = (s32[2,256]{1,0:T(2,128)S(1)}, s32[2,256]{1,0:T(2,128)}, u32[]{:S(2)}) copy-start(s32[2,256]{1,0:T(2,128)} %param.10) | copy-start | bytes 6148
  17.5 37.9 %copy-start.38 = (s32[2]{0:T(128)S(1)}, s32[2]{0:T(128)}, u32[]{:S(2)}) copy-start(s32[2]{0:T(128)} %len_ref.3) | copy-start | bytes 28
  18.6 445.9 %reduce-scatter.3.cloned.1.call-start = ((), (), s32[]{:S(2)}) async-start(), calls=%async_computation.3 | async-start | bytes 13926400 | tf_op jit(solution)/shard_map/reduce_scatter | solution.py:531
  45.2 10.6 %copy-start.23 = (f32[32,1024]{1,0:T(8,128)}, f32[32,1024]{1,0:T(8,128)S(1)}, u32[]{:S(2)}) copy-start(f32[32,1024]{1,0:T(8,128)S(1)} %reshape.309) | copy-start | bytes 393220
  45.3 16.7 %copy-start.2 = (f32[33,1280]{1,0:T(8,128)}, f32[33,1280]{1,0:T(8,128)S(1)}, u32[]{:S(2)}) copy-start(f32[33,1280]{1,0:T(8,128)S(1)} %convert_element_type.61) | copy-start | bytes 506884
  45.8 13.0 %copy-start.25 = (f32[1280]{0:T(1024)}, f32[1280]{0:T(1024)S(1)}, u32[]{:S(2)}) copy-start(f32[1280]{0:T(1024)S(1)} %mul.239) | copy-start | bytes 15364
  61.9 8.3 %collective-permute-start = (f32[80,1024]{1,0:T(8,128)}, f32[80,1024]{1,0:T(8,128)}, u32[]{:S(2)}, u32[]{:S(2)}) collective-permute-start(f32[80,1024]{1,0:T(8,128)} %get-tuple-element.95), channel_id=1, source_target_pairs={{0,32},{32,64},{64,96},{96,0},{1,33},{33,65},{65,97},{97,1},{2,34}... | collective-permute-start | bytes 983048 | tf_op jit(solution)/shard_map/ppermute | solution.py:465
  64.2 98.7 %copy-start.17 = (pred[2,256,128]{2,1,0:T(32,128)(4,1)}, pred[2,256,128]{2,1,0:T(32,128)(4,1)S(1)}, u32[]{:S(2)}) copy-start(pred[2,256,128]{2,1,0:T(32,128)(4,1)S(1)} %get-tuple-element.92) | copy-start | bytes 196612
  64.8 12.9 %collective-permute-start.1 = (f32[80,1024]{1,0:T(8,128)}, f32[80,1024]{1,0:T(8,128)S(1)}, u32[]{:S(2)}, u32[]{:S(2)}) collective-permute-start(f32[80,1024]{1,0:T(8,128)} %get-tuple-element.95), channel_id=1, source_target_pairs={{0,64},{32,96},{64,0},{96,32},{1,65},{33,97},{65,1},{97,33},{2,66}... | collective-permute-start | bytes 983048 | tf_op jit(solution)/shard_map/ppermute | solution.py:465
  68.1 11.9 %collective-permute-start.2 = (f32[80,1024]{1,0:T(8,128)}, f32[80,1024]{1,0:T(8,128)S(1)}, u32[]{:S(2)}, u32[]{:S(2)}) collective-permute-start(f32[80,1024]{1,0:T(8,128)} %get-tuple-element.95), channel_id=1, source_target_pairs={{0,96},{32,0},{64,32},{96,64},{1,97},{33,1},{65,33},{97,65},{2,98}... | collective-permute-start | bytes 983048 | tf_op jit(solution)/shard_map/ppermute | solution.py:465
  115.8 47.1 %copy-start.22 = (bf16[33,1280]{1,0:T(8,128)(2,1)S(1)}, bf16[33,1280]{1,0:T(8,128)(2,1)}, u32[]{:S(2)}) copy-start(bf16[33,1280]{1,0:T(8,128)(2,1)} %param.12) | copy-start | bytes 253444
  115.8 47.1 %copy-start.34 = (f32[2,256]{1,0:T(2,128)S(1)}, f32[2,256]{1,0:T(2,128)}, u32[]{:S(2)}) copy-start(f32[2,256]{1,0:T(2,128)} %get-tuple-element.71) | copy-start | bytes 6148
  161.7 4.1 collective-permute-start.4
  173.4 10.8 %collective-permute-start.5 = (bf16[512,1280]{1,0:T(8,128)(2,1)}, bf16[512,1280]{1,0:T(8,128)(2,1)}, u32[]{:S(2)}, u32[]{:S(2)}) collective-permute-start(bf16[512,1280]{1,0:T(8,128)(2,1)} %add_convert_fusion), channel_id=1, source_target_pairs={{0,1},{1,0},{2,3},{3,2},{4,5},{5,4},{6,7},{7,6},{8,9},{9,8},{10,11... | collective-permute-start | bytes 3932168 | tf_op jit(solution)/shard_map/ppermute | solution.py:488
  173.8 27.6 %collective-permute-start.7 = (bf16[512,1280]{1,0:T(8,128)(2,1)}, bf16[512,1280]{1,0:T(8,128)(2,1)}, u32[]{:S(2)}, u32[]{:S(2)}) collective-permute-start(bf16[512,1280]{1,0:T(8,128)(2,1)} %bitcast.18), channel_id=1, source_target_pairs={{0,1},{1,0},{2,3},{3,2},{4,5},{5,4},{6,7},{7,6},{8,9},{9,8},{10,11... | collective-permute-start | bytes 3932168 | tf_op jit(solution)/shard_map/ppermute | solution.py:447
  178.5 22.9 %copy-start.4 = (bf16[16,160,1280]{2,1,0:T(8,128)(2,1)}, bf16[16,160,1280]{2,1,0:T(8,128)(2,1)S(1)}, u32[]{:S(2)}) copy-start(bf16[16,160,1280]{2,1,0:T(8,128)(2,1)S(1)} %slice.117) | copy-start | bytes 19660804
  184.2 9.5 %copy-start.12 = (bf16[16,80,1280]{2,1,0:T(8,128)(2,1)}, bf16[16,80,1280]{2,1,0:T(8,128)(2,1)S(1)}, u32[]{:S(2)}) copy-start(bf16[16,80,1280]{2,1,0:T(8,128)(2,1)S(1)} %get-tuple-element.76) | copy-start | bytes 9830404
  184.3 9.5 %copy-start.14 = (bf16[16,80,1280]{2,1,0:T(8,128)(2,1)}, bf16[16,80,1280]{2,1,0:T(8,128)(2,1)S(1)}, u32[]{:S(2)}) copy-start(bf16[16,80,1280]{2,1,0:T(8,128)(2,1)S(1)} %get-tuple-element.75) | copy-start | bytes 9830404
  228.2 237.5 %reduce-scatter.5.cloned.1.call-start = ((), (), s32[]{:S(2)}) async-start(), calls=%async_computation.4 | async-start | bytes 13926400 | tf_op jit(solution)/shard_map/reduce_scatter | solution.py:530
  248.1 6.5 %copy-start.13 = (bf16[16,80,1280]{2,1,0:T(8,128)(2,1)S(1)}, bf16[16,80,1280]{2,1,0:T(8,128)(2,1)}, u32[]{:S(2)}) copy-start(bf16[16,80,1280]{2,1,0:T(8,128)(2,1)} %copy-done.12) | copy-start | bytes 9830404
  248.1 15.7 %slice-start = ((s8[6553600]{0:T(1024)(128)(4,1)}), s8[4194304]{0:T(1024)(128)(4,1)S(1)}, s32[]{:S(2)}) async-start(s8[6553600]{0:T(1024)(128)(4,1)} %bitcast.96), calls=%async_computation.6 | async-start | bytes 8388608
  248.1 15.7 %slice-start.4 = ((s8[5242880]{0:T(1024)(128)(4,1)}), s8[4194304]{0:T(1024)(128)(4,1)S(1)}, s32[]{:S(2)}) async-start(s8[5242880]{0:T(1024)(128)(4,1)} %bitcast.101), calls=%async_computation.10 | async-start | bytes 8388608
  254.6 9.2 %slice-start.1 = ((s8[6553600]{0:T(1024)(128)(4,1)}), s8[2359296]{0:T(1024)(128)(4,1)S(1)}, s32[]{:S(2)}) async-start(s8[6553600]{0:T(1024)(128)(4,1)} %bitcast.96), calls=%async_computation.7 | async-start | bytes 4718592
  254.6 9.2 %slice-start.5 = ((s8[5242880]{0:T(1024)(128)(4,1)}), s8[1048576]{0:T(1024)(128)(4,1)S(1)}, s32[]{:S(2)}) async-start(s8[5242880]{0:T(1024)(128)(4,1)} %bitcast.101), calls=%async_computation.11 | async-start | bytes 2097152
  263.3 15.5 %collective-permute-start.8 = (f32[512,1280]{1,0:T(8,128)}, f32[512,1280]{1,0:T(8,128)}, u32[]{:S(2)}, u32[]{:S(2)}) collective-permute-start(f32[512,1280]{1,0:T(8,128)} %slice.150), channel_id=1, source_target_pairs={{0,1},{1,0},{2,3},{3,2},{4,5},{5,4},{6,7},{7,6},{8,9},{9,8},{10,11... | collective-permute-start | bytes 7864328 | tf_op jit(solution)/shard_map/ppermute | solution.py:502
  273.9 8.8 %collective-permute-start.6 = (f32[512,1280]{1,0:T(8,128)}, f32[512,1280]{1,0:T(8,128)}, u32[]{:S(2)}, u32[]{:S(2)}) collective-permute-start(f32[512,1280]{1,0:T(8,128)} %slice.145), channel_id=1, source_target_pairs={{0,1},{1,0},{2,3},{3,2},{4,5},{5,4},{6,7},{7,6},{8,9},{9,8},{10,11... | collective-permute-start | bytes 7864328 | tf_op jit(solution)/shard_map/ppermute | solution.py:494
  278.7 4.1 slice-start.2
  278.8 4.0 slice-start.3
  282.8 4.2 copy-start.11
  351.3 8.3 %copy-start.9 = (bf16[512,1280]{1,0:T(8,128)(2,1)S(1)}, bf16[512,1280]{1,0:T(8,128)(2,1)}, u32[]{:S(2)}) copy-start(bf16[512,1280]{1,0:T(8,128)(2,1)} %copy-done.8) | copy-start | bytes 3932164
  351.3 8.2 %copy-start.16 = (bf16[1280,512]{1,0:T(8,128)(2,1)S(1)}, bf16[1280,512]{1,0:T(8,128)(2,1)}, u32[]{:S(2)}) copy-start(bf16[1280,512]{1,0:T(8,128)(2,1)} %copy.37) | copy-start | bytes 3932164
  355.0 10.6 %collective-permute-start.9 = (f32[80,1024]{1,0:T(8,128)S(1)}, f32[80,1024]{1,0:T(8,128)S(1)}, u32[]{:S(2)}, u32[]{:S(2)}) collective-permute-start(f32[80,1024]{1,0:T(8,128)S(1)} %get-tuple-element.80), channel_id=1, source_target_pairs={{0,32},{32,64},{64,96},{96,0},{1,33},{33,65},{65,97},{97,1},{2,34}... | collective-permute-start | bytes 983048 | tf_op jit(solution)/shard_map/ppermute | solution.py:515
  356.6 9.1 %collective-permute-start.11 = (f32[80,1024]{1,0:T(8,128)S(1)}, f32[80,1024]{1,0:T(8,128)S(1)}, u32[]{:S(2)}, u32[]{:S(2)}) collective-permute-start(f32[80,1024]{1,0:T(8,128)S(1)} %get-tuple-element.81), channel_id=1, source_target_pairs={{0,96},{32,0},{64,32},{96,64},{1,97},{33,1},{65,33},{97,65},{2,98}... | collective-permute-start | bytes 983048 | tf_op jit(solution)/shard_map/ppermute | solution.py:515
  358.0 15.5 %collective-permute-start.10 = (f32[80,1024]{1,0:T(8,128)S(1)}, f32[80,1024]{1,0:T(8,128)S(1)}, u32[]{:S(2)}, u32[]{:S(2)}) collective-permute-start(f32[80,1024]{1,0:T(8,128)S(1)} %get-tuple-element.82), channel_id=1, source_target_pairs={{0,64},{32,96},{64,0},{96,32},{1,65},{33,97},{65,1},{97,33},{2,66}... | collective-permute-start | bytes 983048 | tf_op jit(solution)/shard_map/ppermute | solution.py:515
  359.5 14.0 %copy-start.1 = (bf16[1280,1024]{1,0:T(8,128)(2,1)S(1)}, bf16[1280,1024]{1,0:T(8,128)(2,1)}, u32[]{:S(2)}) copy-start(bf16[1280,1024]{1,0:T(8,128)(2,1)} %all-gather.4.cloned.1.call-done) | copy-start | bytes 7864324
  364.2 11.9 %copy-start.3 = (f32[33,1280]{1,0:T(8,128)S(1)}, f32[33,1280]{1,0:T(8,128)}, u32[]{:S(2)}) copy-start(f32[33,1280]{1,0:T(8,128)} %copy-done.2) | copy-start | bytes 506884
  364.2 11.9 %copy-start.26 = (f32[1280]{0:T(1024)S(1)}, f32[1280]{0:T(1024)}, u32[]{:S(2)}) copy-start(f32[1280]{0:T(1024)} %copy-done.25) | copy-start | bytes 15364
  364.2 11.9 %copy-start.29 = (f32[2,33]{1,0:T(2,128)S(1)}, f32[2,33]{1,0:T(2,128)}, u32[]{:S(2)}) copy-start(f32[2,33]{1,0:T(2,128)} %copy-done.28) | copy-start | bytes 796
  364.2 11.9 %copy-start.31 = (f32[2,33]{1,0:T(2,128)S(1)}, f32[2,33]{1,0:T(2,128)}, u32[]{:S(2)}) copy-start(f32[2,33]{1,0:T(2,128)} %copy-done.30) | copy-start | bytes 796
  364.2 11.9 %copy-start.33 = (f32[2,33]{1,0:T(2,128)S(1)}, f32[2,33]{1,0:T(2,128)}, u32[]{:S(2)}) copy-start(f32[2,33]{1,0:T(2,128)} %copy-done.32) | copy-start | bytes 796
  364.2 12.3 %copy-start.18 = (pred[2,256,128]{2,1,0:T(32,128)(4,1)S(1)}, pred[2,256,128]{2,1,0:T(32,128)(4,1)}, u32[]{:S(2)}) copy-start(pred[2,256,128]{2,1,0:T(32,128)(4,1)} %copy-done.17) | copy-start | bytes 196612
  505.5 7.3 %collective-permute-start.12 = (f32[40,2560]{1,0:T(8,128)}, f32[40,2560]{1,0:T(8,128)}, u32[]{:S(2)}, u32[]{:S(2)}) collective-permute-start(f32[40,2560]{1,0:T(8,128)} %constant_dynamic-slice_fusion.1), channel_id=1, source_target_pairs={{0,1},{1,0},{2,3},{3,2},{4,5},{5,4},{6,7},{7,6},{8,9},{9,8},{10,11... | collective-permute-start | bytes 1228808 | tf_op jit(solution)/shard_map/ppermute | solution.py:543
  (14 other events, 40.6 us)
Sparse Core Ops, SparseCore 0:
  10.8 47.8 all-gather.3
  60.9 99.2 all-gather.5
  228.4 93.8 reduce-scatter.2
  325.5 107.7 reduce-scatter.4

commit v3 on v2

--- a/solution.py
+++ b/solution.py
@@ -84,56 +84,61 @@
     return q, k.astype(BF16), v.astype(BF16)
 
 
+def head_masks():
+    low = lax.broadcasted_iota(jnp.int32, (QLEN, LANES), 1) < HDIM
+    return low, jnp.logical_not(low)
+
+
+def key_mask(seq_len):
+    return lax.broadcasted_iota(jnp.int32, (SEQ, QLEN), 0) < seq_len
+
+
+def head_cols(head):
+    return slice(HDIM * head, HDIM * (head + 1))
+
+
 def attn_fwd_kernel(len_ref, ohk_ref, ohq_ref, tq_ref, tk_ref, tv_ref, csk_ref, csq_ref, o_ref, lse_ref):
-    seq_len = len_ref[pl.program_id(0)]
     q, k, v = expand_qkv(ohk_ref, ohq_ref, tq_ref, tk_ref, tv_ref, csk_ref, csq_ref)
-    low = lax.broadcasted_iota(jnp.int32, (QLEN, LANES), 1) < HDIM
-    key_ok = lax.broadcasted_iota(jnp.int32, (QLEN, SEQ), 1) < seq_len
-    outs, stats = [], []
-    for head in range(2):
-        q_h = jnp.where(low if head == 0 else jnp.logical_not(low), q, 0.0).astype(BF16)
-        s = jnp.where(key_ok, mm(q_h, k, NT), NEG_BIG)
-        top = jnp.max(s, axis=-1, keepdims=True)
+    key_ok = key_mask(len_ref[pl.program_id(0)])
+    v_t = v.T
+    outs = []
+    for head, mine in enumerate(head_masks()):
+        q_h = jnp.where(mine, q, 0.0).astype(BF16)
+        s = jnp.where(key_ok, mm(k, q_h, NT), NEG_BIG)
+        top = jnp.max(s, axis=0, keepdims=True)
         e = jnp.exp(s - top)
-        total = jnp.sum(e, axis=-1, keepdims=True)
-        outs.append(mm(e.astype(BF16), v) / total)
-        stats.append(jnp.broadcast_to(top + jnp.log(total), (QLEN, LANES)))
-    o_ref[0] = jnp.where(low, outs[0], outs[1]).astype(BF16)
-    lse_ref[0] = jnp.where(low, stats[0], stats[1])
-
-
-def attn_bwd_kernel(len_ref, ohk_ref, ohq_ref, tq_ref, tk_ref, tv_ref, csk_ref, csq_ref, do_ref, lse_ref, sq_ref, sk_ref, sv_ref):
-    seq_len = len_ref[pl.program_id(0)]
+        total = jnp.sum(e, axis=0, keepdims=True)
+        outs.append(mm(v_t[head_cols(head)], e.astype(BF16)) / total)
+        lse_ref[0, 0, head:head + 1, :] = top + jnp.log(total)
+    o_ref[0] = jnp.concatenate(outs, axis=0).T.astype(BF16)
+
+
+def attn_bwd_kernel(len_ref, ohk_ref, ohq_ref, tq_ref, tk_ref, tv_ref, csk_ref, csq_ref, okt_ref, oqt_ref, do_ref, lse_ref, sq_ref, sk_ref, sv_ref):
     q, k, v = expand_qkv(ohk_ref, ohq_ref, tq_ref, tk_ref, tv_ref, csk_ref, csq_ref)
     d_o = do_ref[0]
-    low = lax.broadcasted_iota(jnp.int32, (QLEN, LANES), 1) < HDIM
-    key_ok = lax.broadcasted_iota(jnp.int32, (QLEN, SEQ), 1) < seq_len
+    key_ok = key_mask(len_ref[pl.program_id(0)])
+    k_t = k.T
     dv, dk, dqs = None, None, []
-    for head in range(2):
-        mine = low if head == 0 else jnp.logical_not(low)
+    for head, mine in enumerate(head_masks()):
         q_h = jnp.where(mine, q, 0.0).astype(BF16)
         do_h = jnp.where(mine, d_o, jnp.zeros_like(d_o))
-        s = mm(q_h, k, NT)
-        p = jnp.where(key_ok, jnp.exp(s - lse_ref[0, :, HDIM * head:HDIM * head + 1]), 0.0)
-        t = p * mm(do_h, v, NT)
-        ds = (t - p * jnp.sum(t, axis=-1, keepdims=True)).astype(BF16)
-        dv_h = mm(p.astype(BF16), do_h, TN)
-        dk_h = mm(ds, q_h, TN)
+        p = jnp.where(key_ok, jnp.exp(mm(k, q_h, NT) - lse_ref[0, 0, head:head + 1, :]), 0.0)
+        t = p * mm(v, do_h, NT)
+        ds = (t - p * jnp.sum(t, axis=0, keepdims=True)).astype(BF16)
+        dv_h = mm(p.astype(BF16), do_h)
+        dk_h = mm(ds, q_h)
         dv = dv_h if dv is None else dv + dv_h
         dk = dk_h if dk is None else dk + dk_h
-        dqs.append(mm(ds, k))
-    dq = jnp.where(low, dqs[0], dqs[1])
-    ohk = ohk_ref[0]
-    ohq = ohq_ref[0]
-    top = TN
-    real = lax.broadcasted_iota(jnp.int32, (ROWS, LANES), 0) < VOCAB
-
-    def by_token(onehot, d_in):
-        return jnp.where(real, mm(onehot, d_in.astype(BF16), top)[:ROWS], 0.0)
-    s_q = by_token(ohq, dq * csq_ref[:, :LANES]) + rot_half(by_token(ohq, dq * csq_ref[:, LANES:]), -1.0)
-    sq_ref[0] = s_q * HDIM ** -0.5
-    sk_ref[0] = by_token(ohk, dk * csk_ref[:, :LANES]) + rot_half(by_token(ohk, dk * csk_ref[:, LANES:]), -1.0)
-    sv_ref[0] = by_token(ohk, dv)
+        dqs.append(mm(k_t[head_cols(head)], ds))
+    dq = jnp.concatenate(dqs, axis=0).T
+
+    def by_token(onehot_t, d_in):
+        return mm(onehot_t, d_in.astype(BF16))
+    s_q = by_token(oqt_ref[0], jnp.concatenate([dq * csq_ref[:, :LANES], dq * csq_ref[:, LANES:]], axis=1))
+    sq_ref[0] = (s_q[:, :LANES] + rot_half(s_q[:, LANES:], -1.0)) * HDIM ** -0.5
+    s_k = by_token(okt_ref[0], jnp.concatenate([dk * csk_ref[:, :LANES], dk * csk_ref[:, LANES:]], axis=1))
+    sk_ref[0] = s_k[:, :LANES] + rot_half(s_k[:, LANES:], -1.0)
+    sv_ref[0] = by_token(okt_ref[0], dv)
 
 
 def tab_spec():
@@ -157,20 +162,24 @@
     return pl.BlockSpec((1, QLEN, LANES), lambda b, j: (b, 0, j))
 
 
+def lse_spec():
+    return pl.BlockSpec((1, 1, 8, QLEN), lambda b, j: (b, j, 0, 0))
+
+
 def attn_fwd(lengths, ohk, ohq, tq, tk, tv, csk, csq):
     return pl.pallas_call(
-        attn_fwd_kernel, grid=(2, PAIRS), in_specs=attn_specs(), out_specs=[row_spec(), row_spec()],
-        out_shape=[jax.ShapeDtypeStruct((2, QLEN, DIM), BF16), jax.ShapeDtypeStruct((2, QLEN, DIM), F32)],
+        attn_fwd_kernel, grid=(2, PAIRS), in_specs=attn_specs(), out_specs=[row_spec(), lse_spec()],
+        out_shape=[jax.ShapeDtypeStruct((2, QLEN, DIM), BF16), jax.ShapeDtypeStruct((2, PAIRS, 8, QLEN), F32)],
         cost_estimate=COST,
         name='attn_fwd')(lengths, ohk, ohq, tq, tk, tv, csk, csq)
 
 
-def attn_bwd(lengths, ohk, ohq, tq, tk, tv, csk, csq, d_o, lse):
+def attn_bwd(lengths, ohk, ohq, tq, tk, tv, csk, csq, okt, oqt, d_o, lse):
     return pl.pallas_call(
-        attn_bwd_kernel, grid=(2, PAIRS), in_specs=attn_specs() + [row_spec(), row_spec()],
+        attn_bwd_kernel, grid=(2, PAIRS), in_specs=attn_specs() + [pl.BlockSpec((1, ROWS, SEQ), lambda b, j: (b, 0, 0)), pl.BlockSpec((1, ROWS, QLEN), lambda b, j: (b, 0, 0)), row_spec(), lse_spec()],
         out_specs=[tab_spec()] * 3, out_shape=[jax.ShapeDtypeStruct((2, ROWS, DIM), F32)] * 3,
         cost_estimate=COST,
-        name='attn_bwd')(lengths, ohk, ohq, tq, tk, tv, csk, csq, d_o, lse)
+        name='attn_bwd')(lengths, ohk, ohq, tq, tk, tv, csk, csq, okt, oqt, d_o, lse)
 
 
 class Ring:
@@ -219,20 +228,26 @@
         self.drain()
         return low, high
 
-    def ag_start(self, slot):
-        self.slot = slot
-        self.a1 = self.send(slot(self.me, ALL), slot(self.me, ALL), self.right)
-        self.a2 = self.send(slot(self.me, ALL), slot(self.me, ALL), self.left)
+    def ag_start(self, slot, own=None, split=True):
+        self.slot, self.split = slot, split
+        home = slot(self.me, ALL)
+        own = home if own is None else own
+        self.a1 = self.send(own, home, self.right)
+        self.a2 = self.send(own, home, self.left)
 
     def ag_mid(self):
         self.a1.wait_recv()
-        self.a3 = self.send(self.slot(self.left, LO), self.slot(self.left, LO), self.right)
+        part = self.slot(self.left, LO if self.split else ALL)
+        self.a3 = self.send(part, part, self.right)
         self.a2.wait_recv()
-        self.a4 = self.send(self.slot(self.right, HI), self.slot(self.right, HI), self.left)
+        if self.split:
+            part = self.slot(self.right, HI)
+            self.a4 = self.send(part, part, self.left)
 
     def ag_end(self):
         self.a3.wait_recv()
-        self.a4.wait_recv()
+        if self.split:
+            self.a4.wait_recv()
         self.drain()
 
 
@@ -338,6 +353,52 @@
         compiler_params=pltpu.CompilerParams(collective_id=1, has_side_effects=True, vmem_limit_bytes=56 * 1024 * 1024),
         cost_estimate=COST,
         name='reduce_oq')(d_out, d_qkv)
+
+
+def first_kernel(wq_ref, wo_ref, pack_ref, tok_ref, gq, go, gp, gt, sends, recvs):
+    ports = ports_of(sends, recvs)
+    ci = lax.axis_index('c')
+    y1, z1, yp, xt = Ring('y', ports), Ring('z', ports), Ring('y', ports), Ring('x', ports)
+    y2, z2, zp = Ring('y', ports), Ring('z', ports), Ring('z', ports)
+    yi, zi = y1.me, z1.me
+    meet()
+    y1.ag_start(lambda k, h: gq.at[zi, k, ci] if h == ALL else gq.at[zi, k, ci, :, pl.ds(QCOLS // 2 * h, QCOLS // 2)], wq_ref)
+    z1.ag_start(lambda k, h: go.at[k, yi, ci] if h == ALL else go.at[k, yi, ci, :, pl.ds(HALF_D * h, HALF_D)], wo_ref)
+    yp.ag_start(lambda k, h: gp.at[zi, k, ci], pack_ref, False)
+    xt.ag_start(lambda k, h: gt.at[k], tok_ref, False)
+    gq[zi, yi, ci] = wq_ref[...]
+    go[zi, yi, ci] = wo_ref[...]
+    gp[zi, yi, ci] = pack_ref[...]
+    gt[xt.me] = tok_ref[...]
+    stage = (y1, z1, yp, xt)
+    for ring in stage:
+        ring.ag_mid()
+    for ring in stage:
+        ring.ag_end()
+    z2.ag_start(lambda k, h: gq.at[k, :, ci] if h == ALL else gq.at[k, pl.ds(2 * h, 2), ci])
+    y2.ag_start(lambda k, h: go.at[:, k, ci] if h == ALL else go.at[pl.ds(2 * h, 2), k, ci])
+    zp.ag_start(lambda k, h: gp.at[k, :, ci], None, False)
+    stage = (z2, y2, zp)
+    for ring in stage:
+        ring.ag_mid()
+    for ring in stage:
+        ring.ag_end()
+    swaps = [core_copy(ref.at[:, :, ci], ref.at[:, :, ci], ports) for ref in (gq, go, gp)]
+    for swap in swaps:
+        swap.start()
+    for swap in swaps:
+        swap.wait_recv()
+        swap.wait_send()
+
+
+def gather_first(wq, wo, pack, tok):
+    return pl.pallas_call(
+        first_kernel, in_specs=vmem(4), out_specs=vmem(4),
+        out_shape=[jax.ShapeDtypeStruct((4, 4, 2) + wq.shape, BF16), jax.ShapeDtypeStruct((4, 4, 2) + wo.shape, BF16),
+                   jax.ShapeDtypeStruct((4, 4, 2) + pack.shape, F32), jax.ShapeDtypeStruct((4,) + tok.shape, jnp.int32)],
+        scratch_shapes=[pltpu.SemaphoreType.DMA((28,)), pltpu.SemaphoreType.DMA((28,))],
+        compiler_params=pltpu.CompilerParams(collective_id=3, has_side_effects=True, vmem_limit_bytes=24 * 1024 * 1024),
+        cost_estimate=COST, name='gather_first')(wq, wo, pack, tok)
 
 
 SMALL = 48
@@ -430,19 +491,20 @@
         chip = lax.axis_index('z') * 4 + lax.axis_index('y')
         fi = chip * 2 + ci
         wq_loc = lax.dynamic_slice_in_dim(jnp.pad(w_qkv.reshape(ROWS, 3 * DIM), ((0, 0), (0, 256))), QCOLS * xi, QCOLS, axis=1)
-        qkv_w = lax.all_gather(wq_loc, FSDP, axis=0, tiled=True)
         packed = jnp.concatenate([layer_vecs.reshape(360), b_up, jnp.zeros((504,), F32)]).reshape(8, LANES)
-        packed = lax.all_gather(packed, FSDP, axis=0, tiled=True).reshape(32, 1024)
-        vecs = packed[:, :360].reshape(32, 9, ROWS).transpose(1, 0, 2).reshape(9, DIM)
-        up_b = lax.dynamic_index_in_dim(packed[:, 360:520].reshape(16, 2, 160), ci, axis=1, keepdims=False).reshape(FFH)
-        tok_all = lax.all_gather(tokens, 'x', axis=1, tiled=True)
         up_loc = w_up.reshape(ROWS, 16, 2, 160)
         up_mine = lax.dynamic_index_in_dim(up_loc, ci, axis=2, keepdims=False).reshape(ROWS, FFH)
         up_send = lax.dynamic_index_in_dim(up_loc, 1 - ci, axis=2, keepdims=False).reshape(ROWS, FFH)
         up_recv = lax.ppermute(up_send, 'c', SWAP)
         up_pair = jnp.concatenate([jnp.where(ci == 0, up_mine, up_recv), jnp.where(ci == 0, up_recv, up_mine)], axis=0)
-        shard = jnp.concatenate([up_pair[:, :DIM], up_pair[:, DIM:], w_down, w_out], axis=0)
+        shard = jnp.concatenate([up_pair[:, :DIM], up_pair[:, DIM:], w_down], axis=0)
+        shard, packed = lax.optimization_barrier((shard, packed))
         gathered = lax.all_gather(shard, CHIP, axis=0, tiled=False)
+        qkv_w, out_w, packed, tok_all = gather_first(wq_loc, w_out, packed, tokens.reshape(4, LANES))
+        qkv_w, out_w, packed = qkv_w.reshape(DIM, QCOLS), out_w.reshape(DIM, DIM), packed.reshape(32, 8 * LANES)
+        tok_all = tok_all.reshape(4, 2, QLEN).transpose(1, 0, 2).reshape(2, SEQ)
+        vecs = packed[:, :360].reshape(32, 9, ROWS).transpose(1, 0, 2).reshape(9, DIM)
+        up_b = lax.dynamic_index_in_dim(packed[:, 360:520].reshape(16, 2, 160), ci, axis=1, keepdims=False).reshape(FFH)
         grad_own = grad_out.reshape(TOK, DIM)
         grad2 = jnp.concatenate([grad_own, lax.ppermute(grad_own, 'c', SWAP)], axis=0)
 
@@ -454,6 +516,9 @@
         ohk = one_hot3(tok_eff)
         ohq = one_hot3(tok_own)
         oh_own = ohq[:, :, :VOCAB]
+        rows = jnp.arange(ROWS)[:, None]
+        okt = (tok_eff[:, None, :] == rows).astype(BF16)
+        oqt = (tok_own[:, None, :] == rows).astype(BF16)
         row_scale = jnp.where(jnp.arange(VOCAB)[None, :] == MASK_ID, 0.0, drop_scale[:, None])
         e_rows = embed_table.astype(F32)[None] * row_scale[:, :, None]
         xhat1, inv1 = ln_stats(e_rows)
@@ -472,13 +537,6 @@
         csq = lax.dynamic_slice_in_dim(csk, xi * QLEN, QLEN, axis=0)
 
         attn_o, lse = attn_fwd(lengths, ohk, ohq, *tabs, csk, csq)
-        attn_o, gathered = lax.optimization_barrier((attn_o, gathered))
-        up_w0 = gathered[:, 0:80].reshape(DIM, DIM)
-        up_w1 = gathered[:, 80:160].reshape(DIM, DIM)
-        down_w = gathered[:, 160:320].reshape(2 * DIM, DIM)
-        out_mine = gathered[:, 320:360]
-        out_recv = lax.ppermute(out_mine, 'c', SWAP)
-        out_w = jnp.stack([jnp.where(ci == 0, out_mine, out_recv), jnp.where(ci == 0, out_recv, out_mine)], axis=1).reshape(DIM, DIM)
         attn_o2 = attn_o.reshape(TOK, DIM)
         keep_own = jnp.where(tok_own == MASK_ID, 0.0, drop_scale[:, None])
         embedded = jnp.einsum('bsv,vd->bsd', oh_own, embed_table, preferred_element_type=F32) * keep_own[:, :, None]
@@ -486,6 +544,10 @@
         xhat2, inv2 = ln_stats(x1)
         nm = (xhat2 * vecs[6] + vecs[7]).astype(BF16)
         nm2 = jnp.concatenate([nm, lax.ppermute(nm, 'c', SWAP)], axis=0)
+        nm2, gathered = lax.optimization_barrier((nm2, gathered))
+        up_w0 = gathered[:, 0:80].reshape(DIM, DIM)
+        up_w1 = gathered[:, 80:160].reshape(DIM, DIM)
+        down_w = gathered[:, 160:320].reshape(2 * DIM, DIM)
         up_lin = jnp.concatenate([mm(nm2, up_w0), mm(nm2, up_w1)], axis=1) + up_b
         cdf = 0.5 * (1.0 + lax.erf(up_lin * 0.7071067811865476))
         gelu_b = (up_lin * cdf).astype(BF16)
@@ -505,7 +567,7 @@
         d_resid_b = d_resid.astype(BF16)
         d_outw = mm(attn_o2, d_resid_b, TN)
         d_attn_b = mm(d_resid_b, out_w, NT).astype(BF16)
-        s_q, s_k, s_v = attn_bwd(lengths, ohk, ohq, *tabs, csk, csq, d_attn_b.reshape(2, QLEN, DIM), lse)
+        s_q, s_k, s_v = attn_bwd(lengths, ohk, ohq, *tabs, csk, csq, okt, oqt, d_attn_b.reshape(2, QLEN, DIM), lse)
 
         d_bqkv = jnp.stack([jnp.sum(part, axis=(0, 1)) for part in (s_q, s_k, s_v)])
         s_all = jnp.concatenate([s_q, s_k, s_v, jnp.zeros((2, ROWS, 256), F32)], axis=2).reshape(2 * ROWS, 4 * QCOLS)

time: 537 us -> 502 us (0.935)
  waiting for transfers between devices: 65.6 us -> 17.7 us
  Pallas kernels: 215 us -> 262 us
  blocking collectives: 35.7 us -> 0 us
  local copies, waits for them, and re-layouts: 52.6 us -> 59.9 us
    pallas_call x0 -> x1, Pallas kernels: none -> 45.7 us  [gather_first(): pl.pallas_call(first_kernel, in_specs=vmem(4), out_specs=vmem(4), out_sha...]
    all_gather x1, waiting for transfers between devices: 44.3 us -> 0.01 us  [local_step(): gathered = lax.all_gather(shard, CHIP, axis=0, tiled=False)]
    all_gather x2 -> x0, blocking collectives: 35.7 us -> none  [the longest x1 26.3 us: local_step(): packed = lax.all_gather(packed, FSDP, axis=0, tiled=True).reshape(32, 1024)]
    pallas_call x1, Pallas kernels: 60.3 us -> 53.7 us  [attn_bwd(): pl.pallas_call(attn_bwd_kernel, grid=(2, PAIRS), in_specs=attn_specs() +...]
    dot_general x12, matrix products: 87.3 us -> 81 us  [mm(): return lax.dot_general(a, b, (dims, ((), ())), preferred_element_type=F32)]
    pallas_call x1, Pallas kernels: 34.7 us -> 40.9 us  [attn_fwd(): pl.pallas_call(attn_fwd_kernel, grid=(2, PAIRS), in_specs=attn_specs(), o...]
    unnamed x96 -> x119, local copies, waits for them, and re-layouts: 12.4 us -> 16.4 us
  transfers between devices with their start and end apart: 17 -> 15, of which waited for: 8 -> 5; matrix products, arithmetic and copies ran while one was open for 24% -> 27% of each run, Pallas kernels for 34% -> 46%
where the time goes in v3:
time: 502 us; the launch traced here: 493 us
  Pallas kernels  262 us (52%)
  matrix products  90.6 us (18%)
  local copies, waits for them, and re-layouts  59.9 us (12%)
  other arithmetic  35.4 us (7%)
  waiting for transfers between devices  17.7 us (4%)
  between operations  15.4 us (3%)
  starting transfers between devices  11.8 us (2%)
    pallas_call x1, Pallas kernels, reduce_oq(): pl.pallas_call(oq_kernel, in_specs=vmem(2), out_specs=vmem(2), out_shape=...  85.1 us
    dot_general x12, matrix products, mm(): return lax.dot_general(a, b, (dims, ((), ())), preferred_element_type=F32)  81 us
    pallas_call x1, Pallas kernels, attn_bwd(): pl.pallas_call(attn_bwd_kernel, grid=(2, PAIRS), in_specs=attn_specs() +...  53.7 us
    pallas_call x1, Pallas kernels, gather_first(): pl.pallas_call(first_kernel, in_specs=vmem(4), out_specs=vmem(4), out_sha...  45.7 us
    pallas_call x1, Pallas kernels, attn_fwd(): pl.pallas_call(attn_fwd_kernel, grid=(2, PAIRS), in_specs=attn_specs(), o...  40.9 us
    pallas_call x1, Pallas kernels, reduce_last(): pl.pallas_call(last_kernel, in_specs=vmem(3), out_specs=vmem(3), out_shap...  36.9 us
    unnamed x119, local copies, waits for them, and re-layouts  16.4 us
  transfers between devices with their start and end apart: 15, of which 5 were waited for; matrix products, arithmetic and copies ran while one was open for 27% of the time, Pallas kernels for 46%

profile of v3, /device:TPU:1, one launch (start us, length us, event | category | flops | bytes accessed | tf_op | source)
XLA Modules:
  0.0 493.3 jit_solution(774915466248582302)
XLA Ops:
  7.2 1.8 reshape.362
  9.0 4.1 dynamic-slice_reduce_fusion.1
  13.5 1.4 collective-permute-start
  20.8 45.7 %gather_first.1 = (bf16[4,4,2,40,1024]{4,3,2,1,0:T(8,128)(2,1)S(1)}, bf16[4,4,2,40,1280]{4,3,2,1,0:T(8,128)(2,1)S(1)}, f32[4,4,2,8,128]{4,3,2,1,0:T(8,128)S(1)}, s32[4,4,128]{2,1,0:T(4,128)S(1)}) custom-call(bf16[40,1024]{1,0:T(8,128)(2,1)S(1)} %pad_dynamic-slice_fusion.2.wq_ref, bf16[40,1280]{1,0:T(8,128)(2,1)S(1)} %copy-done.3, ...), custom_call_target="tpu_custom_call" | custom-call | flops 20000000000 | bytes 15000000 | tf_op jit(solution)/shard_map/gather_first/pallas_call | solution.py:395
  66.5 1.7 copy-done.4
  73.0 2.1 collective-permute-start.2
  75.3 2.6 collective-permute-start.3
  78.9 2.0 convolution_multiply_fusion
  83.9 7.5 %collective-permute-done.1 = f32[80,1024]{1,0:T(8,128)S(1)} collective-permute-done((f32[80,1024]{1,0:T(8,128)}, f32[80,1024]{1,0:T(8,128)S(1)}, u32[]{:S(2)}, u32[]{:S(2)}) %collective-permute-start.1) | collective-permute-done | bytes 327712 | tf_op jit(solution)/shard_map/ppermute | solution.py:530
  92.6 40.9 %attn_fwd.1 = (bf16[2,256,1280]{2,1,0:T(8,128)(2,1)}, f32[2,10,8,256]{3,2,1,0:T(8,128)}) custom-call(s32[2]{0:T(128)} %len_ref.3, bf16[2,1024,128]{2,1,0:T(8,128)(2,1)} %and_convert_fusion.ohk_ref, bf16[2,256,128]{2,1,0:T(8,128)(2,1)} %get-tuple-element.102.ohq_ref, f32[2,40,1280]{2,1,0:T(8,128)} %get-tuple-element.97.tq_ref, ...), custom_call_target="tpu_custom_call" | custom-call | flops 20000000000 | bytes 15000000 | tf_op jit(solution)/shard_map/attn_fwd/pallas_call | solution.py:170
  133.6 4.2 fusion.51
  138.4 1.5 add_convert_fusion
  143.0 3.4 pad_maximum_fusion
  146.4 6.8 %slice.113 = bf16[16,160,1280]{2,1,0:T(8,128)(2,1)} slice(bf16[16,320,1280]{2,1,0:T(8,128)(2,1)} %bitcast.104), slice={[0:16], [160:320], [0:1280]} | slice | bytes 13107200 | tf_op jit(solution)/shard_map/slice | solution.py:550
  153.2 2.2 copy-done.8
  155.4 2.1 fusion.48
  157.9 5.2 %fusion.53 = f32[1024,1280]{1,0:T(8,128)} fusion(bf16[1024,1280]{1,0:T(8,128)(2,1)S(1)} %copy-done.21, bf16[1280,1280]{1,0:T(8,128)(2,1)S(1)} %bitcast.118), kind=kOutput, calls=%fused_computation.142 | convolution fusion | flops 3355443200 | bytes 11141120 | tf_op jit(solution)/shard_map/dot_general | solution.py:43
  163.1 5.3 %fusion.52 = f32[1024,1280]{1,0:T(8,128)} fusion(bf16[1024,1280]{1,0:T(8,128)(2,1)S(1)} %copy-done.21, bf16[1280,1280]{1,0:T(8,128)(2,1)S(1)} %bitcast.121), kind=kOutput, calls=%fused_computation.141 | convolution fusion | flops 3355443200 | bytes 11141120 | tf_op jit(solution)/shard_map/dot_general | solution.py:43
  168.5 14.3 %fusion.49 = (f32[2560]{0:T(1024)}, bf16[1024,2560]{1,0:T(8,128)(2,1)}) fusion(f32[2560]{0:T(1024)S(1)} %add.264, f32[1024,1280]{1,0:T(8,128)} %fusion.53, f32[1024,1280]{1,0:T(8,128)} %fusion.52, bf16[2560,1280]{1,0:T(8,128)(2,1)S(1)} %bitcast.108, bf16[512,1280]{1,0:T(8,128)(2,1)} %collective-permute-done.6, bf16[512,1280]{1,0:T(8,128)(2,1)} %bitcast.18), kind=kOutput, calls=%fused_computation.138 | convolution fusion | flops 6750205440 | bytes 24924160 | tf_op jit(solution)/shard_map/dot_general | solution.py:43
  182.7 12.5 %fusion.55 = f32[1280,2560]{1,0:T(8,128)} fusion(bf16[1024,1280]{1,0:T(8,128)(2,1)S(1)} %copy-done.22, bf16[1024,2560]{1,0:T(8,128)(2,1)} %get-tuple-element.88), kind=kOutput, calls=%fused_computation.144 | convolution fusion | flops 6710886400 | bytes 20971520 | tf_op jit(solution)/shard_map/dot_general | solution.py:43
  195.7 5.5 %multiply_convert_fusion = bf16[1024,2560]{1,0:T(8,128)(2,1)S(1)} fusion(f32[1024,1280]{1,0:T(8,128)} %fusion.53, f32[1024,1280]{1,0:T(8,128)} %fusion.52, f32[2560]{0:T(1024)S(1)} %add.264), kind=kLoop, calls=%fused_computation.7 | loop fusion | flops 18350080 | bytes 15738880 | tf_op jit(solution)/shard_map/convert_element_type | solution.py:553
  201.3 2.3 copy-done.13
  203.6 11.8 %fusion.13 = f32[2560,1280]{1,0:T(8,128)} fusion(bf16[1024,2560]{1,0:T(8,128)(2,1)S(1)} %multiply_convert_fusion, bf16[512,1280]{1,0:T(8,128)(2,1)} %collective-permute-done.6, bf16[512,1280]{1,0:T(8,128)(2,1)} %bitcast.18), kind=kOutput, calls=%fused_computation.34 | convolution fusion | flops 6716129280 | bytes 20971520 | tf_op jit(solution)/shard_map/dot_general | solution.py:43
  215.4 6.4 %fusion.7 = f32[1024,1280]{1,0:T(8,128)S(1)} fusion(bf16[1280,1280]{1,0:T(8,128)(2,1)} %bitcast.120, bf16[1024,2560]{1,0:T(8,128)(2,1)} %get-tuple-element.88), kind=kOutput, calls=%fused_computation.16 | convolution fusion | flops 3355443200 | bytes 11141120 | tf_op jit(solution)/shard_map/dot_general | solution.py:43
  221.9 5.5 %convolution_add_fusion = f32[1024,1280]{1,0:T(8,128)S(1)} fusion(f32[1024,1280]{1,0:T(8,128)S(1)} %fusion.7, bf16[1280,1280]{1,0:T(8,128)(2,1)S(1)} %bitcast.119, bf16[1024,2560]{1,0:T(8,128)(2,1)} %get-tuple-element.88), kind=kOutput, calls=%fused_computation.9 | convolution fusion | flops 3356753920 | bytes 16384000 | tf_op jit(solution)/shard_map/dot_general | solution.py:43
  227.4 1.8 slice.147
  229.2 1.4 copy-done.12
  231.1 6.9 %fusion.54 = f32[1024,1280]{1,0:T(8,128)S(1)} fusion(bf16[1024,2560]{1,0:T(8,128)(2,1)S(1)} %bitcast.113, bf16[2560,1280]{1,0:T(8,128)(2,1)S(1)} %bitcast.111), kind=kOutput, calls=%fused_computation.143 | convolution fusion | flops 6710886400 | bytes 17039360 | tf_op jit(solution)/shard_map/dot_general | solution.py:43
  238.0 1.8 slice.142
  239.8 1.4 copy-done.11
  241.6 1.5 convert_reduce_fusion
  246.7 2.4 copy.37
  249.9 4.7 multiply_reduce_fusion
  254.7 4.6 fusion.47
  259.3 3.0 convolution_convert_fusion
  262.3 53.7 %attn_bwd.1 = (f32[2,40,1280]{2,1,0:T(8,128)}, f32[2,40,1280]{2,1,0:T(8,128)}, f32[2,40,1280]{2,1,0:T(8,128)}) custom-call(s32[2]{0:T(128)} %len_ref.3, bf16[2,1024,128]{2,1,0:T(8,128)(2,1)} %and_convert_fusion.ohk_ref, bf16[2,256,128]{2,1,0:T(8,128)(2,1)} %get-tuple-element.102.ohq_ref, f32[2,40,1280]{2,1,0:T(8,128)} %get-tuple-element.97.tq_ref, ...), custom_call_target="tpu_custom_call" | custom-call | flops 20000000000 | bytes 15000000 | tf_op jit(solution)/shard_map/attn_bwd/pallas_call | solution.py:178
  319.4 1.4 maximum_maximum_fusion
  321.5 2.3 collective-permute-start.10
  324.2 4.6 fusion.14.d_out_ref
  328.8 2.4 collective-permute-done.8
  331.2 7.1 %collective-permute-done.9 = f32[80,1024]{1,0:T(8,128)S(1)} collective-permute-done((f32[80,1024]{1,0:T(8,128)S(1)}, f32[80,1024]{1,0:T(8,128)S(1)}, u32[]{:S(2)}, u32[]{:S(2)}) %collective-permute-start.9) | collective-permute-done | bytes 327712 | tf_op jit(solution)/shard_map/ppermute | solution.py:577
  338.5 2.6 fusion.30
  341.8 4.6 fusion.34.d_qkv_ref
  346.4 85.1 %reduce_oq.1 = (f32[40,1280]{1,0:T(8,128)}, f32[40,4096]{1,0:T(8,128)}) custom-call(f32[16,2,40,1280]{3,2,1,0:T(8,128)} %fusion.14.d_out_ref, f32[16,2,40,1024]{3,2,1,0:T(8,128)} %fusion.34.d_qkv_ref), custom_call_target="tpu_custom_call" | custom-call | flops 20000000000 | bytes 15000000 | tf_op jit(solution)/shard_map/reduce_oq/pallas_call | solution.py:346
  433.9 36.9 %reduce_last.1 = (f32[4,80,640]{2,1,0:T(8,128)S(1)}, f32[4,40,1280]{2,1,0:T(8,128)S(1)}, f32[2,48,640]{2,1,0:T(8,128)S(1)}) custom-call(f32[4,80,640]{2,1,0:T(8,128)S(1)} %bitcast.95, f32[4,40,1280]{2,1,0:T(8,128)S(1)} %bitcast.98, f32[48,1280]{1,0:T(8,128)S(1)} %concatenate.35.small_ref), custom_call_target="tpu_custom_call" | custom-call | tf_op jit(solution)/shard_map/reduce_last/pallas_call | solution.py:471
  472.1 1.9 slice.124
  474.0 1.5 reshape.390
  482.1 2.7 reshape.392
  (254 shorter events, 42.7 us)
Async XLA Ops:
  7.2 7.8 %copy-start.46 = (f32[9,40]{1,0:T(8,128)S(1)}, f32[9,40]{1,0:T(8,128)}, u32[]{:S(2)}) copy-start(f32[9,40]{1,0:T(8,128)} %param.13) | copy-start | bytes 4324
  7.2 8.3 %copy-start.48 = (f32[160]{0:T(256)S(1)}, f32[160]{0:T(256)}, u32[]{:S(2)}) copy-start(f32[160]{0:T(256)} %param.17) | copy-start | bytes 1924
  7.2 139.2 %all-gather.3.cloned.1.call-start = ((), (), s32[]{:S(2)}) async-start(), calls=%async_computation.4 | async-start | bytes 13926400 | tf_op jit(solution)/shard_map/all_gather | solution.py:502
  7.2 8.9 %copy-start.29 = (bf16[160,1280]{1,0:T(8,128)(2,1)S(1)}, bf16[160,1280]{1,0:T(8,128)(2,1)}, u32[]{:S(2)}) copy-start(bf16[160,1280]{1,0:T(8,128)(2,1)} %param.18) | copy-start | bytes 1228804
  13.1 4.1 copy-start.30
  13.5 2.5 collective-permute-start
  17.1 414.4 %reduce-scatter.3.cloned.1.call-start = ((), (), s32[]{:S(2)}) async-start(), calls=%async_computation.2 | async-start | bytes 13926400 | tf_op jit(solution)/shard_map/reduce_scatter | solution.py:593
  17.3 53.0 %copy-start.9 = (f32[33,1280]{1,0:T(8,128)}, f32[33,1280]{1,0:T(8,128)S(1)}, u32[]{:S(2)}) copy-start(f32[33,1280]{1,0:T(8,128)S(1)} %convert_element_type.68) | copy-start | bytes 506884
  20.8 49.0 %copy-start.49 = (s32[2]{0:T(128)S(1)}, s32[2]{0:T(128)}, u32[]{:S(2)}) copy-start(s32[2]{0:T(128)} %len_ref.3) | copy-start | bytes 28
  73.0 18.4 %collective-permute-start.2 = (f32[80,1024]{1,0:T(8,128)}, f32[80,1024]{1,0:T(8,128)S(1)}, u32[]{:S(2)}, u32[]{:S(2)}) collective-permute-start(f32[80,1024]{1,0:T(8,128)} %get-tuple-element.105), channel_id=1, source_target_pairs={{0,64},{32,96},{64,0},{96,32},{1,65},{33,97},{65,1},{97,33},{2,66}... | collective-permute-start | bytes 983048 | tf_op jit(solution)/shard_map/ppermute | solution.py:530
  75.0 16.3 %copy-start.17 = (f32[80,4096]{1,0:T(8,128)S(1)}, f32[80,4096]{1,0:T(8,128)}, u32[]{:S(2)}) copy-start(f32[80,4096]{1,0:T(8,128)} %copy-done.16) | copy-start | bytes 3932164
  75.0 16.3 %collective-permute-start.1 = (f32[80,1024]{1,0:T(8,128)}, f32[80,1024]{1,0:T(8,128)S(1)}, u32[]{:S(2)}, u32[]{:S(2)}) collective-permute-start(f32[80,1024]{1,0:T(8,128)} %get-tuple-element.105), channel_id=1, source_target_pairs={{0,32},{32,64},{64,96},{96,0},{1,33},{33,65},{65,97},{97,1},{2,34}... | collective-permute-start | bytes 983048 | tf_op jit(solution)/shard_map/ppermute | solution.py:530
  75.3 16.1 %collective-permute-start.3 = (f32[80,1024]{1,0:T(8,128)}, f32[80,1024]{1,0:T(8,128)S(1)}, u32[]{:S(2)}, u32[]{:S(2)}) collective-permute-start(f32[80,1024]{1,0:T(8,128)} %get-tuple-element.105), channel_id=1, source_target_pairs={{0,96},{32,0},{64,32},{96,64},{1,97},{33,1},{65,33},{97,65},{2,98}... | collective-permute-start | bytes 983048 | tf_op jit(solution)/shard_map/ppermute | solution.py:530
  78.1 13.4 %copy-start.42 = (s32[2,256]{1,0:T(2,128)}, s32[2,256]{1,0:T(2,128)S(1)}, u32[]{:S(2)}) copy-start(s32[2,256]{1,0:T(2,128)S(1)} %get-tuple-element.84) | copy-start | bytes 6148
  78.9 12.6 %copy-start.27 = (pred[2,256,128]{2,1,0:T(32,128)(4,1)}, pred[2,256,128]{2,1,0:T(32,128)(4,1)S(1)}, u32[]{:S(2)}) copy-start(pred[2,256,128]{2,1,0:T(32,128)(4,1)S(1)} %get-tuple-element.103) | copy-start | bytes 196612
  92.6 40.9 %copy-start.5 = (bf16[4,4,2,40,1280]{4,3,2,1,0:T(8,128)(2,1)S(1)}, bf16[4,4,2,40,1280]{4,3,2,1,0:T(8,128)(2,1)}, u32[]{:S(2)}) copy-start(bf16[4,4,2,40,1280]{4,3,2,1,0:T(8,128)(2,1)} %copy-done.4) | copy-start | bytes 9830404
  140.0 3.0 collective-permute-start.4
  140.3 28.2 %collective-permute-start.6 = (bf16[512,1280]{1,0:T(8,128)(2,1)}, bf16[512,1280]{1,0:T(8,128)(2,1)}, u32[]{:S(2)}, u32[]{:S(2)}) collective-permute-start(bf16[512,1280]{1,0:T(8,128)(2,1)} %bitcast.18), channel_id=1, source_target_pairs={{0,1},{1,0},{2,3},{3,2},{4,5},{5,4},{6,7},{7,6},{8,9},{9,8},{10,11... | collective-permute-start | bytes 3932168 | tf_op jit(solution)/shard_map/ppermute | solution.py:509
  146.4 9.0 %copy-start.8 = (bf16[5120,1280]{1,0:T(8,128)(2,1)S(1)}, bf16[5120,1280]{1,0:T(8,128)(2,1)}, u32[]{:S(2)}) copy-start(bf16[5120,1280]{1,0:T(8,128)(2,1)} %all-gather.3.cloned.1.call-done) | copy-start | bytes 39321604
  157.5 5.6 %copy-start.18 = (bf16[16,80,1280]{2,1,0:T(8,128)(2,1)}, bf16[16,80,1280]{2,1,0:T(8,128)(2,1)S(1)}, u32[]{:S(2)}) copy-start(bf16[16,80,1280]{2,1,0:T(8,128)(2,1)S(1)} %get-tuple-element.86) | copy-start | bytes 9830404
  157.9 5.2 %copy-start.20 = (bf16[16,80,1280]{2,1,0:T(8,128)(2,1)S(1)}, bf16[16,80,1280]{2,1,0:T(8,128)(2,1)}, u32[]{:S(2)}) copy-start(bf16[16,80,1280]{2,1,0:T(8,128)(2,1)} %get-tuple-element.85) | copy-start | bytes 9830404
  157.9 10.6 %slice-start = ((s8[6553600]{0:T(1024)(128)(4,1)}), s8[4194304]{0:T(1024)(128)(4,1)S(1)}, s32[]{:S(2)}) async-start(s8[6553600]{0:T(1024)(128)(4,1)} %bitcast.106), calls=%async_computation.5 | async-start | bytes 8388608
  163.1 5.3 %slice-start.1 = ((s8[6553600]{0:T(1024)(128)(4,1)}), s8[2359296]{0:T(1024)(128)(4,1)S(1)}, s32[]{:S(2)}) async-start(s8[6553600]{0:T(1024)(128)(4,1)} %bitcast.106), calls=%async_computation.6 | async-start | bytes 4718592
  168.5 14.3 %copy-start.22 = (bf16[1024,1280]{1,0:T(8,128)(2,1)S(1)}, bf16[1024,1280]{1,0:T(8,128)(2,1)}, u32[]{:S(2)}) copy-start(bf16[1024,1280]{1,0:T(8,128)(2,1)} %pad_maximum_fusion) | copy-start | bytes 7864324
  195.2 237.5 %reduce-scatter.5.cloned.1.call-start = ((), (), s32[]{:S(2)}) async-start(), calls=%async_computation.3 | async-start | bytes 13926400 | tf_op jit(solution)/shard_map/reduce_scatter | solution.py:592
  215.4 6.5 %copy-start.19 = (bf16[16,80,1280]{2,1,0:T(8,128)(2,1)S(1)}, bf16[16,80,1280]{2,1,0:T(8,128)(2,1)}, u32[]{:S(2)}) copy-start(bf16[16,80,1280]{2,1,0:T(8,128)(2,1)} %copy-done.18) | copy-start | bytes 9830404
  215.4 15.6 %slice-start.2 = ((s8[6553600]{0:T(1024)(128)(4,1)}), s8[4194304]{0:T(1024)(128)(4,1)S(1)}, s32[]{:S(2)}) async-start(s8[6553600]{0:T(1024)(128)(4,1)} %bitcast.109), calls=%async_computation.7 | async-start | bytes 8388608
  215.4 15.6 %slice-start.4 = ((s8[5242880]{0:T(1024)(128)(4,1)}), s8[4194304]{0:T(1024)(128)(4,1)S(1)}, s32[]{:S(2)}) async-start(s8[5242880]{0:T(1024)(128)(4,1)} %bitcast.112), calls=%async_computation.9 | async-start | bytes 8388608
  221.9 9.2 %slice-start.3 = ((s8[6553600]{0:T(1024)(128)(4,1)}), s8[2359296]{0:T(1024)(128)(4,1)S(1)}, s32[]{:S(2)}) async-start(s8[6553600]{0:T(1024)(128)(4,1)} %bitcast.109), calls=%async_computation.8 | async-start | bytes 4718592
  221.9 9.2 %slice-start.5 = ((s8[5242880]{0:T(1024)(128)(4,1)}), s8[1048576]{0:T(1024)(128)(4,1)S(1)}, s32[]{:S(2)}) async-start(s8[5242880]{0:T(1024)(128)(4,1)} %bitcast.112), calls=%async_computation.10 | async-start | bytes 2097152
  230.6 19.4 %collective-permute-start.7 = (f32[512,1280]{1,0:T(8,128)}, f32[512,1280]{1,0:T(8,128)}, u32[]{:S(2)}, u32[]{:S(2)}) collective-permute-start(f32[512,1280]{1,0:T(8,128)} %slice.147), channel_id=1, source_target_pairs={{0,1},{1,0},{2,3},{3,2},{4,5},{5,4},{6,7},{7,6},{8,9},{9,8},{10,11... | collective-permute-start | bytes 7864328 | tf_op jit(solution)/shard_map/ppermute | solution.py:564
  238.0 7.3 %copy-start.43 = (s32[2,256]{1,0:T(2,128)S(1)}, s32[2,256]{1,0:T(2,128)}, u32[]{:S(2)}) copy-start(s32[2,256]{1,0:T(2,128)} %copy-done.42) | copy-start | bytes 6148
  241.2 13.5 %collective-permute-start.5 = (f32[512,1280]{1,0:T(8,128)}, f32[512,1280]{1,0:T(8,128)}, u32[]{:S(2)}, u32[]{:S(2)}) collective-permute-start(f32[512,1280]{1,0:T(8,128)} %slice.142), channel_id=1, source_target_pairs={{0,1},{1,0},{2,3},{3,2},{4,5},{5,4},{6,7},{7,6},{8,9},{9,8},{10,11... | collective-permute-start | bytes 7864328 | tf_op jit(solution)/shard_map/ppermute | solution.py:556
  249.9 4.8 copy-start.7
  249.9 4.8 copy-start.37
  317.1 7.0 %copy-start.15 = (bf16[512,1280]{1,0:T(8,128)(2,1)S(1)}, bf16[512,1280]{1,0:T(8,128)(2,1)}, u32[]{:S(2)}) copy-start(bf16[512,1280]{1,0:T(8,128)(2,1)} %copy-done.14) | copy-start | bytes 3932164
  317.1 7.0 %copy-start.24 = (bf16[1280,512]{1,0:T(8,128)(2,1)S(1)}, bf16[1280,512]{1,0:T(8,128)(2,1)}, u32[]{:S(2)}) copy-start(bf16[1280,512]{1,0:T(8,128)(2,1)} %copy.37) | copy-start | bytes 3932164
  320.8 10.4 %collective-permute-start.8 = (f32[80,1024]{1,0:T(8,128)S(1)}, f32[80,1024]{1,0:T(8,128)S(1)}, u32[]{:S(2)}, u32[]{:S(2)}) collective-permute-start(f32[80,1024]{1,0:T(8,128)S(1)} %get-tuple-element.90), channel_id=1, source_target_pairs={{0,32},{32,64},{64,96},{96,0},{1,33},{33,65},{65,97},{97,1},{2,34}... | collective-permute-start | bytes 983048 | tf_op jit(solution)/shard_map/ppermute | solution.py:577
  321.5 9.7 %collective-permute-start.10 = (f32[80,1024]{1,0:T(8,128)S(1)}, f32[80,1024]{1,0:T(8,128)S(1)}, u32[]{:S(2)}, u32[]{:S(2)}) collective-permute-start(f32[80,1024]{1,0:T(8,128)S(1)} %get-tuple-element.91), channel_id=1, source_target_pairs={{0,96},{32,0},{64,32},{96,64},{1,97},{33,1},{65,33},{97,65},{2,98}... | collective-permute-start | bytes 983048 | tf_op jit(solution)/shard_map/ppermute | solution.py:577
  323.8 14.6 %collective-permute-start.9 = (f32[80,1024]{1,0:T(8,128)S(1)}, f32[80,1024]{1,0:T(8,128)S(1)}, u32[]{:S(2)}, u32[]{:S(2)}) collective-permute-start(f32[80,1024]{1,0:T(8,128)S(1)} %get-tuple-element.92), channel_id=1, source_target_pairs={{0,64},{32,96},{64,0},{96,32},{1,65},{33,97},{65,1},{97,33},{2,66}... | collective-permute-start | bytes 983048 | tf_op jit(solution)/shard_map/ppermute | solution.py:577
  324.1 14.3 %copy-start.1 = (bf16[4,4,2,40,1024]{4,3,2,1,0:T(8,128)(2,1)S(1)}, bf16[4,4,2,40,1024]{4,3,2,1,0:T(8,128)(2,1)}, u32[]{:S(2)}) copy-start(bf16[4,4,2,40,1024]{4,3,2,1,0:T(8,128)(2,1)} %copy-done) | copy-start | bytes 7864324
  324.1 14.3 %copy-start.10 = (f32[33,1280]{1,0:T(8,128)S(1)}, f32[33,1280]{1,0:T(8,128)}, u32[]{:S(2)}) copy-start(f32[33,1280]{1,0:T(8,128)} %copy-done.9) | copy-start | bytes 506884
  324.1 14.3 %copy-start.34 = (f32[1280]{0:T(1024)S(1)}, f32[1280]{0:T(1024)}, u32[]{:S(2)}) copy-start(f32[1280]{0:T(1024)} %copy-done.33) | copy-start | bytes 15364
  324.1 14.3 %copy-start.36 = (f32[2,33]{1,0:T(2,128)S(1)}, f32[2,33]{1,0:T(2,128)}, u32[]{:S(2)}) copy-start(f32[2,33]{1,0:T(2,128)} %copy-done.35) | copy-start | bytes 796
  324.1 14.3 %copy-start.40 = (f32[2,33]{1,0:T(2,128)S(1)}, f32[2,33]{1,0:T(2,128)}, u32[]{:S(2)}) copy-start(f32[2,33]{1,0:T(2,128)} %copy-done.39) | copy-start | bytes 796
  324.1 14.3 %copy-start.45 = (f32[2,33]{1,0:T(2,128)S(1)}, f32[2,33]{1,0:T(2,128)}, u32[]{:S(2)}) copy-start(f32[2,33]{1,0:T(2,128)} %copy-done.44) | copy-start | bytes 796
  328.8 12.4 %copy-start.28 = (pred[2,256,128]{2,1,0:T(32,128)(4,1)S(1)}, pred[2,256,128]{2,1,0:T(32,128)(4,1)}, u32[]{:S(2)}) copy-start(pred[2,256,128]{2,1,0:T(32,128)(4,1)} %copy-done.27) | copy-start | bytes 196612
  471.7 7.3 %collective-permute-start.11 = (f32[40,2560]{1,0:T(8,128)}, f32[40,2560]{1,0:T(8,128)}, u32[]{:S(2)}, u32[]{:S(2)}) collective-permute-start(f32[40,2560]{1,0:T(8,128)} %constant_dynamic-slice_fusion.1), channel_id=1, source_target_pairs={{0,1},{1,0},{2,3},{3,2},{4,5},{5,4},{6,7},{7,6},{8,9},{9,8},{10,11... | collective-permute-start | bytes 1228808 | tf_op jit(solution)/shard_map/ppermute | solution.py:605
  (23 other events, 52.4 us)
Sparse Core Ops, SparseCore 0:
  17.2 104.7 all-gather.2
  195.3 93.1 reduce-scatter.2
  292.0 107.8 reduce-scatter.4

commit v4 on v3

--- a/solution.py
+++ b/solution.py
@@ -99,18 +99,20 @@
 
 def attn_fwd_kernel(len_ref, ohk_ref, ohq_ref, tq_ref, tk_ref, tv_ref, csk_ref, csq_ref, o_ref, lse_ref):
     q, k, v = expand_qkv(ohk_ref, ohq_ref, tq_ref, tk_ref, tv_ref, csk_ref, csq_ref)
-    key_ok = key_mask(len_ref[pl.program_id(0)])
-    v_t = v.T
-    outs = []
-    for head, mine in enumerate(head_masks()):
+    key_ok = lax.broadcasted_iota(jnp.int32, (QLEN, SEQ), 1) < len_ref[pl.program_id(0)]
+    outs, stats = [], []
+    for mine in head_masks():
         q_h = jnp.where(mine, q, 0.0).astype(BF16)
-        s = jnp.where(key_ok, mm(k, q_h, NT), NEG_BIG)
-        top = jnp.max(s, axis=0, keepdims=True)
+        s = jnp.where(key_ok, mm(q_h, k, NT), NEG_BIG)
+        top = jnp.max(s, axis=-1, keepdims=True)
         e = jnp.exp(s - top)
-        total = jnp.sum(e, axis=0, keepdims=True)
-        outs.append(mm(v_t[head_cols(head)], e.astype(BF16)) / total)
-        lse_ref[0, 0, head:head + 1, :] = top + jnp.log(total)
-    o_ref[0] = jnp.concatenate(outs, axis=0).T.astype(BF16)
+        total = jnp.sum(e, axis=-1, keepdims=True)
+        outs.append(mm(e.astype(BF16), v) / total)
+        stats.append(jnp.broadcast_to(top + jnp.log(total), (QLEN, LANES)))
+    low = head_masks()[0]
+    o_ref[0] = jnp.where(low, *outs).astype(BF16)
+    stats = jnp.where(low, *stats).T
+    lse_ref[0, 0, :2, :] = jnp.concatenate([stats[:1], stats[HDIM:HDIM + 1]], axis=0)
 
 
 def attn_bwd_kernel(len_ref, ohk_ref, ohq_ref, tq_ref, tk_ref, tv_ref, csk_ref, csq_ref, okt_ref, oqt_ref, do_ref, lse_ref, sq_ref, sk_ref, sv_ref):
@@ -274,6 +276,7 @@
 
 
 CUT = 24
+UP_R = 80
 HALF_W = 1152
 WIDE = DIM + QCOLS
 
@@ -282,18 +285,24 @@
     return pl.ds(0, CUT) if half == LO else pl.ds(CUT, ROWS - CUT)
 
 
+def up_rows(half):
+    return pl.ds(UP_R // 2 * half, UP_R // 2)
+
+
 def ring_bufs(lead, width):
     return [pltpu.VMEM(lead + (CUT if i in (0, 3, 4) else ROWS - CUT, width), F32) for i in range(6)]
 
 
-def oq_kernel(d_out_ref, d_qkv_ref, out_ref, qkv_ref, acc, one_a, one_b, gath, *rest):
-    bufs, ports = [rest[6 * i:6 * i + 6] for i in range(4)], ports_of(*rest[-2:])
+def oq_kernel(d_out_ref, d_qkv_ref, down_ref, out_ref, qkv_ref, down_out, acc, one_a, one_b, gath, *rest):
+    bufs, ports = [rest[6 * i:6 * i + 6] for i in range(5)], ports_of(*rest[-2:])
     ci = lax.axis_index('c')
     meet()
     first = core_copy(d_out_ref.at[:, 1 - ci], acc.at[:, :, pl.ds(0, DIM)], ports)
     second = core_copy(d_qkv_ref.at[:, 1 - ci], acc.at[:, :, pl.ds(DIM, QCOLS)], ports)
     first.start()
     second.start()
+    xd, gd = Ring('x', ports), Ring('x', ports)
+    xd.rs_start(lambda k, h: down_ref.at[k, half_rows(h)], bufs[4])
     first.wait_recv()
 
     def add_out(i, carry):
@@ -311,8 +320,13 @@
     zb = Ring('z', ports)
     ya.rs_start(lambda k, h: grid.at[:, k, half_rows(h), pl.ds(0, HALF_W)], bufs[0])
     zb.rs_start(lambda k, h: grid.at[k, :, half_rows(h), pl.ds(HALF_W, HALF_W)], bufs[1])
+    xd.rs_mid()
     ya.rs_mid()
     zb.rs_mid()
+    low, high = xd.rs_end()
+    down_out[xd.me, half_rows(LO)] = low
+    down_out[xd.me, half_rows(HI)] = high
+    gd.ag_start(lambda k, h: down_out.at[k] if h == ALL else down_out.at[k, half_rows(h)])
     one_a[:, :CUT], one_a[:, CUT:] = ya.rs_end()
     za = Ring('z', ports)
     za.rs_start(lambda k, h: one_a.at[k, half_rows(h)], bufs[2])
@@ -321,6 +335,8 @@
     yb.rs_start(lambda k, h: one_b.at[k, half_rows(h)], bufs[3])
     za.rs_mid()
     yb.rs_mid()
+    gd.ag_mid()
+    gd.ag_end()
     xr = Ring('x', ports)
     low, high = za.rs_end()
     gath[xr.me, :CUT, :HALF_W] = low
@@ -342,17 +358,17 @@
     return [pl.BlockSpec(memory_space=pltpu.VMEM)] * n
 
 
-def reduce_oq(d_out, d_qkv):
+def reduce_oq(d_out, d_qkv, down):
     return pl.pallas_call(
-        oq_kernel, in_specs=vmem(2), out_specs=vmem(2),
-        out_shape=[jax.ShapeDtypeStruct((ROWS, DIM), F32), jax.ShapeDtypeStruct((ROWS, 4 * QCOLS), F32)],
+        oq_kernel, in_specs=vmem(3), out_specs=vmem(3),
+        out_shape=[jax.ShapeDtypeStruct((ROWS, DIM), F32), jax.ShapeDtypeStruct((ROWS, 4 * QCOLS), F32), jax.ShapeDtypeStruct((4, ROWS, DIM), F32)],
         scratch_shapes=[pltpu.VMEM((16, ROWS, WIDE), F32), pltpu.VMEM((4, ROWS, HALF_W), F32), pltpu.VMEM((4, ROWS, HALF_W), F32),
                         pltpu.VMEM((4, ROWS, WIDE), F32)]
-        + ring_bufs((4,), HALF_W) + ring_bufs((4,), HALF_W) + ring_bufs((), HALF_W) + ring_bufs((), HALF_W)
-        + [pltpu.SemaphoreType.DMA((30,)), pltpu.SemaphoreType.DMA((30,))],
+        + ring_bufs((4,), HALF_W) + ring_bufs((4,), HALF_W) + ring_bufs((), HALF_W) + ring_bufs((), HALF_W) + ring_bufs((), DIM)
+        + [pltpu.SemaphoreType.DMA((40,)), pltpu.SemaphoreType.DMA((40,))],
         compiler_params=pltpu.CompilerParams(collective_id=1, has_side_effects=True, vmem_limit_bytes=56 * 1024 * 1024),
         cost_estimate=COST,
-        name='reduce_oq')(d_out, d_qkv)
+        name='reduce_oq')(d_out, d_qkv, down)
 
 
 def first_kernel(wq_ref, wo_ref, pack_ref, tok_ref, gq, go, gp, gt, sends, recvs):
@@ -402,22 +418,16 @@
 
 
 SMALL = 48
-UP_R = 80
-
-
-def last_kernel(up_ref, down_ref, small_ref, up_out, down_out, small_out, pair, sum_y, sum_z, sum_x, *rest):
-    bufs, ports = [rest[6 * i:6 * i + 6] for i in range(2)], ports_of(*rest[-2:])
+
+
+def last_kernel(up_ref, small_ref, up_out, small_out, pair, sum_y, sum_z, sum_x, *rest):
+    bufs, ports = rest[:6], ports_of(*rest[-2:])
     ci = lax.axis_index('c')
     meet()
-
-    def up_rows(half):
-        return pl.ds(40 * half, 40)
     swap = core_copy(small_ref, pair, ports)
     swap.start()
     xu = Ring('x', ports)
-    xd = Ring('x', ports)
-    xu.rs_start(lambda k, h: up_ref.at[k, up_rows(h)], bufs[0])
-    xd.rs_start(lambda k, h: down_ref.at[k, half_rows(h)], bufs[1])
+    xu.rs_start(lambda k, h: up_ref.at[k, up_rows(h)], bufs)
     swap.wait_recv()
     both = small_ref[...] + pair[...]
     mine = jnp.where(ci == 0, both[:, 0:HALF_D], both[:, HALF_D:1280])
@@ -431,50 +441,42 @@
     sum_y[ys.me] = mine
     ys.ag_start(gather(sum_y))
     xu.rs_mid()
-    xd.rs_mid()
     ys.ag_mid()
     ys.ag_end()
     zs = Ring('z', ports)
     sum_z[zs.me] = total(sum_y)
     zs.ag_start(gather(sum_z))
     low, high = xu.rs_end()
-    up_out[xu.me, 0:40] = low
-    up_out[xu.me, 40:80] = high
+    up_out[xu.me, up_rows(LO)] = low
+    up_out[xu.me, up_rows(HI)] = high
     gu = Ring('x', ports)
     gu.ag_start(lambda k, h: up_out.at[k] if h == ALL else up_out.at[k, up_rows(h)])
-    low, high = xd.rs_end()
-    down_out[xd.me, :CUT] = low
-    down_out[xd.me, CUT:] = high
-    gd = Ring('x', ports)
-    gd.ag_start(lambda k, h: down_out.at[k] if h == ALL else down_out.at[k, half_rows(h)])
     zs.ag_mid()
     zs.ag_end()
     xs = Ring('x', ports)
     sum_x[xs.me] = total(sum_z)
     xs.ag_start(gather(sum_x))
     gu.ag_mid()
-    gd.ag_mid()
     xs.ag_mid()
     xs.ag_end()
     small_out[ci] = total(sum_x)
     back = core_copy(small_out.at[ci], small_out.at[ci], ports)
     back.start()
     gu.ag_end()
-    gd.ag_end()
     back.wait_recv()
     back.wait_send()
     swap.wait_send()
 
 
-def reduce_last(up, down, small):
-    up_bufs = [pltpu.VMEM((40, HALF_D), F32) for _ in range(6)]
+def reduce_last(up, small):
+    up_bufs = [pltpu.VMEM((UP_R // 2, HALF_D), F32) for _ in range(6)]
     return pl.pallas_call(
-        last_kernel, in_specs=vmem(3), out_specs=vmem(3),
-        out_shape=[jax.ShapeDtypeStruct((4, UP_R, HALF_D), F32), jax.ShapeDtypeStruct((4, ROWS, DIM), F32), jax.ShapeDtypeStruct((2, SMALL, HALF_D), F32)],
-        scratch_shapes=[pltpu.VMEM((SMALL, DIM), F32)] + [pltpu.VMEM((4, SMALL, HALF_D), F32)] * 3 + up_bufs + ring_bufs((), DIM)
+        last_kernel, in_specs=vmem(2), out_specs=vmem(2),
+        out_shape=[jax.ShapeDtypeStruct((4, UP_R, HALF_D), F32), jax.ShapeDtypeStruct((2, SMALL, HALF_D), F32)],
+        scratch_shapes=[pltpu.VMEM((SMALL, DIM), F32)] + [pltpu.VMEM((4, SMALL, HALF_D), F32)] * 3 + up_bufs
         + [pltpu.SemaphoreType.DMA((34,)), pltpu.SemaphoreType.DMA((34,))],
         compiler_params=pltpu.CompilerParams(collective_id=2, has_side_effects=True, vmem_limit_bytes=40 * 1024 * 1024),
-        name='reduce_last')(up, down, small)
+        name='reduce_last')(up, small)
 
 
 def one_hot3(tok):
@@ -497,9 +499,9 @@
         up_send = lax.dynamic_index_in_dim(up_loc, 1 - ci, axis=2, keepdims=False).reshape(ROWS, FFH)
         up_recv = lax.ppermute(up_send, 'c', SWAP)
         up_pair = jnp.concatenate([jnp.where(ci == 0, up_mine, up_recv), jnp.where(ci == 0, up_recv, up_mine)], axis=0)
-        shard = jnp.concatenate([up_pair[:, :DIM], up_pair[:, DIM:], w_down], axis=0)
-        shard, packed = lax.optimization_barrier((shard, packed))
-        gathered = lax.all_gather(shard, CHIP, axis=0, tiled=False)
+        up_pair, packed = lax.optimization_barrier((up_pair, packed))
+        up_w = lax.all_gather(up_pair, CHIP, axis=0, tiled=True)
+        down_w = lax.all_gather(w_down, CHIP, axis=0, tiled=True)
         qkv_w, out_w, packed, tok_all = gather_first(wq_loc, w_out, packed, tokens.reshape(4, LANES))
         qkv_w, out_w, packed = qkv_w.reshape(DIM, QCOLS), out_w.reshape(DIM, DIM), packed.reshape(32, 8 * LANES)
         tok_all = tok_all.reshape(4, 2, QLEN).transpose(1, 0, 2).reshape(2, SEQ)
@@ -544,11 +546,8 @@
         xhat2, inv2 = ln_stats(x1)
         nm = (xhat2 * vecs[6] + vecs[7]).astype(BF16)
         nm2 = jnp.concatenate([nm, lax.ppermute(nm, 'c', SWAP)], axis=0)
-        nm2, gathered = lax.optimization_barrier((nm2, gathered))
-        up_w0 = gathered[:, 0:80].reshape(DIM, DIM)
-        up_w1 = gathered[:, 80:160].reshape(DIM, DIM)
-        down_w = gathered[:, 160:320].reshape(2 * DIM, DIM)
-        up_lin = jnp.concatenate([mm(nm2, up_w0), mm(nm2, up_w1)], axis=1) + up_b
+        nm2, up_w = lax.optimization_barrier((nm2, up_w))
+        up_lin = mm(nm2, up_w) + up_b
         cdf = 0.5 * (1.0 + lax.erf(up_lin * 0.7071067811865476))
         gelu_b = (up_lin * cdf).astype(BF16)
         slope = cdf + up_lin * (0.3989422804014327 * jnp.exp(-0.5 * up_lin * up_lin))
@@ -557,10 +556,11 @@
         layer_out = (x1 + down2[:TOK] + down_got + vecs[8]).astype(BF16).reshape(2, QLEN, DIM)
 
         d_down = mm(gelu_b, grad2, TN)
+        d_down, grad2 = lax.optimization_barrier((d_down, grad2))
         d_up_lin = mm(grad2, down_w, NT) * slope
         d_up_b = d_up_lin.astype(BF16)
         d_up = mm(nm2, d_up_b, TN)
-        d_nm2 = mm(d_up_b[:, :DIM], up_w0, NT) + mm(d_up_b[:, DIM:], up_w1, NT)
+        d_nm2 = mm(d_up_b, up_w, NT)
         d_nm = d_nm2[:TOK] + lax.ppermute(d_nm2[TOK:], 'c', SWAP)
         grad32 = grad_own.astype(F32)
         d_resid = grad32 + ln_back(d_nm, vecs[6], xhat2, inv2)
@@ -588,11 +588,12 @@
             jnp.sum(d_h * xhat1, axis=(0, 1))[None], jnp.sum(d_h, axis=(0, 1))[None], d_bqkv,
             jnp.sum(d_resid, axis=0)[None], jnp.sum(d_nm * xhat2, axis=0)[None], jnp.sum(d_nm, axis=0)[None],
             jnp.sum(grad32, axis=0)[None], d_up_bias, jnp.zeros((2, DIM), F32)], axis=0)
-        r_out, r_qkv = reduce_oq(d_outw.reshape(16, 2, ROWS, DIM), d_qkvw.reshape(16, 2, ROWS, QCOLS))
         r_down = lax.psum_scatter(d_down, CHIP, scatter_dimension=0, tiled=True)
         r_up = lax.psum_scatter(d_up, CHIP, scatter_dimension=0, tiled=True)
+        r_up = r_up.reshape(UP_R, 4, HALF_D).transpose(1, 0, 2)
+        r_out, r_qkv, r_down = reduce_oq(d_outw.reshape(16, 2, ROWS, DIM), d_qkvw.reshape(16, 2, ROWS, QCOLS), r_down.reshape(4, ROWS, DIM))
         small, r_out = lax.optimization_barrier((small, r_out))
-        r_up, r_down, small = reduce_last(r_up.reshape(2 * ROWS, 4, HALF_D).transpose(1, 0, 2), r_down.reshape(4, ROWS, DIM), small)
+        r_up, small = reduce_last(r_up, small)
         r_up = r_up.transpose(1, 0, 2).reshape(2 * ROWS, FFH)
         r_down = r_down.reshape(160, DIM)
         small = small.transpose(1, 0, 2).reshape(SMALL, DIM)

time: 502 us -> 467 us (0.930)
  Pallas kernels: 262 us -> 236 us
  local copies, waits for them, and re-layouts: 59.9 us -> 47.4 us
    pallas_call x2, Pallas kernels: 122 us -> 108 us  [the longest x1 75.9 us: reduce_oq(): pl.pallas_call(oq_kernel, in_specs=vmem(3), out_specs=vmem(3), out_shape=...]
    slice x2 -> x0, local copies, waits for them, and re-layouts: 8.9 us -> none  [the longest x1 6.76 us: local_step(): down_w = gathered[:, 160:320].reshape(2 * DIM, DIM)]
    pallas_call x1, Pallas kernels: 40.9 us -> 34.7 us  [attn_fwd(): pl.pallas_call(attn_fwd_kernel, grid=(2, PAIRS), in_specs=attn_specs(), o...]
    convert_element_type x1 -> x0, other arithmetic: 5.54 us -> none  [local_step(): gelu_b = (up_lin * cdf).astype(BF16)]
    pallas_call x1, Pallas kernels: 45.7 us -> 40.4 us  [gather_first(): pl.pallas_call(first_kernel, in_specs=vmem(4), out_specs=vmem(4), out_sha...]
    dot_general x12 -> x10, matrix products: 81 us -> 84.4 us  [mm(): return lax.dot_general(a, b, (dims, ((), ())), preferred_element_type=F32)]
    unnamed x119 -> x103, local copies, waits for them, and re-layouts: 16.4 us -> 15.3 us
  transfers between devices with their start and end apart: 15 -> 16, of which waited for: 5 -> 5; matrix products, arithmetic and copies ran while one was open for 27% -> 32% of each run, Pallas kernels for 46% -> 45%
where the time goes in v4:
time: 467 us; the launch traced here: 458 us
  Pallas kernels  236 us (51%)
  matrix products  94 us (20%)
  local copies, waits for them, and re-layouts  47.4 us (10%)
  other arithmetic  33.1 us (7%)
  waiting for transfers between devices  20.2 us (4%)
  between operations  15.2 us (3%)
  starting transfers between devices  11.8 us (3%)
    dot_general x10, matrix products, mm(): return lax.dot_general(a, b, (dims, ((), ())), preferred_element_type=F32)  84.4 us
    pallas_call x1, Pallas kernels, reduce_oq(): pl.pallas_call(oq_kernel, in_specs=vmem(3), out_specs=vmem(3), out_shape=...  75.9 us
    pallas_call x1, Pallas kernels, attn_bwd(): pl.pallas_call(attn_bwd_kernel, grid=(2, PAIRS), in_specs=attn_specs() +...  53.7 us
    pallas_call x1, Pallas kernels, gather_first(): pl.pallas_call(first_kernel, in_specs=vmem(4), out_specs=vmem(4), out_sha...  40.4 us
    pallas_call x1, Pallas kernels, attn_fwd(): pl.pallas_call(attn_fwd_kernel, grid=(2, PAIRS), in_specs=attn_specs(), o...  34.7 us
    pallas_call x1, Pallas kernels, reduce_last(): pl.pallas_call(last_kernel, in_specs=vmem(2), out_specs=vmem(2), out_shap...  31.6 us
    unnamed x103, local copies, waits for them, and re-layouts  15.3 us
    ppermute x3, waiting for transfers between devices, local_step(): lax.ppermute(part, 'x', [(i, (i + hop) % 4) for i in range(4)])  11.1 us
  transfers between devices with their start and end apart: 16, of which 5 were waited for; matrix products, arithmetic and copies ran while one was open for 32% of the time, Pallas kernels for 45%

profile of v4, /device:TPU:1, one launch (start us, length us, event | category | flops | bytes accessed | tf_op | source)
XLA Modules:
  0.0 458.0 jit_solution(10393240722854197664)
XLA Ops:
  7.2 1.7 reshape.353
  9.0 4.1 dynamic-slice_reduce_fusion.1
  13.5 1.4 collective-permute-start
  21.2 40.4 %gather_first.1 = (bf16[4,4,2,40,1024]{4,3,2,1,0:T(8,128)(2,1)S(1)}, bf16[4,4,2,40,1280]{4,3,2,1,0:T(8,128)(2,1)S(1)}, f32[4,4,2,8,128]{4,3,2,1,0:T(8,128)S(1)}, s32[4,4,128]{2,1,0:T(4,128)S(1)}) custom-call(bf16[40,1024]{1,0:T(8,128)(2,1)S(1)} %pad_dynamic-slice_fusion.2.wq_ref, bf16[40,1280]{1,0:T(8,128)(2,1)S(1)} %copy-done.2, ...), custom_call_target="tpu_custom_call" | custom-call | flops 20000000000 | bytes 15000000 | tf_op jit(solution)/shard_map/gather_first/pallas_call | solution.py:411
  61.6 1.7 copy-done.3
  68.2 2.0 collective-permute-start.2
  70.2 1.3 collective-permute-start.3
  72.4 2.0 convolution_multiply_fusion
  74.4 1.1 and_convert_fusion.ohk_ref
  77.4 8.0 %collective-permute-done.1 = f32[80,1024]{1,0:T(8,128)S(1)} collective-permute-done((f32[80,1024]{1,0:T(8,128)S(1)}, f32[80,1024]{1,0:T(8,128)S(1)}, u32[]{:S(2)}, u32[]{:S(2)}) %collective-permute-start.1) | collective-permute-done | bytes 327712 | tf_op jit(solution)/shard_map/ppermute | solution.py:532
  87.0 34.7 %attn_fwd.1 = (bf16[2,256,1280]{2,1,0:T(8,128)(2,1)}, f32[2,10,8,256]{3,2,1,0:T(8,128)}) custom-call(s32[2]{0:T(128)} %len_ref.3, bf16[2,1024,128]{2,1,0:T(8,128)(2,1)} %and_convert_fusion.ohk_ref, bf16[2,256,128]{2,1,0:T(8,128)(2,1)} %get-tuple-element.102.ohq_ref, f32[2,40,1280]{2,1,0:T(8,128)} %get-tuple-element.97.tq_ref, ...), custom_call_target="tpu_custom_call" | custom-call | flops 20000000000 | bytes 15000000 | tf_op jit(solution)/shard_map/attn_fwd/pallas_call | solution.py:172
  121.7 4.2 fusion.45
  126.6 1.5 add_convert_fusion
  128.1 1.3 collective-permute-start.4
  131.9 3.5 pad_maximum_fusion.1
  135.3 3.4 pad_maximum_fusion
  138.7 12.7 %multiply_convert_fusion = (bf16[1024,2560]{1,0:T(8,128)(2,1)S(1)}, f32[1024,2560]{1,0:T(8,128)}) fusion(f32[2560]{0:T(1024)S(1)} %add.261, bf16[1024,1280]{1,0:T(8,128)(2,1)} %pad_maximum_fusion, bf16[1280,2560]{1,0:T(8,128)(2,1)} %all-gather.3.cloned.1.call-done), kind=kOutput, calls=%fused_computation.6 | convolution fusion | flops 6726615040 | bytes 24913920 | tf_op jit(solution)/shard_map/dot_general | solution.py:43
  151.4 2.3 copy-done.47
  153.7 11.7 %fusion.42 = f32[2560,1280]{1,0:T(8,128)} fusion(bf16[1024,2560]{1,0:T(8,128)(2,1)S(1)} %get-tuple-element.108, bf16[512,1280]{1,0:T(8,128)(2,1)} %collective-permute-done.6, bf16[512,1280]{1,0:T(8,128)(2,1)} %bitcast.14), kind=kOutput, calls=%fused_computation.127 | convolution fusion | flops 6716129280 | bytes 20971520 | tf_op jit(solution)/shard_map/dot_general | solution.py:43
  165.8 15.9 %fusion.46 = (f32[2560]{0:T(1024)}, bf16[1024,2560]{1,0:T(8,128)(2,1)S(1)}) fusion(f32[1024,2560]{1,0:T(8,128)} %get-tuple-element.109, f32[2560]{0:T(1024)S(1)} %add.261, bf16[1024,1280]{1,0:T(8,128)(2,1)} %pad_maximum_fusion.1, bf16[2560,1280]{1,0:T(8,128)(2,1)} %all-gather.5.cloned.1.call-done), kind=kOutput, calls=%fused_computation.131 | convolution fusion | flops 6742341120 | bytes 24924160 | tf_op jit(solution)/shard_map/dot_general | solution.py:43
  181.7 2.3 copy-done.46
  184.0 10.1 %fusion.11 = f32[1280,2560]{1,0:T(8,128)} fusion(bf16[1024,1280]{1,0:T(8,128)(2,1)S(1)} %copy-done.15, bf16[1024,2560]{1,0:T(8,128)(2,1)S(1)} %get-tuple-element.112), kind=kOutput, calls=%fused_computation.25 | convolution fusion | flops 6710886400 | bytes 20971520 | tf_op jit(solution)/shard_map/dot_general | solution.py:43
  194.1 10.8 %fusion.9 = f32[1024,1280]{1,0:T(8,128)S(1)} fusion(bf16[1280,2560]{1,0:T(8,128)(2,1)} %all-gather.3.cloned.1.call-done, bf16[1024,2560]{1,0:T(8,128)(2,1)} %copy-done.46), kind=kOutput, calls=%fused_computation.23 | convolution fusion | flops 6710886400 | bytes 17039360 | tf_op jit(solution)/shard_map/dot_general | solution.py:43
  205.0 1.8 slice.115
  206.7 1.4 copy-done.10
  208.1 10.8 %fusion.47 = f32[1024,1280]{1,0:T(8,128)S(1)} fusion(bf16[1024,2560]{1,0:T(8,128)(2,1)} %copy-done.47, bf16[2560,1280]{1,0:T(8,128)(2,1)} %all-gather.5.cloned.1.call-done), kind=kOutput, calls=%fused_computation.132 | convolution fusion | flops 6710886400 | bytes 17039360 | tf_op jit(solution)/shard_map/dot_general | solution.py:43
  218.9 1.8 slice.112
  220.7 1.3 copy-done.9
  223.1 1.5 convert_reduce_fusion
  228.2 2.5 copy.33
  231.5 4.7 %multiply_reduce_fusion = (f32[1280]{0:T(1024)S(1)}, f32[512]{0:T(512)S(1)}, f32[512]{0:T(512)S(1)}, f32[1280]{0:T(1024)S(1)}, f32[512,1280]{1,0:T(8,128)S(1)}) fusion(f32[512,1280]{1,0:T(8,128)} %copy-done.5, f32[512]{0:T(512)S(1)} %add_rsqrt_fusion, f32[512]{0:T(512)S(1)} %broadcast_multiply_fusion.2, f32[1280]{0:T(1024)S(1)} %mul.253, ...), kind=kLoop, calls=%fused_computation.20 | loop fusion | flops 6550016 | bytes 10509312 | tf_op jit(solution)/shard_map/reduce_sum | solution.py:589
  236.2 4.6 fusion.43
  240.8 3.0 convolution_convert_fusion
  243.8 53.7 %attn_bwd.1 = (f32[2,40,1280]{2,1,0:T(8,128)}, f32[2,40,1280]{2,1,0:T(8,128)}, f32[2,40,1280]{2,1,0:T(8,128)}) custom-call(s32[2]{0:T(128)} %len_ref.3, bf16[2,1024,128]{2,1,0:T(8,128)(2,1)} %and_convert_fusion.ohk_ref, bf16[2,256,128]{2,1,0:T(8,128)(2,1)} %get-tuple-element.102.ohq_ref, f32[2,40,1280]{2,1,0:T(8,128)} %get-tuple-element.97.tq_ref, ...), custom_call_target="tpu_custom_call" | custom-call | flops 20000000000 | bytes 15000000 | tf_op jit(solution)/shard_map/attn_bwd/pallas_call | solution.py:180
  299.6 1.2 reduce_sum.194
  300.8 1.4 maximum_maximum_fusion
  302.2 2.2 collective-permute-start.10
  304.5 1.4 collective-permute-start.9
  306.0 4.7 %fusion.14.d_out_ref = f32[16,2,40,1280]{3,2,1,0:T(8,128)} fusion(bf16[16,2,40,512]{3,2,1,0:T(8,128)(2,1)S(1)} %bitcast.113, bf16[512,1280]{1,0:T(8,128)(2,1)S(1)} %copy-done.12), kind=kOutput, calls=%fused_computation.35 | convolution fusion | flops 1677721600 | bytes 9175040 | tf_op jit(solution)/shard_map/dot_general | solution.py:43
  310.7 7.8 %collective-permute-done.10 = f32[80,1024]{1,0:T(8,128)S(1)} collective-permute-done((f32[80,1024]{1,0:T(8,128)S(1)}, f32[80,1024]{1,0:T(8,128)S(1)}, u32[]{:S(2)}, u32[]{:S(2)}) %collective-permute-start.10) | collective-permute-done | bytes 327712 | tf_op jit(solution)/shard_map/ppermute | solution.py:577
  318.5 3.3 collective-permute-done.8
  322.0 2.6 fusion.28
  325.2 4.6 %fusion.32.d_qkv_ref = f32[16,2,40,1024]{3,2,1,0:T(8,128)} fusion(bf16[16,2,40,80]{3,2,1,0:T(8,128)(2,1)S(1)} %bitcast.109, f32[80,1024]{1,0:T(8,128)S(1)} %add_add_fusion), kind=kOutput, calls=%fused_computation.67 | convolution fusion | flops 1258291200 | bytes 5775360 | tf_op jit(solution)/shard_map/dot_general | solution.py:578
  329.9 75.9 %reduce_oq.1 = (f32[40,1280]{1,0:T(8,128)}, f32[40,4096]{1,0:T(8,128)}, f32[4,40,1280]{2,1,0:T(8,128)}) custom-call(f32[16,2,40,1280]{3,2,1,0:T(8,128)} %fusion.14.d_out_ref, f32[16,2,40,1024]{3,2,1,0:T(8,128)} %fusion.32.d_qkv_ref, f32[4,40,1280]{2,1,0:T(8,128)} %bitcast.125), custom_call_target="tpu_custom_call" | custom-call | flops 20000000000 | bytes 15000000 | tf_op jit(solution)/shard_map/reduce_oq/pallas_call | solution.py:362
  405.8 1.3 copy.53
  407.1 31.6 %reduce_last.1 = (f32[4,80,640]{2,1,0:T(8,128)S(1)}, f32[2,48,640]{2,1,0:T(8,128)S(1)}) custom-call(f32[4,80,640]{2,1,0:T(8,128)S(1)} %bitcast.90, f32[48,1280]{1,0:T(8,128)S(1)} %concatenate.27.small_ref), custom_call_target="tpu_custom_call" | custom-call | tf_op jit(solution)/shard_map/reduce_last/pallas_call | solution.py:473
  440.4 1.2 copy.39
  447.0 2.7 reshape.380
  (233 shorter events, 35.9 us)
Async XLA Ops:
  7.2 8.2 %copy-start.42 = (f32[9,40]{1,0:T(8,128)S(1)}, f32[9,40]{1,0:T(8,128)}, u32[]{:S(2)}) copy-start(f32[9,40]{1,0:T(8,128)} %param.13) | copy-start | bytes 4324
  7.2 8.3 %copy-start.44 = (f32[160]{0:T(256)S(1)}, f32[160]{0:T(256)}, u32[]{:S(2)}) copy-start(f32[160]{0:T(256)} %param.17) | copy-start | bytes 1924
  7.2 131.5 %all-gather.3.cloned.1.call-start = ((), (), s32[]{:S(2)}) async-start(), calls=%async_computation.2 | async-start | bytes 6963200 | tf_op jit(solution)/shard_map/all_gather | solution.py:503
  9.0 8.8 %copy-start.20 = (bf16[40,3,20,64]{3,0,2,1:T(8,128)(2,1)S(1)}, bf16[40,3,20,64]{3,0,2,1:T(8,128)(2,1)}, u32[]{:S(2)}) copy-start(bf16[40,3,20,64]{3,0,2,1:T(8,128)(2,1)} %param.14) | copy-start | bytes 921604
  13.5 2.5 collective-permute-start
  16.8 148.9 %all-gather.5.cloned.1.call-start = ((), (), s32[]{:S(2)}) async-start(), calls=%async_computation.3 | async-start | bytes 6963200 | tf_op jit(solution)/shard_map/all_gather | solution.py:504
  16.9 115.0 %collective-permute-start.6 = (bf16[512,1280]{1,0:T(8,128)(2,1)}, bf16[512,1280]{1,0:T(8,128)(2,1)}, u32[]{:S(2)}, u32[]{:S(2)}) collective-permute-start(bf16[512,1280]{1,0:T(8,128)(2,1)} %bitcast.14), channel_id=1, source_target_pairs={{0,1},{1,0},{2,3},{3,2},{4,5},{5,4},{6,7},{7,6},{8,9},{9,8},{10,11... | collective-permute-start | bytes 3932168 | tf_op jit(solution)/shard_map/ppermute | solution.py:511
  17.6 312.3 %reduce-scatter.5.cloned.1.call-start = ((), (), s32[]{:S(2)}) async-start(), calls=%async_computation.5 | async-start | bytes 13926400 | tf_op jit(solution)/shard_map/reduce_scatter | solution.py:591
  18.3 47.6 %copy-start.7 = (f32[33,1280]{1,0:T(8,128)}, f32[33,1280]{1,0:T(8,128)S(1)}, u32[]{:S(2)}) copy-start(f32[33,1280]{1,0:T(8,128)S(1)} %convert_element_type.68) | copy-start | bytes 506884
  21.2 42.2 %copy-start.45 = (s32[2]{0:T(128)S(1)}, s32[2]{0:T(128)}, u32[]{:S(2)}) copy-start(s32[2]{0:T(128)} %len_ref.3) | copy-start | bytes 28
  63.3 3.9 copy-start
  63.5 3.6 copy-start.31
  68.2 8.4 %copy-start.30 = (f32[32,40]{1,0:T(8,128)S(1)}, f32[32,40]{1,0:T(8,128)}, u32[]{:S(2)}) copy-start(f32[32,40]{1,0:T(8,128)} %get-tuple-element.81) | copy-start | bytes 15364
  68.2 8.5 %copy-start.29 = (f32[32,40]{1,0:T(8,128)S(1)}, f32[32,40]{1,0:T(8,128)}, u32[]{:S(2)}) copy-start(f32[32,40]{1,0:T(8,128)} %get-tuple-element.80) | copy-start | bytes 15364
  68.2 17.2 %collective-permute-start.1 = (f32[80,1024]{1,0:T(8,128)S(1)}, f32[80,1024]{1,0:T(8,128)S(1)}, u32[]{:S(2)}, u32[]{:S(2)}) collective-permute-start(f32[80,1024]{1,0:T(8,128)S(1)} %get-tuple-element.105), channel_id=1, source_target_pairs={{0,32},{32,64},{64,96},{96,0},{1,33},{33,65},{65,97},{97,1},{2,34}... | collective-permute-start | bytes 983048 | tf_op jit(solution)/shard_map/ppermute | solution.py:532
  68.2 17.2 %copy-start.14 = (f32[80,4096]{1,0:T(8,128)S(1)}, f32[80,4096]{1,0:T(8,128)}, u32[]{:S(2)}) copy-start(f32[80,4096]{1,0:T(8,128)} %copy-done.13) | copy-start | bytes 3932164
  68.2 17.2 %collective-permute-start.2 = (f32[80,1024]{1,0:T(8,128)S(1)}, f32[80,1024]{1,0:T(8,128)S(1)}, u32[]{:S(2)}, u32[]{:S(2)}) collective-permute-start(f32[80,1024]{1,0:T(8,128)S(1)} %get-tuple-element.105), channel_id=1, source_target_pairs={{0,64},{32,96},{64,0},{96,32},{1,65},{33,97},{65,1},{97,33},{2,66}... | collective-permute-start | bytes 983048 | tf_op jit(solution)/shard_map/ppermute | solution.py:532
  70.2 15.6 %collective-permute-start.3 = (f32[80,1024]{1,0:T(8,128)S(1)}, f32[80,1024]{1,0:T(8,128)S(1)}, u32[]{:S(2)}, u32[]{:S(2)}) collective-permute-start(f32[80,1024]{1,0:T(8,128)S(1)} %get-tuple-element.105), channel_id=1, source_target_pairs={{0,96},{32,0},{64,32},{96,64},{1,97},{33,1},{65,33},{97,65},{2,98}... | collective-permute-start | bytes 983048 | tf_op jit(solution)/shard_map/ppermute | solution.py:532
  71.7 3.9 copy-start.38
  72.4 13.4 %copy-start.21 = (pred[2,256,128]{2,1,0:T(32,128)(4,1)}, pred[2,256,128]{2,1,0:T(32,128)(4,1)S(1)}, u32[]{:S(2)}) copy-start(pred[2,256,128]{2,1,0:T(32,128)(4,1)S(1)} %get-tuple-element.103) | copy-start | bytes 196612
  87.0 34.7 %copy-start.4 = (bf16[4,4,2,40,1280]{4,3,2,1,0:T(8,128)(2,1)S(1)}, bf16[4,4,2,40,1280]{4,3,2,1,0:T(8,128)(2,1)}, u32[]{:S(2)}) copy-start(bf16[4,4,2,40,1280]{4,3,2,1,0:T(8,128)(2,1)} %copy-done.3) | copy-start | bytes 9830404
  128.1 7.2 %collective-permute-start.4 = (bf16[512,1280]{1,0:T(8,128)(2,1)}, bf16[512,1280]{1,0:T(8,128)(2,1)}, u32[]{:S(2)}, u32[]{:S(2)}) collective-permute-start(bf16[512,1280]{1,0:T(8,128)(2,1)} %add_convert_fusion), channel_id=1, source_target_pairs={{0,1},{1,0},{2,3},{3,2},{4,5},{5,4},{6,7},{7,6},{8,9},{9,8},{10,11... | collective-permute-start | bytes 3932168 | tf_op jit(solution)/shard_map/ppermute | solution.py:548
  165.5 240.4 %reduce-scatter.3.cloned.1.call-start = ((), (), s32[]{:S(2)}) async-start(), calls=%async_computation.4 | async-start | bytes 13926400 | tf_op jit(solution)/shard_map/reduce_scatter | solution.py:592
  165.7 18.2 %copy-start.15 = (bf16[1024,1280]{1,0:T(8,128)(2,1)S(1)}, bf16[1024,1280]{1,0:T(8,128)(2,1)}, u32[]{:S(2)}) copy-start(bf16[1024,1280]{1,0:T(8,128)(2,1)} %pad_maximum_fusion) | copy-start | bytes 7864324
  204.9 3.2 copy-start.10
  208.1 23.3 %collective-permute-start.7 = (f32[512,1280]{1,0:T(8,128)}, f32[512,1280]{1,0:T(8,128)}, u32[]{:S(2)}, u32[]{:S(2)}) collective-permute-start(f32[512,1280]{1,0:T(8,128)} %slice.115), channel_id=1, source_target_pairs={{0,1},{1,0},{2,3},{3,2},{4,5},{5,4},{6,7},{7,6},{8,9},{9,8},{10,11... | collective-permute-start | bytes 7864328 | tf_op jit(solution)/shard_map/ppermute | solution.py:564
  218.9 3.2 copy-start.9
  218.9 7.9 %copy-start.39 = (s32[2,256]{1,0:T(2,128)S(1)}, s32[2,256]{1,0:T(2,128)}, u32[]{:S(2)}) copy-start(s32[2,256]{1,0:T(2,128)} %copy-done.38) | copy-start | bytes 6148
  222.1 14.2 %collective-permute-start.5 = (f32[512,1280]{1,0:T(8,128)}, f32[512,1280]{1,0:T(8,128)}, u32[]{:S(2)}, u32[]{:S(2)}) collective-permute-start(f32[512,1280]{1,0:T(8,128)} %slice.112), channel_id=1, source_target_pairs={{0,1},{1,0},{2,3},{3,2},{4,5},{5,4},{6,7},{7,6},{8,9},{9,8},{10,11... | collective-permute-start | bytes 7864328 | tf_op jit(solution)/shard_map/ppermute | solution.py:555
  231.4 4.8 %copy-start.6 = (f32[512,1280]{1,0:T(8,128)S(1)}, f32[512,1280]{1,0:T(8,128)}, u32[]{:S(2)}) copy-start(f32[512,1280]{1,0:T(8,128)} %copy-done.5) | copy-start | bytes 7864324
  231.4 4.8 %copy-start.33 = (f32[1280]{0:T(1024)S(1)}, f32[1280]{0:T(1024)}, u32[]{:S(2)}) copy-start(f32[1280]{0:T(1024)} %add.268) | copy-start | bytes 15364
  299.6 6.4 %copy-start.12 = (bf16[512,1280]{1,0:T(8,128)(2,1)S(1)}, bf16[512,1280]{1,0:T(8,128)(2,1)}, u32[]{:S(2)}) copy-start(bf16[512,1280]{1,0:T(8,128)(2,1)} %copy-done.11) | copy-start | bytes 3932164
  299.6 6.4 %copy-start.17 = (bf16[1280,512]{1,0:T(8,128)(2,1)S(1)}, bf16[1280,512]{1,0:T(8,128)(2,1)}, u32[]{:S(2)}) copy-start(bf16[1280,512]{1,0:T(8,128)(2,1)} %copy.33) | copy-start | bytes 3932164
  302.2 16.3 %collective-permute-start.10 = (f32[80,1024]{1,0:T(8,128)S(1)}, f32[80,1024]{1,0:T(8,128)S(1)}, u32[]{:S(2)}, u32[]{:S(2)}) collective-permute-start(f32[80,1024]{1,0:T(8,128)S(1)} %get-tuple-element.91), channel_id=1, source_target_pairs={{0,96},{32,0},{64,32},{96,64},{1,97},{33,1},{65,33},{97,65},{2,98}... | collective-permute-start | bytes 983048 | tf_op jit(solution)/shard_map/ppermute | solution.py:577
  304.5 17.3 %collective-permute-start.8 = (f32[80,1024]{1,0:T(8,128)S(1)}, f32[80,1024]{1,0:T(8,128)S(1)}, u32[]{:S(2)}, u32[]{:S(2)}) collective-permute-start(f32[80,1024]{1,0:T(8,128)S(1)} %get-tuple-element.90), channel_id=1, source_target_pairs={{0,32},{32,64},{64,96},{96,0},{1,33},{33,65},{65,97},{97,1},{2,34}... | collective-permute-start | bytes 983048 | tf_op jit(solution)/shard_map/ppermute | solution.py:577
  304.5 17.3 %collective-permute-start.9 = (f32[80,1024]{1,0:T(8,128)S(1)}, f32[80,1024]{1,0:T(8,128)S(1)}, u32[]{:S(2)}, u32[]{:S(2)}) collective-permute-start(f32[80,1024]{1,0:T(8,128)S(1)} %get-tuple-element.92), channel_id=1, source_target_pairs={{0,64},{32,96},{64,0},{96,32},{1,65},{33,97},{65,1},{97,33},{2,66}... | collective-permute-start | bytes 983048 | tf_op jit(solution)/shard_map/ppermute | solution.py:577
  306.0 15.9 %copy-start.1 = (bf16[4,4,2,40,1024]{4,3,2,1,0:T(8,128)(2,1)S(1)}, bf16[4,4,2,40,1024]{4,3,2,1,0:T(8,128)(2,1)}, u32[]{:S(2)}) copy-start(bf16[4,4,2,40,1024]{4,3,2,1,0:T(8,128)(2,1)} %copy-done) | copy-start | bytes 7864324
  306.0 15.9 %copy-start.8 = (f32[33,1280]{1,0:T(8,128)S(1)}, f32[33,1280]{1,0:T(8,128)}, u32[]{:S(2)}) copy-start(f32[33,1280]{1,0:T(8,128)} %copy-done.7) | copy-start | bytes 506884
  306.0 15.9 %copy-start.28 = (f32[1280]{0:T(1024)S(1)}, f32[1280]{0:T(1024)}, u32[]{:S(2)}) copy-start(f32[1280]{0:T(1024)} %copy-done.27) | copy-start | bytes 15364
  306.0 15.9 %copy-start.32 = (f32[2,33]{1,0:T(2,128)S(1)}, f32[2,33]{1,0:T(2,128)}, u32[]{:S(2)}) copy-start(f32[2,33]{1,0:T(2,128)} %copy-done.31) | copy-start | bytes 796
  306.0 15.9 %copy-start.36 = (f32[2,33]{1,0:T(2,128)S(1)}, f32[2,33]{1,0:T(2,128)}, u32[]{:S(2)}) copy-start(f32[2,33]{1,0:T(2,128)} %copy-done.35) | copy-start | bytes 796
  306.0 15.9 %copy-start.41 = (f32[2,33]{1,0:T(2,128)S(1)}, f32[2,33]{1,0:T(2,128)}, u32[]{:S(2)}) copy-start(f32[2,33]{1,0:T(2,128)} %copy-done.40) | copy-start | bytes 796
  310.7 13.9 %copy-start.22 = (pred[2,256,128]{2,1,0:T(32,128)(4,1)S(1)}, pred[2,256,128]{2,1,0:T(32,128)(4,1)}, u32[]{:S(2)}) copy-start(pred[2,256,128]{2,1,0:T(32,128)(4,1)} %copy-done.21) | copy-start | bytes 196612
  321.9 3.3 copy-start.16
  405.8 34.1 %copy-start.23 = (f32[40,4096]{1,0:T(8,128)S(1)}, f32[40,4096]{1,0:T(8,128)}, u32[]{:S(2)}) copy-start(f32[40,4096]{1,0:T(8,128)} %get-tuple-element.48) | copy-start | bytes 1966084
  439.6 4.3 collective-permute-start.11
  445.8 3.8 copy-start.26
  445.9 4.5 copy-start.18
  (16 other events, 31.4 us)
Sparse Core Ops, SparseCore 0:
  16.9 67.2 all-gather.2
  86.4 61.8 all-gather.4
  165.6 93.5 reduce-scatter.4
  262.5 100.4 reduce-scatter.2

commit v5 on v4

--- a/solution.py
+++ b/solution.py
@@ -309,16 +309,16 @@
         acc[i, :, :DIM] += d_out_ref[i, ci]
         return carry
     lax.fori_loop(0, 16, add_out, 0)
+    grid = acc.reshape(4, 4, ROWS, WIDE)
+    ya = Ring('y', ports)
+    ya.rs_start(lambda k, h: grid.at[:, k, half_rows(h), pl.ds(0, HALF_W)], bufs[0])
     second.wait_recv()
 
     def add_qkv(i, carry):
         acc[i, :, DIM:] += d_qkv_ref[i, ci]
         return carry
     lax.fori_loop(0, 16, add_qkv, 0)
-    grid = acc.reshape(4, 4, ROWS, WIDE)
-    ya = Ring('y', ports)
     zb = Ring('z', ports)
-    ya.rs_start(lambda k, h: grid.at[:, k, half_rows(h), pl.ds(0, HALF_W)], bufs[0])
     zb.rs_start(lambda k, h: grid.at[k, :, half_rows(h), pl.ds(HALF_W, HALF_W)], bufs[1])
     xd.rs_mid()
     ya.rs_mid()

time: 467 us -> 468 us (level)
  no operation moved by 1% of the time
where the time goes in v5:
time: 468 us; the launch traced here: 459 us
  Pallas kernels  237 us (51%)
  matrix products  94 us (20%)
  local copies, waits for them, and re-layouts  47.4 us (10%)
  other arithmetic  33.1 us (7%)
  waiting for transfers between devices  20.2 us (4%)
  between operations  15.2 us (3%)
  starting transfers between devices  11.8 us (3%)
    dot_general x10, matrix products, mm(): return lax.dot_general(a, b, (dims, ((), ())), preferred_element_type=F32)  84.4 us
    pallas_call x1, Pallas kernels, reduce_oq(): pl.pallas_call(oq_kernel, in_specs=vmem(3), out_specs=vmem(3), out_shape=...  76.6 us
    pallas_call x1, Pallas kernels, attn_bwd(): pl.pallas_call(attn_bwd_kernel, grid=(2, PAIRS), in_specs=attn_specs() +...  53.7 us
    pallas_call x1, Pallas kernels, gather_first(): pl.pallas_call(first_kernel, in_specs=vmem(4), out_specs=vmem(4), out_sha...  40.4 us
    pallas_call x1, Pallas kernels, attn_fwd(): pl.pallas_call(attn_fwd_kernel, grid=(2, PAIRS), in_specs=attn_specs(), o...  34.7 us
    pallas_call x1, Pallas kernels, reduce_last(): pl.pallas_call(last_kernel, in_specs=vmem(2), out_specs=vmem(2), out_shap...  31.7 us
    unnamed x103, local copies, waits for them, and re-layouts  15.3 us
    ppermute x3, waiting for transfers between devices, local_step(): lax.ppermute(part, 'x', [(i, (i + hop) % 4) for i in range(4)])  11.1 us
  transfers between devices with their start and end apart: 16, of which 5 were waited for; matrix products, arithmetic and copies ran while one was open for 32% of the time, Pallas kernels for 45%

profile of v5, /device:TPU:1, one launch (start us, length us, event | category | flops | bytes accessed | tf_op | source)
XLA Modules:
  0.0 458.7 jit_solution(2865237229439509199)
XLA Ops:
  7.2 1.7 reshape.353
  9.0 4.1 dynamic-slice_reduce_fusion.1
  13.5 1.4 collective-permute-start
  21.2 40.4 %gather_first.1 = (bf16[4,4,2,40,1024]{4,3,2,1,0:T(8,128)(2,1)S(1)}, bf16[4,4,2,40,1280]{4,3,2,1,0:T(8,128)(2,1)S(1)}, f32[4,4,2,8,128]{4,3,2,1,0:T(8,128)S(1)}, s32[4,4,128]{2,1,0:T(4,128)S(1)}) custom-call(bf16[40,1024]{1,0:T(8,128)(2,1)S(1)} %pad_dynamic-slice_fusion.2.wq_ref, bf16[40,1280]{1,0:T(8,128)(2,1)S(1)} %copy-done.2, ...), custom_call_target="tpu_custom_call" | custom-call | flops 20000000000 | bytes 15000000 | tf_op jit(solution)/shard_map/gather_first/pallas_call | solution.py:411
  61.6 1.7 copy-done.3
  68.2 2.0 collective-permute-start.2
  70.2 1.3 collective-permute-start.3
  72.4 2.0 convolution_multiply_fusion
  74.4 1.1 and_convert_fusion.ohk_ref
  77.4 8.0 %collective-permute-done.1 = f32[80,1024]{1,0:T(8,128)S(1)} collective-permute-done((f32[80,1024]{1,0:T(8,128)S(1)}, f32[80,1024]{1,0:T(8,128)S(1)}, u32[]{:S(2)}, u32[]{:S(2)}) %collective-permute-start.1) | collective-permute-done | bytes 327712 | tf_op jit(solution)/shard_map/ppermute | solution.py:532
  87.0 34.7 %attn_fwd.1 = (bf16[2,256,1280]{2,1,0:T(8,128)(2,1)}, f32[2,10,8,256]{3,2,1,0:T(8,128)}) custom-call(s32[2]{0:T(128)} %len_ref.3, bf16[2,1024,128]{2,1,0:T(8,128)(2,1)} %and_convert_fusion.ohk_ref, bf16[2,256,128]{2,1,0:T(8,128)(2,1)} %get-tuple-element.102.ohq_ref, f32[2,40,1280]{2,1,0:T(8,128)} %get-tuple-element.97.tq_ref, ...), custom_call_target="tpu_custom_call" | custom-call | flops 20000000000 | bytes 15000000 | tf_op jit(solution)/shard_map/attn_fwd/pallas_call | solution.py:172
  121.7 4.2 fusion.45
  126.6 1.5 add_convert_fusion
  128.1 1.3 collective-permute-start.4
  131.9 3.5 pad_maximum_fusion.1
  135.3 3.4 pad_maximum_fusion
  138.7 12.7 %multiply_convert_fusion = (bf16[1024,2560]{1,0:T(8,128)(2,1)S(1)}, f32[1024,2560]{1,0:T(8,128)}) fusion(f32[2560]{0:T(1024)S(1)} %add.261, bf16[1024,1280]{1,0:T(8,128)(2,1)} %pad_maximum_fusion, bf16[1280,2560]{1,0:T(8,128)(2,1)} %all-gather.3.cloned.1.call-done), kind=kOutput, calls=%fused_computation.6 | convolution fusion | flops 6726615040 | bytes 24913920 | tf_op jit(solution)/shard_map/dot_general | solution.py:43
  151.4 2.3 copy-done.47
  153.7 11.7 %fusion.42 = f32[2560,1280]{1,0:T(8,128)} fusion(bf16[1024,2560]{1,0:T(8,128)(2,1)S(1)} %get-tuple-element.108, bf16[512,1280]{1,0:T(8,128)(2,1)} %collective-permute-done.6, bf16[512,1280]{1,0:T(8,128)(2,1)} %bitcast.14), kind=kOutput, calls=%fused_computation.127 | convolution fusion | flops 6716129280 | bytes 20971520 | tf_op jit(solution)/shard_map/dot_general | solution.py:43
  165.8 15.9 %fusion.46 = (f32[2560]{0:T(1024)}, bf16[1024,2560]{1,0:T(8,128)(2,1)S(1)}) fusion(f32[1024,2560]{1,0:T(8,128)} %get-tuple-element.109, f32[2560]{0:T(1024)S(1)} %add.261, bf16[1024,1280]{1,0:T(8,128)(2,1)} %pad_maximum_fusion.1, bf16[2560,1280]{1,0:T(8,128)(2,1)} %all-gather.5.cloned.1.call-done), kind=kOutput, calls=%fused_computation.131 | convolution fusion | flops 6742341120 | bytes 24924160 | tf_op jit(solution)/shard_map/dot_general | solution.py:43
  181.7 2.3 copy-done.46
  184.0 10.1 %fusion.11 = f32[1280,2560]{1,0:T(8,128)} fusion(bf16[1024,1280]{1,0:T(8,128)(2,1)S(1)} %copy-done.15, bf16[1024,2560]{1,0:T(8,128)(2,1)S(1)} %get-tuple-element.112), kind=kOutput, calls=%fused_computation.25 | convolution fusion | flops 6710886400 | bytes 20971520 | tf_op jit(solution)/shard_map/dot_general | solution.py:43
  194.1 10.8 %fusion.9 = f32[1024,1280]{1,0:T(8,128)S(1)} fusion(bf16[1280,2560]{1,0:T(8,128)(2,1)} %all-gather.3.cloned.1.call-done, bf16[1024,2560]{1,0:T(8,128)(2,1)} %copy-done.46), kind=kOutput, calls=%fused_computation.23 | convolution fusion | flops 6710886400 | bytes 17039360 | tf_op jit(solution)/shard_map/dot_general | solution.py:43
  205.0 1.8 slice.115
  206.7 1.4 copy-done.10
  208.1 10.8 %fusion.47 = f32[1024,1280]{1,0:T(8,128)S(1)} fusion(bf16[1024,2560]{1,0:T(8,128)(2,1)} %copy-done.47, bf16[2560,1280]{1,0:T(8,128)(2,1)} %all-gather.5.cloned.1.call-done), kind=kOutput, calls=%fused_computation.132 | convolution fusion | flops 6710886400 | bytes 17039360 | tf_op jit(solution)/shard_map/dot_general | solution.py:43
  218.9 1.8 slice.112
  220.7 1.3 copy-done.9
  223.1 1.5 convert_reduce_fusion
  228.2 2.5 copy.33
  231.5 4.7 %multiply_reduce_fusion = (f32[1280]{0:T(1024)S(1)}, f32[512]{0:T(512)S(1)}, f32[512]{0:T(512)S(1)}, f32[1280]{0:T(1024)S(1)}, f32[512,1280]{1,0:T(8,128)S(1)}) fusion(f32[512,1280]{1,0:T(8,128)} %copy-done.5, f32[512]{0:T(512)S(1)} %add_rsqrt_fusion, f32[512]{0:T(512)S(1)} %broadcast_multiply_fusion.2, f32[1280]{0:T(1024)S(1)} %mul.253, ...), kind=kLoop, calls=%fused_computation.20 | loop fusion | flops 6550016 | bytes 10509312 | tf_op jit(solution)/shard_map/reduce_sum | solution.py:589
  236.2 4.6 fusion.43
  240.8 3.0 convolution_convert_fusion
  243.8 53.7 %attn_bwd.1 = (f32[2,40,1280]{2,1,0:T(8,128)}, f32[2,40,1280]{2,1,0:T(8,128)}, f32[2,40,1280]{2,1,0:T(8,128)}) custom-call(s32[2]{0:T(128)} %len_ref.3, bf16[2,1024,128]{2,1,0:T(8,128)(2,1)} %and_convert_fusion.ohk_ref, bf16[2,256,128]{2,1,0:T(8,128)(2,1)} %get-tuple-element.102.ohq_ref, f32[2,40,1280]{2,1,0:T(8,128)} %get-tuple-element.97.tq_ref, ...), custom_call_target="tpu_custom_call" | custom-call | flops 20000000000 | bytes 15000000 | tf_op jit(solution)/shard_map/attn_bwd/pallas_call | solution.py:180
  299.6 1.2 reduce_sum.194
  300.8 1.4 maximum_maximum_fusion
  302.2 2.2 collective-permute-start.10
  304.5 1.4 collective-permute-start.9
  306.0 4.7 %fusion.14.d_out_ref = f32[16,2,40,1280]{3,2,1,0:T(8,128)} fusion(bf16[16,2,40,512]{3,2,1,0:T(8,128)(2,1)S(1)} %bitcast.113, bf16[512,1280]{1,0:T(8,128)(2,1)S(1)} %copy-done.12), kind=kOutput, calls=%fused_computation.35 | convolution fusion | flops 1677721600 | bytes 9175040 | tf_op jit(solution)/shard_map/dot_general | solution.py:43
  310.7 7.8 %collective-permute-done.10 = f32[80,1024]{1,0:T(8,128)S(1)} collective-permute-done((f32[80,1024]{1,0:T(8,128)S(1)}, f32[80,1024]{1,0:T(8,128)S(1)}, u32[]{:S(2)}, u32[]{:S(2)}) %collective-permute-start.10) | collective-permute-done | bytes 327712 | tf_op jit(solution)/shard_map/ppermute | solution.py:577
  318.5 3.3 collective-permute-done.8
  322.0 2.6 fusion.28
  325.2 4.6 %fusion.32.d_qkv_ref = f32[16,2,40,1024]{3,2,1,0:T(8,128)} fusion(bf16[16,2,40,80]{3,2,1,0:T(8,128)(2,1)S(1)} %bitcast.109, f32[80,1024]{1,0:T(8,128)S(1)} %add_add_fusion), kind=kOutput, calls=%fused_computation.67 | convolution fusion | flops 1258291200 | bytes 5775360 | tf_op jit(solution)/shard_map/dot_general | solution.py:578
  329.9 76.6 %reduce_oq.1 = (f32[40,1280]{1,0:T(8,128)}, f32[40,4096]{1,0:T(8,128)}, f32[4,40,1280]{2,1,0:T(8,128)}) custom-call(f32[16,2,40,1280]{3,2,1,0:T(8,128)} %fusion.14.d_out_ref, f32[16,2,40,1024]{3,2,1,0:T(8,128)} %fusion.32.d_qkv_ref, f32[4,40,1280]{2,1,0:T(8,128)} %bitcast.125), custom_call_target="tpu_custom_call" | custom-call | flops 20000000000 | bytes 15000000 | tf_op jit(solution)/shard_map/reduce_oq/pallas_call | solution.py:362
  406.5 1.3 copy.53
  407.8 31.7 %reduce_last.1 = (f32[4,80,640]{2,1,0:T(8,128)S(1)}, f32[2,48,640]{2,1,0:T(8,128)S(1)}) custom-call(f32[4,80,640]{2,1,0:T(8,128)S(1)} %bitcast.90, f32[48,1280]{1,0:T(8,128)S(1)} %concatenate.27.small_ref), custom_call_target="tpu_custom_call" | custom-call | tf_op jit(solution)/shard_map/reduce_last/pallas_call | solution.py:473
  441.1 1.2 copy.39
  447.7 2.7 reshape.380
  (233 shorter events, 35.9 us)
Async XLA Ops:
  7.2 8.2 %copy-start.42 = (f32[9,40]{1,0:T(8,128)S(1)}, f32[9,40]{1,0:T(8,128)}, u32[]{:S(2)}) copy-start(f32[9,40]{1,0:T(8,128)} %param.13) | copy-start | bytes 4324
  7.2 8.3 %copy-start.44 = (f32[160]{0:T(256)S(1)}, f32[160]{0:T(256)}, u32[]{:S(2)}) copy-start(f32[160]{0:T(256)} %param.17) | copy-start | bytes 1924
  7.2 131.5 %all-gather.3.cloned.1.call-start = ((), (), s32[]{:S(2)}) async-start(), calls=%async_computation.2 | async-start | bytes 6963200 | tf_op jit(solution)/shard_map/all_gather | solution.py:503
  9.0 8.8 %copy-start.20 = (bf16[40,3,20,64]{3,0,2,1:T(8,128)(2,1)S(1)}, bf16[40,3,20,64]{3,0,2,1:T(8,128)(2,1)}, u32[]{:S(2)}) copy-start(bf16[40,3,20,64]{3,0,2,1:T(8,128)(2,1)} %param.14) | copy-start | bytes 921604
  13.5 2.5 collective-permute-start
  16.8 148.9 %all-gather.5.cloned.1.call-start = ((), (), s32[]{:S(2)}) async-start(), calls=%async_computation.3 | async-start | bytes 6963200 | tf_op jit(solution)/shard_map/all_gather | solution.py:504
  16.9 115.0 %collective-permute-start.6 = (bf16[512,1280]{1,0:T(8,128)(2,1)}, bf16[512,1280]{1,0:T(8,128)(2,1)}, u32[]{:S(2)}, u32[]{:S(2)}) collective-permute-start(bf16[512,1280]{1,0:T(8,128)(2,1)} %bitcast.14), channel_id=1, source_target_pairs={{0,1},{1,0},{2,3},{3,2},{4,5},{5,4},{6,7},{7,6},{8,9},{9,8},{10,11... | collective-permute-start | bytes 3932168 | tf_op jit(solution)/shard_map/ppermute | solution.py:511
  17.6 312.3 %reduce-scatter.5.cloned.1.call-start = ((), (), s32[]{:S(2)}) async-start(), calls=%async_computation.5 | async-start | bytes 13926400 | tf_op jit(solution)/shard_map/reduce_scatter | solution.py:591
  18.3 47.6 %copy-start.7 = (f32[33,1280]{1,0:T(8,128)}, f32[33,1280]{1,0:T(8,128)S(1)}, u32[]{:S(2)}) copy-start(f32[33,1280]{1,0:T(8,128)S(1)} %convert_element_type.68) | copy-start | bytes 506884
  21.2 42.2 %copy-start.45 = (s32[2]{0:T(128)S(1)}, s32[2]{0:T(128)}, u32[]{:S(2)}) copy-start(s32[2]{0:T(128)} %len_ref.3) | copy-start | bytes 28
  63.3 3.9 copy-start
  63.5 3.6 copy-start.31
  68.2 8.4 %copy-start.30 = (f32[32,40]{1,0:T(8,128)S(1)}, f32[32,40]{1,0:T(8,128)}, u32[]{:S(2)}) copy-start(f32[32,40]{1,0:T(8,128)} %get-tuple-element.81) | copy-start | bytes 15364
  68.2 8.5 %copy-start.29 = (f32[32,40]{1,0:T(8,128)S(1)}, f32[32,40]{1,0:T(8,128)}, u32[]{:S(2)}) copy-start(f32[32,40]{1,0:T(8,128)} %get-tuple-element.80) | copy-start | bytes 15364
  68.2 17.2 %collective-permute-start.1 = (f32[80,1024]{1,0:T(8,128)S(1)}, f32[80,1024]{1,0:T(8,128)S(1)}, u32[]{:S(2)}, u32[]{:S(2)}) collective-permute-start(f32[80,1024]{1,0:T(8,128)S(1)} %get-tuple-element.105), channel_id=1, source_target_pairs={{0,32},{32,64},{64,96},{96,0},{1,33},{33,65},{65,97},{97,1},{2,34}... | collective-permute-start | bytes 983048 | tf_op jit(solution)/shard_map/ppermute | solution.py:532
  68.2 17.2 %copy-start.14 = (f32[80,4096]{1,0:T(8,128)S(1)}, f32[80,4096]{1,0:T(8,128)}, u32[]{:S(2)}) copy-start(f32[80,4096]{1,0:T(8,128)} %copy-done.13) | copy-start | bytes 3932164
  68.2 17.2 %collective-permute-start.2 = (f32[80,1024]{1,0:T(8,128)S(1)}, f32[80,1024]{1,0:T(8,128)S(1)}, u32[]{:S(2)}, u32[]{:S(2)}) collective-permute-start(f32[80,1024]{1,0:T(8,128)S(1)} %get-tuple-element.105), channel_id=1, source_target_pairs={{0,64},{32,96},{64,0},{96,32},{1,65},{33,97},{65,1},{97,33},{2,66}... | collective-permute-start | bytes 983048 | tf_op jit(solution)/shard_map/ppermute | solution.py:532
  70.2 15.6 %collective-permute-start.3 = (f32[80,1024]{1,0:T(8,128)S(1)}, f32[80,1024]{1,0:T(8,128)S(1)}, u32[]{:S(2)}, u32[]{:S(2)}) collective-permute-start(f32[80,1024]{1,0:T(8,128)S(1)} %get-tuple-element.105), channel_id=1, source_target_pairs={{0,96},{32,0},{64,32},{96,64},{1,97},{33,1},{65,33},{97,65},{2,98}... | collective-permute-start | bytes 983048 | tf_op jit(solution)/shard_map/ppermute | solution.py:532
  71.7 3.9 copy-start.38
  72.4 13.4 %copy-start.21 = (pred[2,256,128]{2,1,0:T(32,128)(4,1)}, pred[2,256,128]{2,1,0:T(32,128)(4,1)S(1)}, u32[]{:S(2)}) copy-start(pred[2,256,128]{2,1,0:T(32,128)(4,1)S(1)} %get-tuple-element.103) | copy-start | bytes 196612
  87.0 34.7 %copy-start.4 = (bf16[4,4,2,40,1280]{4,3,2,1,0:T(8,128)(2,1)S(1)}, bf16[4,4,2,40,1280]{4,3,2,1,0:T(8,128)(2,1)}, u32[]{:S(2)}) copy-start(bf16[4,4,2,40,1280]{4,3,2,1,0:T(8,128)(2,1)} %copy-done.3) | copy-start | bytes 9830404
  128.1 7.2 %collective-permute-start.4 = (bf16[512,1280]{1,0:T(8,128)(2,1)}, bf16[512,1280]{1,0:T(8,128)(2,1)}, u32[]{:S(2)}, u32[]{:S(2)}) collective-permute-start(bf16[512,1280]{1,0:T(8,128)(2,1)} %add_convert_fusion), channel_id=1, source_target_pairs={{0,1},{1,0},{2,3},{3,2},{4,5},{5,4},{6,7},{7,6},{8,9},{9,8},{10,11... | collective-permute-start | bytes 3932168 | tf_op jit(solution)/shard_map/ppermute | solution.py:548
  165.5 241.0 %reduce-scatter.3.cloned.1.call-start = ((), (), s32[]{:S(2)}) async-start(), calls=%async_computation.4 | async-start | bytes 13926400 | tf_op jit(solution)/shard_map/reduce_scatter | solution.py:592
  165.7 18.2 %copy-start.15 = (bf16[1024,1280]{1,0:T(8,128)(2,1)S(1)}, bf16[1024,1280]{1,0:T(8,128)(2,1)}, u32[]{:S(2)}) copy-start(bf16[1024,1280]{1,0:T(8,128)(2,1)} %pad_maximum_fusion) | copy-start | bytes 7864324
  204.9 3.2 copy-start.10
  208.1 23.3 %collective-permute-start.7 = (f32[512,1280]{1,0:T(8,128)}, f32[512,1280]{1,0:T(8,128)}, u32[]{:S(2)}, u32[]{:S(2)}) collective-permute-start(f32[512,1280]{1,0:T(8,128)} %slice.115), channel_id=1, source_target_pairs={{0,1},{1,0},{2,3},{3,2},{4,5},{5,4},{6,7},{7,6},{8,9},{9,8},{10,11... | collective-permute-start | bytes 7864328 | tf_op jit(solution)/shard_map/ppermute | solution.py:564
  218.9 3.2 copy-start.9
  218.9 7.9 %copy-start.39 = (s32[2,256]{1,0:T(2,128)S(1)}, s32[2,256]{1,0:T(2,128)}, u32[]{:S(2)}) copy-start(s32[2,256]{1,0:T(2,128)} %copy-done.38) | copy-start | bytes 6148
  222.1 14.2 %collective-permute-start.5 = (f32[512,1280]{1,0:T(8,128)}, f32[512,1280]{1,0:T(8,128)}, u32[]{:S(2)}, u32[]{:S(2)}) collective-permute-start(f32[512,1280]{1,0:T(8,128)} %slice.112), channel_id=1, source_target_pairs={{0,1},{1,0},{2,3},{3,2},{4,5},{5,4},{6,7},{7,6},{8,9},{9,8},{10,11... | collective-permute-start | bytes 7864328 | tf_op jit(solution)/shard_map/ppermute | solution.py:555
  231.4 4.8 %copy-start.6 = (f32[512,1280]{1,0:T(8,128)S(1)}, f32[512,1280]{1,0:T(8,128)}, u32[]{:S(2)}) copy-start(f32[512,1280]{1,0:T(8,128)} %copy-done.5) | copy-start | bytes 7864324
  231.4 4.8 %copy-start.33 = (f32[1280]{0:T(1024)S(1)}, f32[1280]{0:T(1024)}, u32[]{:S(2)}) copy-start(f32[1280]{0:T(1024)} %add.268) | copy-start | bytes 15364
  299.6 6.4 %copy-start.12 = (bf16[512,1280]{1,0:T(8,128)(2,1)S(1)}, bf16[512,1280]{1,0:T(8,128)(2,1)}, u32[]{:S(2)}) copy-start(bf16[512,1280]{1,0:T(8,128)(2,1)} %copy-done.11) | copy-start | bytes 3932164
  299.6 6.4 %copy-start.17 = (bf16[1280,512]{1,0:T(8,128)(2,1)S(1)}, bf16[1280,512]{1,0:T(8,128)(2,1)}, u32[]{:S(2)}) copy-start(bf16[1280,512]{1,0:T(8,128)(2,1)} %copy.33) | copy-start | bytes 3932164
  302.2 16.3 %collective-permute-start.10 = (f32[80,1024]{1,0:T(8,128)S(1)}, f32[80,1024]{1,0:T(8,128)S(1)}, u32[]{:S(2)}, u32[]{:S(2)}) collective-permute-start(f32[80,1024]{1,0:T(8,128)S(1)} %get-tuple-element.91), channel_id=1, source_target_pairs={{0,96},{32,0},{64,32},{96,64},{1,97},{33,1},{65,33},{97,65},{2,98}... | collective-permute-start | bytes 983048 | tf_op jit(solution)/shard_map/ppermute | solution.py:577
  304.5 17.3 %collective-permute-start.8 = (f32[80,1024]{1,0:T(8,128)S(1)}, f32[80,1024]{1,0:T(8,128)S(1)}, u32[]{:S(2)}, u32[]{:S(2)}) collective-permute-start(f32[80,1024]{1,0:T(8,128)S(1)} %get-tuple-element.90), channel_id=1, source_target_pairs={{0,32},{32,64},{64,96},{96,0},{1,33},{33,65},{65,97},{97,1},{2,34}... | collective-permute-start | bytes 983048 | tf_op jit(solution)/shard_map/ppermute | solution.py:577
  304.5 17.3 %collective-permute-start.9 = (f32[80,1024]{1,0:T(8,128)S(1)}, f32[80,1024]{1,0:T(8,128)S(1)}, u32[]{:S(2)}, u32[]{:S(2)}) collective-permute-start(f32[80,1024]{1,0:T(8,128)S(1)} %get-tuple-element.92), channel_id=1, source_target_pairs={{0,64},{32,96},{64,0},{96,32},{1,65},{33,97},{65,1},{97,33},{2,66}... | collective-permute-start | bytes 983048 | tf_op jit(solution)/shard_map/ppermute | solution.py:577
  306.0 15.9 %copy-start.1 = (bf16[4,4,2,40,1024]{4,3,2,1,0:T(8,128)(2,1)S(1)}, bf16[4,4,2,40,1024]{4,3,2,1,0:T(8,128)(2,1)}, u32[]{:S(2)}) copy-start(bf16[4,4,2,40,1024]{4,3,2,1,0:T(8,128)(2,1)} %copy-done) | copy-start | bytes 7864324
  306.0 15.9 %copy-start.8 = (f32[33,1280]{1,0:T(8,128)S(1)}, f32[33,1280]{1,0:T(8,128)}, u32[]{:S(2)}) copy-start(f32[33,1280]{1,0:T(8,128)} %copy-done.7) | copy-start | bytes 506884
  306.0 15.9 %copy-start.28 = (f32[1280]{0:T(1024)S(1)}, f32[1280]{0:T(1024)}, u32[]{:S(2)}) copy-start(f32[1280]{0:T(1024)} %copy-done.27) | copy-start | bytes 15364
  306.0 15.9 %copy-start.32 = (f32[2,33]{1,0:T(2,128)S(1)}, f32[2,33]{1,0:T(2,128)}, u32[]{:S(2)}) copy-start(f32[2,33]{1,0:T(2,128)} %copy-done.31) | copy-start | bytes 796
  306.0 15.9 %copy-start.36 = (f32[2,33]{1,0:T(2,128)S(1)}, f32[2,33]{1,0:T(2,128)}, u32[]{:S(2)}) copy-start(f32[2,33]{1,0:T(2,128)} %copy-done.35) | copy-start | bytes 796
  306.0 15.9 %copy-start.41 = (f32[2,33]{1,0:T(2,128)S(1)}, f32[2,33]{1,0:T(2,128)}, u32[]{:S(2)}) copy-start(f32[2,33]{1,0:T(2,128)} %copy-done.40) | copy-start | bytes 796
  310.7 13.9 %copy-start.22 = (pred[2,256,128]{2,1,0:T(32,128)(4,1)S(1)}, pred[2,256,128]{2,1,0:T(32,128)(4,1)}, u32[]{:S(2)}) copy-start(pred[2,256,128]{2,1,0:T(32,128)(4,1)} %copy-done.21) | copy-start | bytes 196612
  321.9 3.3 copy-start.16
  406.5 34.2 %copy-start.23 = (f32[40,4096]{1,0:T(8,128)S(1)}, f32[40,4096]{1,0:T(8,128)}, u32[]{:S(2)}) copy-start(f32[40,4096]{1,0:T(8,128)} %get-tuple-element.48) | copy-start | bytes 1966084
  440.3 4.3 collective-permute-start.11
  446.6 3.8 copy-start.26
  446.6 4.5 copy-start.18
  (16 other events, 31.4 us)
Sparse Core Ops, SparseCore 0:
  16.9 67.2 all-gather.2
  86.4 61.8 all-gather.4
  165.6 93.5 reduce-scatter.4
  262.5 103.3 reduce-scatter.2
